TPU v7x, 256 devices: a whole 4x4x8 slice. The times are simulated.
256 devices in a mesh: dp: 16 (over z_hi, x), tp: 16 (over z_lo, y, core).
Axes of the slice: x: 4, y: 4, z: 8 (z_hi: 4, z_lo: 2; z = z_hi * 2 + z_lo), core: 2. Of those that a mesh axis runs over, the one named last changes fastest.
Arguments:
- gradients: bfloat16 [16, 4, 5120, 1280], P('dp', None, 'tp'), may hold values from -6 to 6
- right_factor: float32 [4, 1280, 32], replicated, may hold values from -6 to 6
- weights_before: float32 [4, 5120, 1280], P(None, 'tp', 'dp'), may hold values from -0.15625 to 0.15625
- momentum: float32 [4, 5120, 1280], P(None, 'tp', 'dp'), may hold values from -0.3125 to 0.3125
Outputs:
- new_weights: float32 [4, 5120, 1280], P(None, 'tp', 'dp')
- new_basis: float32 [4, 1280, 32], replicated
- new_momentum: float32 [4, 5120, 1280], P(None, 'tp', 'dp')
All inputs are finite; a program needn't handle non-finite values.
Results may differ from a plain program's by a relative error of at most 0.003.
Values sent between devices are 32-bit elements; how exact they have to be, the bound alone decides.
No kernel may reach another device: no remote copies, remote signals or barrier semaphores. Data moves between devices by JAX's collectives and lax.ppermute only.
A program may use at most 64 MiB of HBM per device.

v0:
```python
import jax
import jax.numpy as jnp
from jax import lax
from jax.experimental import pallas as pl
from jax.experimental.pallas import tpu as pltpu
from jax.sharding import PartitionSpec as P


RANK = 32
LAYERS = 4
LR = LAYERS * RANK
HALF = LR // 2
HIGH = lax.Precision.HIGHEST
SMALL = pltpu.CompilerParams(vmem_limit_bytes=16 * 2**20)

X_RINGS = [[z * 4 + x for x in range(4)] for z in range(4)]
Z_RINGS = [[z * 4 + x for z in range(4)] for x in range(4)]
CORE_PAIRS = [(j, j ^ 1) for j in range(16)]
CHIP_GROUPS = [[2 * chip + core for chip in range(8)] for core in range(2)]


def hop(rings, step):
    return [(ring[j], ring[(j + step) % len(ring)]) for ring in rings for j in range(len(ring))]


def to_ring(arrays, rings):
    got = []
    for k, array in enumerate(arrays, 1):
        got.append(lax.ppermute(array, "dp", hop(rings, k)))
    return got


def sum_of_ring(array, rings):
    one, two, three = to_ring([array] * 3, rings)
    return (array + two) + (one + three)


def left_kernel(grads, basis, own, one, two, three, total):
    layer = pl.program_id(0)
    small = basis[...].astype(jnp.bfloat16)
    rows = lax.broadcasted_iota(jnp.int32, (LR, small.shape[1]), 0) // RANK
    wide = jnp.where(rows == layer, jnp.concatenate([small] * LAYERS, axis=0), 0)
    part = lax.dot_general(
        grads[...], wide, (((1,), (1,)), ((), ())), preferred_element_type=jnp.float32
    )

    @pl.when(layer == 0)
    def _():
        total[...] = part

    @pl.when(layer > 0)
    def _():
        total[...] += part

    @pl.when(layer == LAYERS - 1)
    def _():
        rows = own.shape[0]
        x = lax.rem(lax.axis_index("dp"), 4)
        for step, out in enumerate((own, one, two, three)):
            start = lax.rem(x + step, 4) * rows
            out[...] = total[pl.ds(pl.multiple_of(start, 8), rows), :]


def left_parts(grads, basis_t):
    _, layers, rows, width = grads.shape
    piece = jax.ShapeDtypeStruct((rows // 4, LR), jnp.float32)
    return pl.pallas_call(
        left_kernel,
        out_shape=[piece] * 4,
        grid=(layers,),
        in_specs=[
            pl.BlockSpec((None, None, rows, width), lambda l: (0, l, 0, 0)),
            pl.BlockSpec((None, RANK, width), lambda l: (l, 0, 0)),
        ],
        out_specs=[pl.BlockSpec((rows // 4, LR), lambda l: (0, 0))] * 4,
        scratch_shapes=[pltpu.VMEM((rows, LR), jnp.float32)],
        compiler_params=pltpu.CompilerParams(vmem_limit_bytes=54772 * 2**10),
        name="left_parts",
    )(grads, basis_t)


def right_kernel(grads, own, one, two, three, send, keep, left):
    rows = own.shape[0]
    x = lax.rem(lax.axis_index("dp"), 4)
    core = lax.rem(lax.axis_index("tp"), 2)
    for back, piece in enumerate((own, one, two, three)):
        start = lax.rem(x + 4 - back, 4) * rows
        left[pl.ds(pl.multiple_of(start, 8), rows), :] = piece[...]
    whole = left[...]
    small = whole.T.astype(jnp.bfloat16)
    for out, group in ((send, 1 - core), (keep, core)):
        for t in range(2):
            rank = small[t * RANK : (t + 1) * RANK, :]
            other = small[(2 + t) * RANK : (3 + t) * RANK, :]
            out[t * RANK : (t + 1) * RANK, :] = jnp.dot(
                jnp.where(group == 0, rank, other),
                grads[0, 2 * group + t],
                preferred_element_type=jnp.float32,
            )
    full = lax.dot_general(
        whole, whole, (((0,), (0,)), ((), ())), precision=HIGH, preferred_element_type=jnp.float32
    )
    blocks = [full[l * RANK : (l + 1) * RANK, l * RANK : (l + 1) * RANK] for l in range(LAYERS)]
    halves = [jnp.concatenate(blocks[h : h + 2], axis=1) for h in (0, 2)]
    for out, group in ((send, 1 - core), (keep, core)):
        gram = jnp.where(group == 0, halves[0], halves[1])
        for k in range(4):
            out[64:72, k * HALF : (k + 1) * HALF] = gram[8 * k : 8 * k + 8, :]
        out[64:72, 4 * HALF :] = jnp.zeros((8, out.shape[1] - 4 * HALF), jnp.float32)


def right_parts(grads, pieces):
    _, _, rows, width = grads.shape
    half = jax.ShapeDtypeStruct((LR // 2 + 8, width), jnp.float32)
    block = pl.BlockSpec(memory_space=pltpu.VMEM)
    return pl.pallas_call(
        right_kernel,
        out_shape=[half, half, jax.ShapeDtypeStruct((rows, LR), jnp.float32)],
        in_specs=[block] * 5,
        out_specs=[block] * 3,
        compiler_params=SMALL,
        name="right_parts",
    )(grads, *pieces)


def inverse_kernel(packed, out):
    gram = jnp.concatenate([packed[:, k * HALF : (k + 1) * HALF] for k in range(4)], axis=0)
    row = lax.broadcasted_iota(jnp.int32, (RANK, HALF), 0)
    lane = lax.broadcasted_iota(jnp.int32, (RANK, HALF), 1)
    inner = lane % RANK
    on_diagonal = inner == row
    picked = jnp.sum(jnp.where(on_diagonal, gram, 0.0), axis=0, keepdims=True)
    ridge = jnp.zeros((1, HALF), jnp.float32)
    for l in range(2):
        mine = lane[:1] // RANK == l
        mean = jnp.sum(jnp.where(mine, picked, 0.0), axis=1, keepdims=True) / RANK
        ridge = jnp.where(mine, mean, ridge)
    m = gram + jnp.where(on_diagonal, 0.001 * ridge, 0.0)
    for k in range(RANK):
        column = jnp.where(lane < RANK, m[:, k : k + 1], m[:, RANK + k : RANK + k + 1])
        pivot = 1.0 / column[k : k + 1, :]
        scaled = jnp.where(inner[:1] == k, 1.0, m[k : k + 1, :]) * pivot
        m = jnp.where(row == k, scaled, jnp.where(inner == k, 0.0, m) - column * scaled)
    out[...] = m


def inverses(packed):
    return pl.pallas_call(
        inverse_kernel,
        out_shape=jax.ShapeDtypeStruct((RANK, HALF), jnp.float32),
        in_specs=[pl.BlockSpec(memory_space=pltpu.VMEM)],
        out_specs=pl.BlockSpec(memory_space=pltpu.VMEM),
        cost_estimate=pl.CostEstimate(flops=20_000_000, bytes_accessed=32768, transcendentals=0),
        compiler_params=SMALL,
        name="inverses",
    )(packed)


def last_kernel(
    replicas, mine, other, left, mine_inverse, other_inverse, weights, momentum, new_w, new_b, new_m
):
    core = lax.rem(lax.axis_index("tp"), 2)
    columns = weights.shape[1]
    start = lax.axis_index("dp") * columns
    width = mine.shape[1]
    for t in range(LAYERS):
        source, inverse = (mine, mine_inverse) if t < 2 else (other, other_inverse)
        layer = 2 * core + t if t < 2 else 2 * (1 - core) + (t - 2)
        right = source[(t % 2) * RANK : (t % 2 + 1) * RANK, :]
        square = jnp.sum(right * right) / (RANK * width)
        new_b[layer] = right * lax.rsqrt(jnp.full((1, 1), square, jnp.float32) + 1e-12)
        turned = pltpu.roll(right, lax.rem(width - start, width), 1)[:, :LR]
        shift = lax.rem(LR - layer * RANK, LR)
        block = inverse[:, (t % 2) * RANK : (t % 2 + 1) * RANK]
        mixed = jnp.dot(block, turned, precision=HIGH, preferred_element_type=jnp.float32)
        own = pltpu.roll(left[...], shift, 1)[:, :RANK]
        change = lax.dot_general(
            mixed, own, (((0,), (1,)), ((), ())), precision=HIGH, preferred_element_type=jnp.float32
        )[:columns, :] / replicas
        momentum_now = 0.8 * momentum[layer] + change
        new_m[layer] = momentum_now
        new_w[layer] = weights[layer] - 0.05 * momentum_now


def last_step(replicas, mine, other, left, mine_inverse, other_inverse, weights, momentum):
    block = pl.BlockSpec(memory_space=pltpu.VMEM)
    return pl.pallas_call(
        lambda *refs: last_kernel(replicas, *refs),
        out_shape=[
            jax.ShapeDtypeStruct(weights.shape, jnp.float32),
            jax.ShapeDtypeStruct((LAYERS, RANK, mine.shape[1]), jnp.float32),
            jax.ShapeDtypeStruct(weights.shape, jnp.float32),
        ],
        in_specs=[block] * 7,
        out_specs=[block] * 3,
        compiler_params=SMALL,
        name="last_step",
    )(mine, other, left, mine_inverse, other_inverse, weights, momentum)


def one_step(gradients, right_factor, weights_before, momentum):
    width = right_factor.shape[1]
    own, *others = left_parts(gradients, jnp.swapaxes(right_factor, 1, 2))
    one, two, three = to_ring(others, X_RINGS)
    share = sum_of_ring((own + two) + (one + three), Z_RINGS)
    pieces = [share] + to_ring([share] * 3, X_RINGS)

    send, keep, left = right_parts(gradients, pieces)
    pair = keep + lax.ppermute(send, "tp", CORE_PAIRS)
    gram = jnp.broadcast_to(pair[None, 64:, : 4 * HALF], (8, 8, 4 * HALF))
    packet = jnp.concatenate([pair[:64].reshape(8, 8, width), gram], axis=2)
    packet = lax.all_to_all(packet, "tp", 0, 0, tiled=True, axis_index_groups=CHIP_GROUPS)
    packet = jnp.sum(packet, axis=0)
    mine_inverse = inverses(packet[:, width:])
    other_inverse = lax.ppermute(mine_inverse, "tp", CORE_PAIRS)
    share = sum_of_ring(packet[:, :width], X_RINGS)
    share = sum_of_ring(share, Z_RINGS)
    mine = lax.all_to_all(
        jnp.broadcast_to(share[None], (8, 8, width)), "tp", 0, 0, tiled=True, axis_index_groups=CHIP_GROUPS
    ).reshape(HALF, width)
    other = lax.ppermute(mine, "tp", CORE_PAIRS)
    new_w, new_b, new_m = last_step(
        lax.axis_size("dp"),
        mine,
        other,
        left,
        mine_inverse,
        other_inverse,
        jnp.swapaxes(weights_before, 1, 2),
        jnp.swapaxes(momentum, 1, 2),
    )
    return tuple(jnp.swapaxes(array, 1, 2) for array in (new_w, new_b, new_m))


def solution(mesh):
    return jax.shard_map(
        one_step,
        mesh=mesh,
        in_specs=(P("dp", None, "tp", None), P(), P(None, "tp", "dp"), P(None, "tp", "dp")),
        out_specs=(P(None, "tp", "dp"), P(), P(None, "tp", "dp")),
        check_vma=False,
    )
```

profile of v0, /device:TPU:1, one launch (start us, length us, event | category | flops | bytes accessed | tf_op | source)
XLA Modules:
  0.0 92.6 jit_solution(8989155645197341846)
XLA Ops:
  0.6 0.0 copy-start
  0.6 3.8 %left_parts.1 = (f32[80,128]{1,0:T(8,128)S(1)}, f32[80,128]{1,0:T(8,128)S(1)}, f32[80,128]{1,0:T(8,128)S(1)}, f32[80,128]{1,0:T(8,128)S(1)}) custom-call(bf16[1,4,320,1280]{3,2,1,0:T(8,128)(2,1)} %grads.3, f32[4,32,1280]{2,1,0:T(8,128)} %bitcast.13), custom_call_target="tpu_custom_call" | custom-call | tf_op jit(solution)/shard_map/left_parts/pallas_call | solution.py:67
  4.5 3.7 %collective-permute-start = (f32[80,128]{1,0:T(8,128)S(1)}, f32[80,128]{1,0:T(8,128)S(1)}, u32[]{:S(2)}, u32[]{:S(2)}) collective-permute-start(f32[80,128]{1,0:T(8,128)S(1)} %get-tuple-element.14), channel_id=1, source_target_pairs={{0,32},{16,48},{32,0},{48,16},{64,96},{80,112},{96,64},{112,80},{1... | collective-permute-start | bytes 122888 | tf_op jit(solution)/shard_map/ppermute | solution.py:29
  8.1 0.3 collective-permute-start.1
  8.4 2.4 %collective-permute-start.2 = (f32[80,128]{1,0:T(8,128)S(1)}, f32[80,128]{1,0:T(8,128)S(1)}, u32[]{:S(2)}, u32[]{:S(2)}) collective-permute-start(f32[80,128]{1,0:T(8,128)S(1)} %get-tuple-element.16), channel_id=1, source_target_pairs={{0,48},{16,0},{32,16},{48,32},{64,112},{80,64},{96,80},{112,96},{1... | collective-permute-start | bytes 122888 | tf_op jit(solution)/shard_map/ppermute | solution.py:29
  10.8 0.0 collective-permute-done
  10.8 1.7 %collective-permute-done.1 = f32[80,128]{1,0:T(8,128)S(1)} collective-permute-done((f32[80,128]{1,0:T(8,128)S(1)}, f32[80,128]{1,0:T(8,128)S(1)}, u32[]{:S(2)}, u32[]{:S(2)}) %collective-permute-start.1) | collective-permute-done | bytes 40992 | tf_op jit(solution)/shard_map/ppermute | solution.py:29
  12.5 0.0 collective-permute-done.2
  12.5 5.8 %collective-permute-start.5 = (f32[80,128]{1,0:T(8,128)S(1)}, f32[80,128]{1,0:T(8,128)S(1)}, u32[]{:S(2)}, u32[]{:S(2)}) collective-permute-start(f32[80,128]{1,0:T(8,128)S(1)} %add_add_fusion.3), channel_id=1, source_target_pairs={{0,192},{64,0},{128,64},{192,128},{16,208},{80,16},{144,80},{208,1... | collective-permute-start | bytes 122888 | tf_op jit(solution)/shard_map/ppermute | solution.py:29
  18.3 0.0 collective-permute-start.4
  18.3 3.3 %collective-permute-start.3 = (f32[80,128]{1,0:T(8,128)S(1)}, f32[80,128]{1,0:T(8,128)S(1)}, u32[]{:S(2)}, u32[]{:S(2)}) collective-permute-start(f32[80,128]{1,0:T(8,128)S(1)} %add_add_fusion.3), channel_id=1, source_target_pairs={{0,128},{64,192},{128,0},{192,64},{16,144},{80,208},{144,16},{208,... | collective-permute-start | bytes 122888 | tf_op jit(solution)/shard_map/ppermute | solution.py:29
  21.5 0.0 collective-permute-done.5
  21.5 1.7 %collective-permute-done.4 = f32[80,128]{1,0:T(8,128)S(1)} collective-permute-done((f32[80,128]{1,0:T(8,128)S(1)}, f32[80,128]{1,0:T(8,128)S(1)}, u32[]{:S(2)}, u32[]{:S(2)}) %collective-permute-start.4) | collective-permute-done | bytes 40992 | tf_op jit(solution)/shard_map/ppermute | solution.py:29
  23.2 1.8 %collective-permute-done.3 = f32[80,128]{1,0:T(8,128)S(1)} collective-permute-done((f32[80,128]{1,0:T(8,128)S(1)}, f32[80,128]{1,0:T(8,128)S(1)}, u32[]{:S(2)}, u32[]{:S(2)}) %collective-permute-start.3) | collective-permute-done | bytes 40992 | tf_op jit(solution)/shard_map/ppermute | solution.py:29
  25.1 2.7 %collective-permute-start.8 = (f32[80,128]{1,0:T(8,128)S(1)}, f32[80,128]{1,0:T(8,128)S(1)}, u32[]{:S(2)}, u32[]{:S(2)}) collective-permute-start(f32[80,128]{1,0:T(8,128)S(1)} %add_add_fusion.2.own), channel_id=1, source_target_pairs={{0,48},{16,0},{32,16},{48,32},{64,112},{80,64},{96,80},{112,96},{1... | collective-permute-start | bytes 122888 | tf_op jit(solution)/shard_map/ppermute | solution.py:29
  27.8 0.0 collective-permute-start.7
  27.8 0.7 collective-permute-start.6
  28.5 0.4 collective-permute-done.8.three
  28.9 3.4 %collective-permute-done.7.two = f32[80,128]{1,0:T(8,128)S(1)} collective-permute-done((f32[80,128]{1,0:T(8,128)S(1)}, f32[80,128]{1,0:T(8,128)S(1)}, u32[]{:S(2)}, u32[]{:S(2)}) %collective-permute-start.7) | collective-permute-done | bytes 40992 | tf_op jit(solution)/shard_map/ppermute | solution.py:29
  32.3 0.0 collective-permute-done.6.one
  32.3 0.0 copy-done
  32.3 1.0 %right_parts.1 = (f32[72,1280]{1,0:T(8,128)S(1)}, f32[72,1280]{1,0:T(8,128)S(1)}, f32[320,128]{1,0:T(8,128)S(1)}) custom-call(bf16[1,4,320,1280]{3,2,1,0:T(8,128)(2,1)S(1)} %copy-done, f32[80,128]{1,0:T(8,128)S(1)} %add_add_fusion.2.own, f32[80,128]{1,0:T(8,128)S(1)} %collective-permute-done.6.one, f32[80,128]{1,0:T(8,128)S(1)} %collective-permute-done.7.two, ...), custom_call_target="tpu_custom_call" | custom-call | tf_op jit(solution)/shard_map/right_parts/pallas_call | solution.py:116
  33.4 0.0 copy-start.1
  33.4 0.0 copy-start.2
  33.4 5.6 %collective-permute-start.9 = (f32[72,1280]{1,0:T(8,128)S(1)}, f32[72,1280]{1,0:T(8,128)S(1)}, u32[]{:S(2)}, u32[]{:S(2)}) collective-permute-start(f32[72,1280]{1,0:T(8,128)S(1)} %get-tuple-element.18), channel_id=1, source_target_pairs={{0,1},{1,0},{2,3},{3,2},{4,5},{5,4},{6,7},{7,6},{8,9},{9,8},{10,11... | collective-permute-start | bytes 1105928 | tf_op jit(solution)/shard_map/ppermute | solution.py:209
  38.9 1.3 %collective-permute-done.9 = f32[72,1280]{1,0:T(8,128)S(1)} collective-permute-done((f32[72,1280]{1,0:T(8,128)S(1)}, f32[72,1280]{1,0:T(8,128)S(1)}, u32[]{:S(2)}, u32[]{:S(2)}) %collective-permute-start.9) | collective-permute-done | bytes 368672 | tf_op jit(solution)/shard_map/ppermute | solution.py:209
  40.2 0.1 add.45
  40.4 11.9 %all_to_all.10 = f32[8,8,1536]{2,1,0:T(8,128)S(1)} all-to-all(f32[8,8,1536]{2,1,0:T(8,128)S(1)} %pad_maximum_fusion), channel_id=1, replica_groups={{0,2,4,6,8,10,12,14},{1,3,5,7,9,11,13,15},{16,18,20,22,24,26,28,30},{17..., dimensions={0} | all-to-all | bytes 786432 | tf_op jit(solution)/shard_map/all_to_all | solution.py:212
  52.4 0.1 collective-permute-start.11
  52.5 2.7 %collective-permute-start.12 = (f32[8,1280]{1,0:T(8,128)S(1)}, f32[8,1280]{1,0:T(8,128)S(1)}, u32[]{:S(2)}, u32[]{:S(2)}) collective-permute-start(f32[8,1280]{1,0:T(8,128)S(1)} %slice.18), channel_id=1, source_target_pairs={{0,48},{16,0},{32,16},{48,32},{64,112},{80,64},{96,80},{112,96},{1... | collective-permute-start | bytes 122888 | tf_op jit(solution)/shard_map/ppermute | solution.py:29
  55.1 0.4 collective-permute-start.10
  55.5 1.0 %collective-permute-done.11 = f32[8,1280]{1,0:T(8,128)S(1)} collective-permute-done((f32[8,1280]{1,0:T(8,128)S(1)}, f32[8,1280]{1,0:T(8,128)S(1)}, u32[]{:S(2)}, u32[]{:S(2)}) %collective-permute-start.11) | collective-permute-done | bytes 40992 | tf_op jit(solution)/shard_map/ppermute | solution.py:29
  56.5 0.0 collective-permute-done.12
  56.5 3.0 %collective-permute-done.10 = f32[8,1280]{1,0:T(8,128)S(1)} collective-permute-done((f32[8,1280]{1,0:T(8,128)S(1)}, f32[8,1280]{1,0:T(8,128)S(1)}, u32[]{:S(2)}, u32[]{:S(2)}) %collective-permute-start.10) | collective-permute-done | bytes 40992 | tf_op jit(solution)/shard_map/ppermute | solution.py:29
  59.5 3.9 %collective-permute-start.15 = (f32[8,1280]{1,0:T(8,128)S(1)}, f32[8,1280]{1,0:T(8,128)S(1)}, u32[]{:S(2)}, u32[]{:S(2)}) collective-permute-start(f32[8,1280]{1,0:T(8,128)S(1)} %add_add_fusion.1), channel_id=1, source_target_pairs={{0,192},{64,0},{128,64},{192,128},{16,208},{80,16},{144,80},{208,1... | collective-permute-start | bytes 122888 | tf_op jit(solution)/shard_map/ppermute | solution.py:29
  63.4 0.0 collective-permute-start.14
  63.4 2.2 %collective-permute-start.13 = (f32[8,1280]{1,0:T(8,128)S(1)}, f32[8,1280]{1,0:T(8,128)S(1)}, u32[]{:S(2)}, u32[]{:S(2)}) collective-permute-start(f32[8,1280]{1,0:T(8,128)S(1)} %add_add_fusion.1), channel_id=1, source_target_pairs={{0,128},{64,192},{128,0},{192,64},{16,144},{80,208},{144,16},{208,... | collective-permute-start | bytes 122888 | tf_op jit(solution)/shard_map/ppermute | solution.py:29
  65.6 0.0 collective-permute-done.15
  65.6 2.8 %collective-permute-done.14 = f32[8,1280]{1,0:T(8,128)S(1)} collective-permute-done((f32[8,1280]{1,0:T(8,128)S(1)}, f32[8,1280]{1,0:T(8,128)S(1)}, u32[]{:S(2)}, u32[]{:S(2)}) %collective-permute-start.14) | collective-permute-done | bytes 40992 | tf_op jit(solution)/shard_map/ppermute | solution.py:29
  68.4 1.8 %collective-permute-done.13 = f32[8,1280]{1,0:T(8,128)S(1)} collective-permute-done((f32[8,1280]{1,0:T(8,128)S(1)}, f32[8,1280]{1,0:T(8,128)S(1)}, u32[]{:S(2)}, u32[]{:S(2)}) %collective-permute-start.13) | collective-permute-done | bytes 40992 | tf_op jit(solution)/shard_map/ppermute | solution.py:29
  70.3 9.6 %all_to_all.11 = f32[8,8,1280]{2,1,0:T(8,128)S(1)} all-to-all(f32[8,8,1280]{2,1,0:T(8,128)S(1)} %broadcast_in_dim.5), channel_id=1, replica_groups={{0,2,4,6,8,10,12,14},{1,3,5,7,9,11,13,15},{16,18,20,22,24,26,28,30},{17..., dimensions={0} | all-to-all | bytes 655360 | tf_op jit(solution)/shard_map/all_to_all | solution.py:218
  79.8 5.7 %collective-permute-start.16 = (f32[64,1280]{1,0:T(8,128)S(1)}, f32[64,1280]{1,0:T(8,128)S(1)}, u32[]{:S(2)}, u32[]{:S(2)}) collective-permute-start(f32[64,1280]{1,0:T(8,128)S(1)} %bitcast.9), channel_id=1, source_target_pairs={{0,1},{1,0},{2,3},{3,2},{4,5},{5,4},{6,7},{7,6},{8,9},{9,8},{10,11... | collective-permute-start | bytes 983048 | tf_op jit(solution)/shard_map/ppermute | solution.py:221
  85.5 2.9 %inverses.1.refs_3_ = f32[32,64]{1,0:T(8,128)S(1)} custom-call(f32[8,256]{1,0:T(8,128)S(1)} %slice.19.packed), custom_call_target="tpu_custom_call" | custom-call | flops 20000000 | bytes 32768 | tf_op jit(solution)/shard_map/inverses/pallas_call | solution.py:148
  88.4 0.1 collective-permute-start.17
  88.5 1.2 %collective-permute-done.17.refs_4_ = f32[32,64]{1,0:T(8,128)S(1)} collective-permute-done((f32[32,64]{1,0:T(8,128)S(1)}, f32[32,64]{1,0:T(8,128)S(1)}, u32[]{:S(2)}, u32[]{:S(2)}) %collective-permute-start.17) | collective-permute-done | bytes 8224 | tf_op jit(solution)/shard_map/ppermute | solution.py:215
  89.7 0.0 collective-permute-done.16.refs_1_
  89.7 0.0 copy-done.1
  89.7 0.0 copy-done.2
  89.7 2.9 %last_step.1 = (f32[4,80,320]{2,1,0:T(8,128)}, f32[4,32,1280]{2,1,0:T(8,128)}, f32[4,80,320]{2,1,0:T(8,128)}) custom-call(f32[64,1280]{1,0:T(8,128)S(1)} %bitcast.10, f32[64,1280]{1,0:T(8,128)S(1)} %collective-permute-done.16.refs_1_, f32[320,128]{1,0:T(8,128)S(1)} %get-tuple-element.19.refs_2_, f32[32,64]{1,0:T(8,128)S(1)} %inverses.1.refs_3_, ...), custom_call_target="tpu_custom_call" | custom-call | tf_op jit(solution)/shard_map/last_step/pallas_call | solution.py:187
  (12 shorter events, 0.2 us)
Async XLA Ops:
  0.6 31.7 %copy-start = (bf16[1,4,320,1280]{3,2,1,0:T(8,128)(2,1)S(1)}, bf16[1,4,320,1280]{3,2,1,0:T(8,128)(2,1)}, u32[]{:S(2)}) copy-start(bf16[1,4,320,1280]{3,2,1,0:T(8,128)(2,1)} %grads.3) | copy-start | bytes 9830404
  4.5 6.3 %collective-permute-start = (f32[80,128]{1,0:T(8,128)S(1)}, f32[80,128]{1,0:T(8,128)S(1)}, u32[]{:S(2)}, u32[]{:S(2)}) collective-permute-start(f32[80,128]{1,0:T(8,128)S(1)} %get-tuple-element.14), channel_id=1, source_target_pairs={{0,32},{16,48},{32,0},{48,16},{64,96},{80,112},{96,64},{112,80},{1... | collective-permute-start | bytes 122888 | tf_op jit(solution)/shard_map/ppermute | solution.py:29
  8.1 4.4 %collective-permute-start.1 = (f32[80,128]{1,0:T(8,128)S(1)}, f32[80,128]{1,0:T(8,128)S(1)}, u32[]{:S(2)}, u32[]{:S(2)}) collective-permute-start(f32[80,128]{1,0:T(8,128)S(1)} %get-tuple-element.15), channel_id=1, source_target_pairs={{0,16},{16,32},{32,48},{48,0},{64,80},{80,96},{96,112},{112,64},{1... | collective-permute-start | bytes 122888 | tf_op jit(solution)/shard_map/ppermute | solution.py:29
  8.4 4.1 %collective-permute-start.2 = (f32[80,128]{1,0:T(8,128)S(1)}, f32[80,128]{1,0:T(8,128)S(1)}, u32[]{:S(2)}, u32[]{:S(2)}) collective-permute-start(f32[80,128]{1,0:T(8,128)S(1)} %get-tuple-element.16), channel_id=1, source_target_pairs={{0,48},{16,0},{32,16},{48,32},{64,112},{80,64},{96,80},{112,96},{1... | collective-permute-start | bytes 122888 | tf_op jit(solution)/shard_map/ppermute | solution.py:29
  12.5 9.0 %collective-permute-start.5 = (f32[80,128]{1,0:T(8,128)S(1)}, f32[80,128]{1,0:T(8,128)S(1)}, u32[]{:S(2)}, u32[]{:S(2)}) collective-permute-start(f32[80,128]{1,0:T(8,128)S(1)} %add_add_fusion.3), channel_id=1, source_target_pairs={{0,192},{64,0},{128,64},{192,128},{16,208},{80,16},{144,80},{208,1... | collective-permute-start | bytes 122888 | tf_op jit(solution)/shard_map/ppermute | solution.py:29
  18.3 5.0 %collective-permute-start.4 = (f32[80,128]{1,0:T(8,128)S(1)}, f32[80,128]{1,0:T(8,128)S(1)}, u32[]{:S(2)}, u32[]{:S(2)}) collective-permute-start(f32[80,128]{1,0:T(8,128)S(1)} %add_add_fusion.3), channel_id=1, source_target_pairs={{0,64},{64,128},{128,192},{192,0},{16,80},{80,144},{144,208},{208,... | collective-permute-start | bytes 122888 | tf_op jit(solution)/shard_map/ppermute | solution.py:29
  18.3 6.8 %collective-permute-start.3 = (f32[80,128]{1,0:T(8,128)S(1)}, f32[80,128]{1,0:T(8,128)S(1)}, u32[]{:S(2)}, u32[]{:S(2)}) collective-permute-start(f32[80,128]{1,0:T(8,128)S(1)} %add_add_fusion.3), channel_id=1, source_target_pairs={{0,128},{64,192},{128,0},{192,64},{16,144},{80,208},{144,16},{208,... | collective-permute-start | bytes 122888 | tf_op jit(solution)/shard_map/ppermute | solution.py:29
  25.1 3.8 %collective-permute-start.8 = (f32[80,128]{1,0:T(8,128)S(1)}, f32[80,128]{1,0:T(8,128)S(1)}, u32[]{:S(2)}, u32[]{:S(2)}) collective-permute-start(f32[80,128]{1,0:T(8,128)S(1)} %add_add_fusion.2.own), channel_id=1, source_target_pairs={{0,48},{16,0},{32,16},{48,32},{64,112},{80,64},{96,80},{112,96},{1... | collective-permute-start | bytes 122888 | tf_op jit(solution)/shard_map/ppermute | solution.py:29
  27.8 4.5 %collective-permute-start.7 = (f32[80,128]{1,0:T(8,128)S(1)}, f32[80,128]{1,0:T(8,128)S(1)}, u32[]{:S(2)}, u32[]{:S(2)}) collective-permute-start(f32[80,128]{1,0:T(8,128)S(1)} %add_add_fusion.2.own), channel_id=1, source_target_pairs={{0,32},{16,48},{32,0},{48,16},{64,96},{80,112},{96,64},{112,80},{1... | collective-permute-start | bytes 122888 | tf_op jit(solution)/shard_map/ppermute | solution.py:29
  27.8 4.5 %collective-permute-start.6 = (f32[80,128]{1,0:T(8,128)S(1)}, f32[80,128]{1,0:T(8,128)S(1)}, u32[]{:S(2)}, u32[]{:S(2)}) collective-permute-start(f32[80,128]{1,0:T(8,128)S(1)} %add_add_fusion.2.own), channel_id=1, source_target_pairs={{0,16},{16,32},{32,48},{48,0},{64,80},{80,96},{96,112},{112,64},{1... | collective-permute-start | bytes 122888 | tf_op jit(solution)/shard_map/ppermute | solution.py:29
  33.4 56.3 %copy-start.1 = (f32[4,320,80]{1,2,0:T(8,128)S(1)}, f32[4,320,80]{1,2,0:T(8,128)}, u32[]{:S(2)}) copy-start(f32[4,320,80]{1,2,0:T(8,128)} %param.6) | copy-start | bytes 1228804
  33.4 56.3 %copy-start.2 = (f32[4,320,80]{1,2,0:T(8,128)S(1)}, f32[4,320,80]{1,2,0:T(8,128)}, u32[]{:S(2)}) copy-start(f32[4,320,80]{1,2,0:T(8,128)} %param.7) | copy-start | bytes 1228804
  33.4 6.9 %collective-permute-start.9 = (f32[72,1280]{1,0:T(8,128)S(1)}, f32[72,1280]{1,0:T(8,128)S(1)}, u32[]{:S(2)}, u32[]{:S(2)}) collective-permute-start(f32[72,1280]{1,0:T(8,128)S(1)} %get-tuple-element.18), channel_id=1, source_target_pairs={{0,1},{1,0},{2,3},{3,2},{4,5},{5,4},{6,7},{7,6},{8,9},{9,8},{10,11... | collective-permute-start | bytes 1105928 | tf_op jit(solution)/shard_map/ppermute | solution.py:209
  52.4 4.1 %collective-permute-start.11 = (f32[8,1280]{1,0:T(8,128)S(1)}, f32[8,1280]{1,0:T(8,128)S(1)}, u32[]{:S(2)}, u32[]{:S(2)}) collective-permute-start(f32[8,1280]{1,0:T(8,128)S(1)} %slice.18), channel_id=1, source_target_pairs={{0,16},{16,32},{32,48},{48,0},{64,80},{80,96},{96,112},{112,64},{1... | collective-permute-start | bytes 122888 | tf_op jit(solution)/shard_map/ppermute | solution.py:29
  52.5 4.1 %collective-permute-start.12 = (f32[8,1280]{1,0:T(8,128)S(1)}, f32[8,1280]{1,0:T(8,128)S(1)}, u32[]{:S(2)}, u32[]{:S(2)}) collective-permute-start(f32[8,1280]{1,0:T(8,128)S(1)} %slice.18), channel_id=1, source_target_pairs={{0,48},{16,0},{32,16},{48,32},{64,112},{80,64},{96,80},{112,96},{1... | collective-permute-start | bytes 122888 | tf_op jit(solution)/shard_map/ppermute | solution.py:29
  55.1 4.4 %collective-permute-start.10 = (f32[8,1280]{1,0:T(8,128)S(1)}, f32[8,1280]{1,0:T(8,128)S(1)}, u32[]{:S(2)}, u32[]{:S(2)}) collective-permute-start(f32[8,1280]{1,0:T(8,128)S(1)} %slice.18), channel_id=1, source_target_pairs={{0,32},{16,48},{32,0},{48,16},{64,96},{80,112},{96,64},{112,80},{1... | collective-permute-start | bytes 122888 | tf_op jit(solution)/shard_map/ppermute | solution.py:29
  59.5 6.1 %collective-permute-start.15 = (f32[8,1280]{1,0:T(8,128)S(1)}, f32[8,1280]{1,0:T(8,128)S(1)}, u32[]{:S(2)}, u32[]{:S(2)}) collective-permute-start(f32[8,1280]{1,0:T(8,128)S(1)} %add_add_fusion.1), channel_id=1, source_target_pairs={{0,192},{64,0},{128,64},{192,128},{16,208},{80,16},{144,80},{208,1... | collective-permute-start | bytes 122888 | tf_op jit(solution)/shard_map/ppermute | solution.py:29
  63.4 5.0 %collective-permute-start.14 = (f32[8,1280]{1,0:T(8,128)S(1)}, f32[8,1280]{1,0:T(8,128)S(1)}, u32[]{:S(2)}, u32[]{:S(2)}) collective-permute-start(f32[8,1280]{1,0:T(8,128)S(1)} %add_add_fusion.1), channel_id=1, source_target_pairs={{0,64},{64,128},{128,192},{192,0},{16,80},{80,144},{144,208},{208,... | collective-permute-start | bytes 122888 | tf_op jit(solution)/shard_map/ppermute | solution.py:29
  63.4 6.8 %collective-permute-start.13 = (f32[8,1280]{1,0:T(8,128)S(1)}, f32[8,1280]{1,0:T(8,128)S(1)}, u32[]{:S(2)}, u32[]{:S(2)}) collective-permute-start(f32[8,1280]{1,0:T(8,128)S(1)} %add_add_fusion.1), channel_id=1, source_target_pairs={{0,128},{64,192},{128,0},{192,64},{16,144},{80,208},{144,16},{208,... | collective-permute-start | bytes 122888 | tf_op jit(solution)/shard_map/ppermute | solution.py:29
  79.8 9.9 %collective-permute-start.16 = (f32[64,1280]{1,0:T(8,128)S(1)}, f32[64,1280]{1,0:T(8,128)S(1)}, u32[]{:S(2)}, u32[]{:S(2)}) collective-permute-start(f32[64,1280]{1,0:T(8,128)S(1)} %bitcast.9), channel_id=1, source_target_pairs={{0,1},{1,0},{2,3},{3,2},{4,5},{5,4},{6,7},{7,6},{8,9},{9,8},{10,11... | collective-permute-start | bytes 983048 | tf_op jit(solution)/shard_map/ppermute | solution.py:221
  88.4 1.3 %collective-permute-start.17 = (f32[32,64]{1,0:T(8,128)S(1)}, f32[32,64]{1,0:T(8,128)S(1)}, u32[]{:S(2)}, u32[]{:S(2)}) collective-permute-start(f32[32,64]{1,0:T(8,128)S(1)} %inverses.1.refs_3_), channel_id=1, source_target_pairs={{0,1},{1,0},{2,3},{3,2},{4,5},{5,4},{6,7},{7,6},{8,9},{9,8},{10,11... | collective-permute-start | bytes 24584 | tf_op jit(solution)/shard_map/ppermute | solution.py:215
where the time goes:
time: 92.7 us; the launch traced here: 92.6 us
  starting transfers between devices  39.4 us (43%)
  blocking collectives  21.5 us (23%)
  waiting for transfers between devices  20.1 us (22%)
  Pallas kernels  10.6 us (11%)
    ppermute x15, starting transfers between devices, to_ring(): got.append(lax.ppermute(array, 'dp', hop(rings, k)))  28 us
    ppermute x15, waiting for transfers between devices, to_ring(): got.append(lax.ppermute(array, 'dp', hop(rings, k)))  17.6 us
    all_to_all x1, blocking collectives, one_step(): lax.all_to_all(packet, 'tp', 0, 0, tiled=True, axis_index_groups=CHIP_GRO...  11.9 us
    all_to_all x1, blocking collectives, one_step(): lax.all_to_all(jnp.broadcast_to(share[None], (8, 8, width)), 'tp', 0, 0,...  9.56 us
    ppermute x1, starting transfers between devices, one_step(): other = lax.ppermute(mine, 'tp', CORE_PAIRS)  5.71 us
    ppermute x1, starting transfers between devices, one_step(): pair = keep + lax.ppermute(send, 'tp', CORE_PAIRS)  5.57 us
    pallas_call x1, Pallas kernels, left_parts(): pl.pallas_call(left_kernel, out_shape=[piece] * 4, grid=(layers,), in_spe...  3.81 us
    pallas_call x1, Pallas kernels, inverses(): pl.pallas_call(inverse_kernel, out_shape=jax.ShapeDtypeStruct((RANK, HALF...  2.9 us
  transfers between devices with their start and end apart: 18, of which 11 were waited for; matrix products, arithmetic and copies ran while one was open for 0% of the time, Pallas kernels for 3%

commit v1 on v0

v1 whole, which is shorter than its diff:
```python
import jax
import jax.numpy as jnp
from jax import lax
from jax.experimental import pallas as pl
from jax.experimental.pallas import tpu as pltpu
from jax.sharding import PartitionSpec as P


RANK = 32
LAYERS = 4
LR = LAYERS * RANK
HALF = LR // 2
HIGH = lax.Precision.HIGHEST
SMALL = pltpu.CompilerParams(vmem_limit_bytes=16 * 2**20)

X_RINGS = [[z * 4 + x for x in range(4)] for z in range(4)]
Z_RINGS = [[z * 4 + x for z in range(4)] for x in range(4)]
CORE_PAIRS = [(j, j ^ 1) for j in range(16)]
CHIP_GROUPS = [[2 * chip + core for chip in range(8)] for core in range(2)]


def hop(rings, step):
    return [(ring[j], ring[(j + step) % len(ring)]) for ring in rings for j in range(len(ring))]


def to_ring(arrays, rings):
    got = []
    for k, array in enumerate(arrays, 1):
        got.append(lax.ppermute(array, "dp", hop(rings, k)))
    return got


def sum_of_ring(array, rings):
    one, two, three = to_ring([array] * 3, rings)
    return (array + two) + (one + three)


def left_kernel(grads, basis, own, one, two, three, total_t, total, held, small, sems):
    layers = held.shape[0]
    copies = []
    for l in range(layers):
        copies.append(
            (
                pltpu.make_async_copy(basis.at[l], small.at[l], sems.at[l]),
                pltpu.make_async_copy(grads.at[0, l], held.at[l], sems.at[layers + l]),
            )
        )
    for pair in copies:
        for copy in pair:
            copy.start()
    for l, pair in enumerate(copies):
        for copy in pair:
            copy.wait()
        total_t[l * RANK : (l + 1) * RANK, :] = lax.dot_general(
            small[l].astype(jnp.bfloat16),
            held[l],
            (((1,), (1,)), ((), ())),
            preferred_element_type=jnp.float32,
        )
    total[...] = total_t[...].T
    rows = own.shape[0]
    x = lax.rem(lax.axis_index("dp"), 4)
    for step, out in enumerate((own, one, two, three)):
        start = lax.rem(x + step, 4) * rows
        out[...] = total[pl.ds(pl.multiple_of(start, 8), rows), :]


def left_parts(grads, basis_t):
    _, layers, rows, width = grads.shape
    piece = jax.ShapeDtypeStruct((rows // 4, LR), jnp.float32)
    return pl.pallas_call(
        left_kernel,
        out_shape=[piece] * 4,
        in_specs=[pl.BlockSpec(memory_space=pl.ANY)] * 2,
        out_specs=[pl.BlockSpec(memory_space=pltpu.VMEM)] * 4,
        scratch_shapes=[
            pltpu.VMEM((LR, rows), jnp.float32),
            pltpu.VMEM((rows, LR), jnp.float32),
            pltpu.VMEM((layers, rows, width), jnp.bfloat16),
            pltpu.VMEM((layers, RANK, width), jnp.float32),
            pltpu.SemaphoreType.DMA((2 * layers,)),
        ],
        compiler_params=pltpu.CompilerParams(vmem_limit_bytes=54772 * 2**10),
        name="left_parts",
    )(grads, basis_t)


def right_send_kernel(grads, own, one, two, three, send, keep_gram, keep_small, left):
    rows = own.shape[0]
    x = lax.rem(lax.axis_index("dp"), 4)
    core = lax.rem(lax.axis_index("tp"), 2)
    for back, piece in enumerate((own, one, two, three)):
        start = lax.rem(x + 4 - back, 4) * rows
        left[pl.ds(pl.multiple_of(start, 8), rows), :] = piece[...]
    whole = left[...]
    small = whole.T.astype(jnp.bfloat16)
    low, high = small[:HALF, :], small[HALF:, :]
    keep_small[...] = jnp.where(core == 0, low, high)
    going = jnp.where(core == 0, high, low)
    for t in range(2):
        send[t * RANK : (t + 1) * RANK, :] = jnp.dot(
            going[t * RANK : (t + 1) * RANK, :],
            grads[0, 2 * (1 - core) + t],
            preferred_element_type=jnp.float32,
        )
    full = lax.dot_general(
        whole, whole, (((0,), (0,)), ((), ())), precision=HIGH, preferred_element_type=jnp.float32
    )
    blocks = [full[l * RANK : (l + 1) * RANK, l * RANK : (l + 1) * RANK] for l in range(LAYERS)]
    first, second = (jnp.concatenate(blocks[h : h + 2], axis=1) for h in (0, 2))
    kept = jnp.where(core == 0, first, second)
    gone = jnp.where(core == 0, second, first)
    for k in range(4):
        lanes = slice(k * HALF, (k + 1) * HALF)
        keep_gram[:, lanes] = kept[8 * k : 8 * k + 8, :]
        send[HALF : HALF + 8, lanes] = gone[8 * k : 8 * k + 8, :]
    send[HALF : HALF + 8, 4 * HALF :] = jnp.zeros((8, send.shape[1] - 4 * HALF), jnp.float32)


def right_send(grads, pieces):
    _, _, rows, width = grads.shape
    block = pl.BlockSpec(memory_space=pltpu.VMEM)
    return pl.pallas_call(
        right_send_kernel,
        out_shape=[
            jax.ShapeDtypeStruct((HALF + 8, width), jnp.float32),
            jax.ShapeDtypeStruct((8, 4 * HALF), jnp.float32),
            jax.ShapeDtypeStruct((HALF, rows), jnp.bfloat16),
            jax.ShapeDtypeStruct((rows, LR), jnp.float32),
        ],
        in_specs=[block] * 5,
        out_specs=[block] * 4,
        compiler_params=SMALL,
        name="right_send",
    )(grads, *pieces)


def right_keep_kernel(grads, small, keep):
    core = lax.rem(lax.axis_index("tp"), 2)
    for t in range(2):
        keep[t * RANK : (t + 1) * RANK, :] = jnp.dot(
            small[t * RANK : (t + 1) * RANK, :], grads[0, 2 * core + t], preferred_element_type=jnp.float32
        )


def right_keep(grads, small):
    block = pl.BlockSpec(memory_space=pltpu.VMEM)
    return pl.pallas_call(
        right_keep_kernel,
        out_shape=jax.ShapeDtypeStruct((HALF, grads.shape[3]), jnp.float32),
        in_specs=[block] * 2,
        out_specs=block,
        cost_estimate=pl.CostEstimate(flops=52_000_000, bytes_accessed=2_000_000, transcendentals=0),
        compiler_params=SMALL,
        name="right_keep",
    )(grads, small)


def solve_left(replicas, inverse, left, group, out):
    factor = jnp.where(group == 0, left[:, :HALF], left[:, HALF:])
    for t in range(2):
        lanes = slice(t * RANK, (t + 1) * RANK)
        out[lanes, :] = (
            lax.dot_general(
                inverse[:, lanes],
                factor[:, lanes],
                (((1,), (1,)), ((), ())),
                precision=HIGH,
                preferred_element_type=jnp.float32,
            )
            / replicas
        )


def inverse_kernel(replicas, packed, left, out, factor):
    gram = jnp.concatenate([packed[:, k * HALF : (k + 1) * HALF] for k in range(4)], axis=0)
    row = lax.broadcasted_iota(jnp.int32, (RANK, HALF), 0)
    lane = lax.broadcasted_iota(jnp.int32, (RANK, HALF), 1)
    inner = lane % RANK
    on_diagonal = inner == row
    picked = jnp.sum(jnp.where(on_diagonal, gram, 0.0), axis=0, keepdims=True)
    ridge = jnp.zeros((1, HALF), jnp.float32)
    for l in range(2):
        mine = lane[:1] // RANK == l
        mean = jnp.sum(jnp.where(mine, picked, 0.0), axis=1, keepdims=True) / RANK
        ridge = jnp.where(mine, mean, ridge)
    m = gram + jnp.where(on_diagonal, 0.001 * ridge, 0.0)
    for k in range(RANK):
        column = jnp.where(lane < RANK, m[:, k : k + 1], m[:, RANK + k : RANK + k + 1])
        pivot = 1.0 / column[k : k + 1, :]
        scaled = jnp.where(inner[:1] == k, 1.0, m[k : k + 1, :]) * pivot
        m = jnp.where(row == k, scaled, jnp.where(inner == k, 0.0, m) - column * scaled)
    out[...] = m
    solve_left(replicas, m, left, lax.rem(lax.axis_index("tp"), 2), factor)


def inverses(replicas, packed, left):
    return pl.pallas_call(
        lambda *refs: inverse_kernel(replicas, *refs),
        out_shape=[
            jax.ShapeDtypeStruct((RANK, HALF), jnp.float32),
            jax.ShapeDtypeStruct((HALF, left.shape[0]), jnp.float32),
        ],
        in_specs=[pl.BlockSpec(memory_space=pltpu.VMEM)] * 2,
        out_specs=[pl.BlockSpec(memory_space=pltpu.VMEM)] * 2,
        cost_estimate=pl.CostEstimate(flops=20_000_000, bytes_accessed=32768, transcendentals=0),
        compiler_params=SMALL,
        name="inverses",
    )(packed, left)


def last_kernel(group, right_half, factor, weights, momentum, outs, scratch):
    new_w, new_b, new_m = outs
    buf_w, buf_b, buf_m, sems = scratch
    columns = weights.shape[1]
    width = right_half.shape[1]
    start = lax.axis_index("dp") * columns
    copies = []
    for t in range(2):
        layer = 2 * group + t
        rows = slice(t * RANK, (t + 1) * RANK)
        right = right_half[rows, :]
        turned = pltpu.roll(right, lax.rem(width - start, width), 1)[:, :LR]
        change = lax.dot_general(
            turned,
            factor[rows, :],
            (((0,), (0,)), ((), ())),
            precision=HIGH,
            preferred_element_type=jnp.float32,
        )[:columns, :]
        square = jnp.sum(right * right) / (RANK * width)
        buf_b[t] = right * lax.rsqrt(jnp.full((1, 1), square, jnp.float32) + 1e-12)
        momentum_now = 0.8 * momentum[layer] + change
        buf_m[t] = momentum_now
        buf_w[t] = weights[layer] - 0.05 * momentum_now
        for k, (buf, out) in enumerate(((buf_b, new_b), (buf_m, new_m), (buf_w, new_w))):
            copies.append(pltpu.make_async_copy(buf.at[t], out.at[layer], sems.at[3 * t + k]))
            copies[-1].start()
    return copies


def last_mine_kernel(replicas, right_half, factor, weights, momentum, left, inverse, *refs):
    core = lax.rem(lax.axis_index("tp"), 2)
    copies = last_kernel(core, right_half, factor, weights, momentum, refs[:3], refs[4:])
    solve_left(replicas, inverse, left, 1 - core, refs[3])
    for copy in copies:
        copy.wait()


def last_other_kernel(right_half, factor, weights, momentum, *refs):
    core = lax.rem(lax.axis_index("tp"), 2)
    for copy in last_kernel(1 - core, right_half, factor, weights, momentum, refs[3:6], refs[6:]):
        copy.wait()


def last_half(kernel, right_half, factor, weights, momentum, *, more=(), outs=()):
    block = pl.BlockSpec(memory_space=pltpu.VMEM)
    anywhere = pl.BlockSpec(memory_space=pl.ANY)
    columns, rows = weights.shape[1:]
    width = right_half.shape[1]
    whole = jax.ShapeDtypeStruct(weights.shape, jnp.float32)
    basis = jax.ShapeDtypeStruct((LAYERS, RANK, width), jnp.float32)
    extra = [jax.ShapeDtypeStruct(factor.shape, jnp.float32)] * bool(more)
    return pl.pallas_call(
        kernel,
        out_shape=[whole, basis, whole] + extra,
        in_specs=[block] * (4 + len(more)) + [anywhere] * len(outs),
        out_specs=[anywhere] * 3 + [block] * len(extra),
        scratch_shapes=[
            pltpu.VMEM((2, columns, rows), jnp.float32),
            pltpu.VMEM((2, RANK, width), jnp.float32),
            pltpu.VMEM((2, columns, rows), jnp.float32),
            pltpu.SemaphoreType.DMA((6,)),
        ],
        input_output_aliases={4 + k: k for k in range(len(outs))},
        cost_estimate=pl.CostEstimate(flops=20_000_000, bytes_accessed=1_000_000, transcendentals=0),
        compiler_params=SMALL,
    )(right_half, factor, weights, momentum, *more, *outs)


def one_step(gradients, right_factor, weights_before, momentum):
    width = right_factor.shape[1]
    own, *others = left_parts(gradients, jnp.swapaxes(right_factor, 1, 2))
    one, two, three = to_ring(others, X_RINGS)
    share = sum_of_ring((own + two) + (one + three), Z_RINGS)
    pieces = [share] + to_ring([share] * 3, X_RINGS)

    send, keep_gram, keep_small, left = right_send(gradients, pieces)
    came = lax.ppermute(send, "tp", CORE_PAIRS)
    pair = right_keep(gradients, keep_small) + came[:HALF]
    gram = jnp.broadcast_to((keep_gram + came[HALF:, : 4 * HALF])[None], (8, 8, 4 * HALF))
    packet = jnp.concatenate([pair.reshape(8, 8, width), gram], axis=2)
    packet = lax.all_to_all(packet, "tp", 0, 0, tiled=True, axis_index_groups=CHIP_GROUPS)
    packet = jnp.sum(packet, axis=0)
    replicas = lax.axis_size("dp")
    mine_inverse, mine_factor = inverses(replicas, packet[:, width:], left)
    other_inverse = lax.ppermute(mine_inverse, "tp", CORE_PAIRS)
    share = sum_of_ring(packet[:, :width], X_RINGS)
    share = sum_of_ring(share, Z_RINGS)
    share, other_inverse = lax.optimization_barrier((share, other_inverse))
    mine = lax.all_to_all(
        jnp.broadcast_to(share[None], (8, 8, width)), "tp", 0, 0, tiled=True, axis_index_groups=CHIP_GROUPS
    ).reshape(HALF, width)
    other = lax.ppermute(mine, "tp", CORE_PAIRS)
    state = jnp.swapaxes(weights_before, 1, 2), jnp.swapaxes(momentum, 1, 2)
    *outs, other_factor = last_half(
        lambda *refs: last_mine_kernel(replicas, *refs),
        mine,
        mine_factor,
        *state,
        more=(left, other_inverse),
    )
    outs = last_half(last_other_kernel, other, other_factor, *state, outs=outs)
    return tuple(jnp.swapaxes(array, 1, 2) for array in outs)


def solution(mesh):
    return jax.shard_map(
        one_step,
        mesh=mesh,
        in_specs=(P("dp", None, "tp", None), P(), P(None, "tp", "dp"), P(None, "tp", "dp")),
        out_specs=(P(None, "tp", "dp"), P(), P(None, "tp", "dp")),
        check_vma=False,
    )
```

time: 92.7 us -> 88.5 us (0.955)
  waiting for transfers between devices: 20.1 us -> 14.8 us
    ppermute x15, waiting for transfers between devices: 17.6 us -> 13 us  [to_ring(): got.append(lax.ppermute(array, 'dp', hop(rings, k)))]
    ppermute x1, starting transfers between devices: 0.07 us -> 4.22 us  [one_step(): other_inverse = lax.ppermute(mine_inverse, 'tp', CORE_PAIRS)]
    ppermute x1, starting transfers between devices: 5.71 us -> 2.33 us  [one_step(): other = lax.ppermute(mine, 'tp', CORE_PAIRS)]
    pallas_call x4 -> x6, Pallas kernels: 10.6 us -> 11.1 us  [the longest x1 3.4 us: left_parts(): pl.pallas_call(left_kernel, out_shape=[piece] * 4, in_specs=[pl.BlockSpec...]
  transfers between devices with their start and end apart: 18 -> 18, of which waited for: 11 -> 9; matrix products, arithmetic and copies ran while one was open for 0% -> 0% of each run, Pallas kernels for 3% -> 6%
where the time goes in v1:
time: 88.5 us; the launch traced here: 88.3 us
  starting transfers between devices  40.3 us (46%)
  blocking collectives  21 us (24%)
  waiting for transfers between devices  14.8 us (17%)
  Pallas kernels  11.1 us (13%)
  between operations  0.91 us (1%)
    ppermute x15, starting transfers between devices, to_ring(): got.append(lax.ppermute(array, 'dp', hop(rings, k)))  28.2 us
    ppermute x15, waiting for transfers between devices, to_ring(): got.append(lax.ppermute(array, 'dp', hop(rings, k)))  13 us
    all_to_all x1, blocking collectives, one_step(): lax.all_to_all(packet, 'tp', 0, 0, tiled=True, axis_index_groups=CHIP_GRO...  11.9 us
    all_to_all x1, blocking collectives, one_step(): lax.all_to_all(jnp.broadcast_to(share[None], (8, 8, width)), 'tp', 0, 0,...  9.1 us
    ppermute x1, starting transfers between devices, one_step(): came = lax.ppermute(send, 'tp', CORE_PAIRS)  5.55 us
    ppermute x1, starting transfers between devices, one_step(): other_inverse = lax.ppermute(mine_inverse, 'tp', CORE_PAIRS)  4.22 us
    pallas_call x1, Pallas kernels, left_parts(): pl.pallas_call(left_kernel, out_shape=[piece] * 4, in_specs=[pl.BlockSpec...  3.4 us
    pallas_call x1, Pallas kernels, inverses(): pl.pallas_call(lambda *refs: inverse_kernel(replicas, *refs), out_shape=[...  3.34 us
  transfers between devices with their start and end apart: 18, of which 9 were waited for; matrix products, arithmetic and copies ran while one was open for 0% of the time, Pallas kernels for 6%

profile of v1, /device:TPU:1, one launch (start us, length us, event | category | flops | bytes accessed | tf_op | source)
XLA Modules:
  0.0 88.3 jit_solution(13076322814626439207)
XLA Ops:
  0.6 0.0 copy-start
  0.6 3.4 %left_parts.1 = (f32[80,128]{1,0:T(8,128)S(1)}, f32[80,128]{1,0:T(8,128)S(1)}, f32[80,128]{1,0:T(8,128)S(1)}, f32[80,128]{1,0:T(8,128)S(1)}) custom-call(bf16[1,4,320,1280]{3,2,1,0:T(8,128)(2,1)} %grads.5, f32[4,32,1280]{2,1,0:T(8,128)} %bitcast.16), custom_call_target="tpu_custom_call" | custom-call | tf_op jit(solution)/shard_map/left_parts/pallas_call | solution.py:71
  4.1 3.6 %collective-permute-start = (f32[80,128]{1,0:T(8,128)S(1)}, f32[80,128]{1,0:T(8,128)S(1)}, u32[]{:S(2)}, u32[]{:S(2)}) collective-permute-start(f32[80,128]{1,0:T(8,128)S(1)} %get-tuple-element.23), channel_id=1, source_target_pairs={{0,32},{16,48},{32,0},{48,16},{64,96},{80,112},{96,64},{112,80},{1... | collective-permute-start | bytes 122888 | tf_op jit(solution)/shard_map/ppermute | solution.py:29
  7.7 0.3 collective-permute-start.1
  8.0 2.4 %collective-permute-start.2 = (f32[80,128]{1,0:T(8,128)S(1)}, f32[80,128]{1,0:T(8,128)S(1)}, u32[]{:S(2)}, u32[]{:S(2)}) collective-permute-start(f32[80,128]{1,0:T(8,128)S(1)} %get-tuple-element.25), channel_id=1, source_target_pairs={{0,48},{16,0},{32,16},{48,32},{64,112},{80,64},{96,80},{112,96},{1... | collective-permute-start | bytes 122888 | tf_op jit(solution)/shard_map/ppermute | solution.py:29
  10.4 0.0 collective-permute-done
  10.4 1.7 %collective-permute-done.1 = f32[80,128]{1,0:T(8,128)S(1)} collective-permute-done((f32[80,128]{1,0:T(8,128)S(1)}, f32[80,128]{1,0:T(8,128)S(1)}, u32[]{:S(2)}, u32[]{:S(2)}) %collective-permute-start.1) | collective-permute-done | bytes 40992 | tf_op jit(solution)/shard_map/ppermute | solution.py:29
  12.1 0.0 collective-permute-done.2
  12.1 5.8 %collective-permute-start.5 = (f32[80,128]{1,0:T(8,128)S(1)}, f32[80,128]{1,0:T(8,128)S(1)}, u32[]{:S(2)}, u32[]{:S(2)}) collective-permute-start(f32[80,128]{1,0:T(8,128)S(1)} %add_add_fusion.3), channel_id=1, source_target_pairs={{0,192},{64,0},{128,64},{192,128},{16,208},{80,16},{144,80},{208,1... | collective-permute-start | bytes 122888 | tf_op jit(solution)/shard_map/ppermute | solution.py:29
  17.9 0.0 collective-permute-start.4
  17.9 3.3 %collective-permute-start.3 = (f32[80,128]{1,0:T(8,128)S(1)}, f32[80,128]{1,0:T(8,128)S(1)}, u32[]{:S(2)}, u32[]{:S(2)}) collective-permute-start(f32[80,128]{1,0:T(8,128)S(1)} %add_add_fusion.3), channel_id=1, source_target_pairs={{0,128},{64,192},{128,0},{192,64},{16,144},{80,208},{144,16},{208,... | collective-permute-start | bytes 122888 | tf_op jit(solution)/shard_map/ppermute | solution.py:29
  21.1 0.0 collective-permute-done.5
  21.1 1.7 %collective-permute-done.4 = f32[80,128]{1,0:T(8,128)S(1)} collective-permute-done((f32[80,128]{1,0:T(8,128)S(1)}, f32[80,128]{1,0:T(8,128)S(1)}, u32[]{:S(2)}, u32[]{:S(2)}) %collective-permute-start.4) | collective-permute-done | bytes 40992 | tf_op jit(solution)/shard_map/ppermute | solution.py:29
  22.8 1.8 %collective-permute-done.3 = f32[80,128]{1,0:T(8,128)S(1)} collective-permute-done((f32[80,128]{1,0:T(8,128)S(1)}, f32[80,128]{1,0:T(8,128)S(1)}, u32[]{:S(2)}, u32[]{:S(2)}) %collective-permute-start.3) | collective-permute-done | bytes 40992 | tf_op jit(solution)/shard_map/ppermute | solution.py:29
  24.7 2.7 %collective-permute-start.8 = (f32[80,128]{1,0:T(8,128)S(1)}, f32[80,128]{1,0:T(8,128)S(1)}, u32[]{:S(2)}, u32[]{:S(2)}) collective-permute-start(f32[80,128]{1,0:T(8,128)S(1)} %add_add_fusion.2.own), channel_id=1, source_target_pairs={{0,48},{16,0},{32,16},{48,32},{64,112},{80,64},{96,80},{112,96},{1... | collective-permute-start | bytes 122888 | tf_op jit(solution)/shard_map/ppermute | solution.py:29
  27.4 0.0 collective-permute-start.7
  27.4 0.7 collective-permute-start.6
  28.1 0.4 collective-permute-done.8.three
  28.5 3.4 %collective-permute-done.7.two = f32[80,128]{1,0:T(8,128)S(1)} collective-permute-done((f32[80,128]{1,0:T(8,128)S(1)}, f32[80,128]{1,0:T(8,128)S(1)}, u32[]{:S(2)}, u32[]{:S(2)}) %collective-permute-start.7) | collective-permute-done | bytes 40992 | tf_op jit(solution)/shard_map/ppermute | solution.py:29
  31.9 0.0 collective-permute-done.6.one
  31.9 0.0 copy-done
  31.9 0.8 right_send.1
  32.7 5.5 %collective-permute-start.9 = (f32[72,1280]{1,0:T(8,128)S(1)}, f32[72,1280]{1,0:T(8,128)S(1)}, u32[]{:S(2)}, u32[]{:S(2)}) collective-permute-start(f32[72,1280]{1,0:T(8,128)S(1)} %get-tuple-element.27), channel_id=1, source_target_pairs={{0,1},{1,0},{2,3},{3,2},{4,5},{5,4},{6,7},{7,6},{8,9},{9,8},{10,11... | collective-permute-start | bytes 1105928 | tf_op jit(solution)/shard_map/ppermute | solution.py:289
  38.3 0.4 right_keep.1
  38.6 0.0 copy-start.1
  38.6 0.0 copy-start.2
  38.7 0.9 %collective-permute-done.9 = f32[72,1280]{1,0:T(8,128)S(1)} collective-permute-done((f32[72,1280]{1,0:T(8,128)S(1)}, f32[72,1280]{1,0:T(8,128)S(1)}, u32[]{:S(2)}, u32[]{:S(2)}) %collective-permute-start.9) | collective-permute-done | bytes 368672 | tf_op jit(solution)/shard_map/ppermute | solution.py:289
  39.6 0.1 fusion
  39.7 11.9 %all_to_all.10 = f32[8,8,1536]{2,1,0:T(8,128)S(1)} all-to-all(f32[8,8,1536]{2,1,0:T(8,128)S(1)} %pad_maximum_fusion), channel_id=1, replica_groups={{0,2,4,6,8,10,12,14},{1,3,5,7,9,11,13,15},{16,18,20,22,24,26,28,30},{17..., dimensions={0} | all-to-all | bytes 786432 | tf_op jit(solution)/shard_map/all_to_all | solution.py:293
  51.7 0.1 collective-permute-start.11
  51.8 2.7 %collective-permute-start.12 = (f32[8,1280]{1,0:T(8,128)S(1)}, f32[8,1280]{1,0:T(8,128)S(1)}, u32[]{:S(2)}, u32[]{:S(2)}) collective-permute-start(f32[8,1280]{1,0:T(8,128)S(1)} %slice.18), channel_id=1, source_target_pairs={{0,48},{16,0},{32,16},{48,32},{64,112},{80,64},{96,80},{112,96},{1... | collective-permute-start | bytes 122888 | tf_op jit(solution)/shard_map/ppermute | solution.py:29
  54.4 0.4 collective-permute-start.10
  54.8 1.0 %collective-permute-done.11 = f32[8,1280]{1,0:T(8,128)S(1)} collective-permute-done((f32[8,1280]{1,0:T(8,128)S(1)}, f32[8,1280]{1,0:T(8,128)S(1)}, u32[]{:S(2)}, u32[]{:S(2)}) %collective-permute-start.11) | collective-permute-done | bytes 40992 | tf_op jit(solution)/shard_map/ppermute | solution.py:29
  55.8 0.0 collective-permute-done.12
  55.8 3.0 %collective-permute-done.10 = f32[8,1280]{1,0:T(8,128)S(1)} collective-permute-done((f32[8,1280]{1,0:T(8,128)S(1)}, f32[8,1280]{1,0:T(8,128)S(1)}, u32[]{:S(2)}, u32[]{:S(2)}) %collective-permute-start.10) | collective-permute-done | bytes 40992 | tf_op jit(solution)/shard_map/ppermute | solution.py:29
  58.8 3.9 %collective-permute-start.15 = (f32[8,1280]{1,0:T(8,128)S(1)}, f32[8,1280]{1,0:T(8,128)S(1)}, u32[]{:S(2)}, u32[]{:S(2)}) collective-permute-start(f32[8,1280]{1,0:T(8,128)S(1)} %add_add_fusion.1), channel_id=1, source_target_pairs={{0,192},{64,0},{128,64},{192,128},{16,208},{80,16},{144,80},{208,1... | collective-permute-start | bytes 122888 | tf_op jit(solution)/shard_map/ppermute | solution.py:29
  62.7 0.0 collective-permute-start.14
  62.7 2.3 %collective-permute-start.13 = (f32[8,1280]{1,0:T(8,128)S(1)}, f32[8,1280]{1,0:T(8,128)S(1)}, u32[]{:S(2)}, u32[]{:S(2)}) collective-permute-start(f32[8,1280]{1,0:T(8,128)S(1)} %add_add_fusion.1), channel_id=1, source_target_pairs={{0,128},{64,192},{128,0},{192,64},{16,144},{80,208},{144,16},{208,... | collective-permute-start | bytes 122888 | tf_op jit(solution)/shard_map/ppermute | solution.py:29
  65.1 3.3 %inverses.1 = (f32[32,64]{1,0:T(8,128)S(1)}, f32[64,320]{1,0:T(8,128)S(1)}) custom-call(f32[8,256]{1,0:T(8,128)S(1)} %slice.19.refs_0_, f32[320,128]{1,0:T(8,128)S(1)} %get-tuple-element.29.refs_1_.refs_4_), custom_call_target="tpu_custom_call" | custom-call | flops 20000000 | bytes 32768 | tf_op jit(solution)/shard_map/inverses/pallas_call | solution.py:198
  68.4 4.2 %collective-permute-start.16 = (f32[32,64]{1,0:T(8,128)S(1)}, f32[32,64]{1,0:T(8,128)S(1)}, u32[]{:S(2)}, u32[]{:S(2)}) collective-permute-start(f32[32,64]{1,0:T(8,128)S(1)} %get-tuple-element.30), channel_id=1, source_target_pairs={{0,1},{1,0},{2,3},{3,2},{4,5},{5,4},{6,7},{7,6},{8,9},{9,8},{10,11... | collective-permute-start | bytes 24584 | tf_op jit(solution)/shard_map/ppermute | solution.py:297
  72.6 0.0 collective-permute-done.15
  72.6 0.0 collective-permute-done.14
  72.6 0.0 collective-permute-done.13
  72.7 0.8 collective-permute-done.16.refs_5_
  73.5 9.1 %all_to_all.11 = f32[8,8,1280]{2,1,0:T(8,128)S(1)} all-to-all(f32[8,8,1280]{2,1,0:T(8,128)S(1)} %broadcast_in_dim.5), channel_id=1, replica_groups={{0,2,4,6,8,10,12,14},{1,3,5,7,9,11,13,15},{16,18,20,22,24,26,28,30},{17..., dimensions={0} | all-to-all | bytes 655360 | tf_op jit(solution)/shard_map/all_to_all | solution.py:301
  82.6 2.3 %collective-permute-start.17 = (f32[64,1280]{1,0:T(8,128)S(1)}, f32[64,1280]{1,0:T(8,128)S(1)}, u32[]{:S(2)}, u32[]{:S(2)}) collective-permute-start(f32[64,1280]{1,0:T(8,128)S(1)} %bitcast.13), channel_id=1, source_target_pairs={{0,1},{1,0},{2,3},{3,2},{4,5},{5,4},{6,7},{7,6},{8,9},{9,8},{10,11... | collective-permute-start | bytes 983048 | tf_op jit(solution)/shard_map/ppermute | solution.py:304
  84.9 0.0 copy-done.1
  84.9 0.0 copy-done.2
  84.9 1.7 %shard_map.67 = (f32[4,80,320]{2,1,0:T(8,128)}, f32[4,32,1280]{2,1,0:T(8,128)}, f32[4,80,320]{2,1,0:T(8,128)}, f32[64,320]{1,0:T(8,128)S(1)}) custom-call(f32[64,1280]{1,0:T(8,128)S(1)} %bitcast.14, f32[64,320]{1,0:T(8,128)S(1)} %get-tuple-element.32.refs_1_, f32[4,80,320]{2,1,0:T(8,128)S(1)} %bitcast.9, f32[4,80,320]{2,1,0:T(8,128)S(1)} %bitcast.11, ...), custom_call_target="tpu_custom_call" | custom-call | flops 20000000 | bytes 1000000 | tf_op jit(solution)/shard_map/pallas_call | solution.py:264
  86.6 0.0 collective-permute-done.17.right_half
  86.6 1.5 %shard_map.68 = (f32[4,80,320]{2,1,0:T(8,128)}, f32[4,32,1280]{2,1,0:T(8,128)}, f32[4,80,320]{2,1,0:T(8,128)}) custom-call(f32[64,1280]{1,0:T(8,128)S(1)} %collective-permute-done.17.right_half, f32[64,320]{1,0:T(8,128)S(1)} %get-tuple-element.34.factor, f32[4,80,320]{2,1,0:T(8,128)S(1)} %bitcast.10, ...), custom_call_target="tpu_custom_call", output_to_operand_aliasing={{0}: (4, {}), {1}: (5, {}), {2}: (6, {})} | custom-call | flops 20000000 | bytes 1000000 | tf_op jit(solution)/shard_map/pallas_call | solution.py:264
  (11 shorter events, 0.1 us)
Async XLA Ops:
  0.6 31.3 %copy-start = (bf16[1,4,320,1280]{3,2,1,0:T(8,128)(2,1)S(1)}, bf16[1,4,320,1280]{3,2,1,0:T(8,128)(2,1)}, u32[]{:S(2)}) copy-start(bf16[1,4,320,1280]{3,2,1,0:T(8,128)(2,1)} %grads.5) | copy-start | bytes 9830404
  4.1 6.3 %collective-permute-start = (f32[80,128]{1,0:T(8,128)S(1)}, f32[80,128]{1,0:T(8,128)S(1)}, u32[]{:S(2)}, u32[]{:S(2)}) collective-permute-start(f32[80,128]{1,0:T(8,128)S(1)} %get-tuple-element.23), channel_id=1, source_target_pairs={{0,32},{16,48},{32,0},{48,16},{64,96},{80,112},{96,64},{112,80},{1... | collective-permute-start | bytes 122888 | tf_op jit(solution)/shard_map/ppermute | solution.py:29
  7.7 4.4 %collective-permute-start.1 = (f32[80,128]{1,0:T(8,128)S(1)}, f32[80,128]{1,0:T(8,128)S(1)}, u32[]{:S(2)}, u32[]{:S(2)}) collective-permute-start(f32[80,128]{1,0:T(8,128)S(1)} %get-tuple-element.24), channel_id=1, source_target_pairs={{0,16},{16,32},{32,48},{48,0},{64,80},{80,96},{96,112},{112,64},{1... | collective-permute-start | bytes 122888 | tf_op jit(solution)/shard_map/ppermute | solution.py:29
  8.0 4.1 %collective-permute-start.2 = (f32[80,128]{1,0:T(8,128)S(1)}, f32[80,128]{1,0:T(8,128)S(1)}, u32[]{:S(2)}, u32[]{:S(2)}) collective-permute-start(f32[80,128]{1,0:T(8,128)S(1)} %get-tuple-element.25), channel_id=1, source_target_pairs={{0,48},{16,0},{32,16},{48,32},{64,112},{80,64},{96,80},{112,96},{1... | collective-permute-start | bytes 122888 | tf_op jit(solution)/shard_map/ppermute | solution.py:29
  12.1 9.1 %collective-permute-start.5 = (f32[80,128]{1,0:T(8,128)S(1)}, f32[80,128]{1,0:T(8,128)S(1)}, u32[]{:S(2)}, u32[]{:S(2)}) collective-permute-start(f32[80,128]{1,0:T(8,128)S(1)} %add_add_fusion.3), channel_id=1, source_target_pairs={{0,192},{64,0},{128,64},{192,128},{16,208},{80,16},{144,80},{208,1... | collective-permute-start | bytes 122888 | tf_op jit(solution)/shard_map/ppermute | solution.py:29
  17.9 5.0 %collective-permute-start.4 = (f32[80,128]{1,0:T(8,128)S(1)}, f32[80,128]{1,0:T(8,128)S(1)}, u32[]{:S(2)}, u32[]{:S(2)}) collective-permute-start(f32[80,128]{1,0:T(8,128)S(1)} %add_add_fusion.3), channel_id=1, source_target_pairs={{0,64},{64,128},{128,192},{192,0},{16,80},{80,144},{144,208},{208,... | collective-permute-start | bytes 122888 | tf_op jit(solution)/shard_map/ppermute | solution.py:29
  17.9 6.8 %collective-permute-start.3 = (f32[80,128]{1,0:T(8,128)S(1)}, f32[80,128]{1,0:T(8,128)S(1)}, u32[]{:S(2)}, u32[]{:S(2)}) collective-permute-start(f32[80,128]{1,0:T(8,128)S(1)} %add_add_fusion.3), channel_id=1, source_target_pairs={{0,128},{64,192},{128,0},{192,64},{16,144},{80,208},{144,16},{208,... | collective-permute-start | bytes 122888 | tf_op jit(solution)/shard_map/ppermute | solution.py:29
  24.7 3.8 %collective-permute-start.8 = (f32[80,128]{1,0:T(8,128)S(1)}, f32[80,128]{1,0:T(8,128)S(1)}, u32[]{:S(2)}, u32[]{:S(2)}) collective-permute-start(f32[80,128]{1,0:T(8,128)S(1)} %add_add_fusion.2.own), channel_id=1, source_target_pairs={{0,48},{16,0},{32,16},{48,32},{64,112},{80,64},{96,80},{112,96},{1... | collective-permute-start | bytes 122888 | tf_op jit(solution)/shard_map/ppermute | solution.py:29
  27.4 4.5 %collective-permute-start.7 = (f32[80,128]{1,0:T(8,128)S(1)}, f32[80,128]{1,0:T(8,128)S(1)}, u32[]{:S(2)}, u32[]{:S(2)}) collective-permute-start(f32[80,128]{1,0:T(8,128)S(1)} %add_add_fusion.2.own), channel_id=1, source_target_pairs={{0,32},{16,48},{32,0},{48,16},{64,96},{80,112},{96,64},{112,80},{1... | collective-permute-start | bytes 122888 | tf_op jit(solution)/shard_map/ppermute | solution.py:29
  27.4 4.5 %collective-permute-start.6 = (f32[80,128]{1,0:T(8,128)S(1)}, f32[80,128]{1,0:T(8,128)S(1)}, u32[]{:S(2)}, u32[]{:S(2)}) collective-permute-start(f32[80,128]{1,0:T(8,128)S(1)} %add_add_fusion.2.own), channel_id=1, source_target_pairs={{0,16},{16,32},{32,48},{48,0},{64,80},{80,96},{96,112},{112,64},{1... | collective-permute-start | bytes 122888 | tf_op jit(solution)/shard_map/ppermute | solution.py:29
  32.7 6.9 %collective-permute-start.9 = (f32[72,1280]{1,0:T(8,128)S(1)}, f32[72,1280]{1,0:T(8,128)S(1)}, u32[]{:S(2)}, u32[]{:S(2)}) collective-permute-start(f32[72,1280]{1,0:T(8,128)S(1)} %get-tuple-element.27), channel_id=1, source_target_pairs={{0,1},{1,0},{2,3},{3,2},{4,5},{5,4},{6,7},{7,6},{8,9},{9,8},{10,11... | collective-permute-start | bytes 1105928 | tf_op jit(solution)/shard_map/ppermute | solution.py:289
  38.6 46.3 %copy-start.1 = (f32[4,320,80]{1,2,0:T(8,128)S(1)}, f32[4,320,80]{1,2,0:T(8,128)}, u32[]{:S(2)}) copy-start(f32[4,320,80]{1,2,0:T(8,128)} %param.6) | copy-start | bytes 1228804
  38.6 46.3 %copy-start.2 = (f32[4,320,80]{1,2,0:T(8,128)S(1)}, f32[4,320,80]{1,2,0:T(8,128)}, u32[]{:S(2)}) copy-start(f32[4,320,80]{1,2,0:T(8,128)} %param.7) | copy-start | bytes 1228804
  51.7 4.1 %collective-permute-start.11 = (f32[8,1280]{1,0:T(8,128)S(1)}, f32[8,1280]{1,0:T(8,128)S(1)}, u32[]{:S(2)}, u32[]{:S(2)}) collective-permute-start(f32[8,1280]{1,0:T(8,128)S(1)} %slice.18), channel_id=1, source_target_pairs={{0,16},{16,32},{32,48},{48,0},{64,80},{80,96},{96,112},{112,64},{1... | collective-permute-start | bytes 122888 | tf_op jit(solution)/shard_map/ppermute | solution.py:29
  51.8 4.1 %collective-permute-start.12 = (f32[8,1280]{1,0:T(8,128)S(1)}, f32[8,1280]{1,0:T(8,128)S(1)}, u32[]{:S(2)}, u32[]{:S(2)}) collective-permute-start(f32[8,1280]{1,0:T(8,128)S(1)} %slice.18), channel_id=1, source_target_pairs={{0,48},{16,0},{32,16},{48,32},{64,112},{80,64},{96,80},{112,96},{1... | collective-permute-start | bytes 122888 | tf_op jit(solution)/shard_map/ppermute | solution.py:29
  54.4 4.4 %collective-permute-start.10 = (f32[8,1280]{1,0:T(8,128)S(1)}, f32[8,1280]{1,0:T(8,128)S(1)}, u32[]{:S(2)}, u32[]{:S(2)}) collective-permute-start(f32[8,1280]{1,0:T(8,128)S(1)} %slice.18), channel_id=1, source_target_pairs={{0,32},{16,48},{32,0},{48,16},{64,96},{80,112},{96,64},{112,80},{1... | collective-permute-start | bytes 122888 | tf_op jit(solution)/shard_map/ppermute | solution.py:29
  58.8 13.9 %collective-permute-start.15 = (f32[8,1280]{1,0:T(8,128)S(1)}, f32[8,1280]{1,0:T(8,128)S(1)}, u32[]{:S(2)}, u32[]{:S(2)}) collective-permute-start(f32[8,1280]{1,0:T(8,128)S(1)} %add_add_fusion.1), channel_id=1, source_target_pairs={{0,192},{64,0},{128,64},{192,128},{16,208},{80,16},{144,80},{208,1... | collective-permute-start | bytes 122888 | tf_op jit(solution)/shard_map/ppermute | solution.py:29
  62.7 9.9 %collective-permute-start.14 = (f32[8,1280]{1,0:T(8,128)S(1)}, f32[8,1280]{1,0:T(8,128)S(1)}, u32[]{:S(2)}, u32[]{:S(2)}) collective-permute-start(f32[8,1280]{1,0:T(8,128)S(1)} %add_add_fusion.1), channel_id=1, source_target_pairs={{0,64},{64,128},{128,192},{192,0},{16,80},{80,144},{144,208},{208,... | collective-permute-start | bytes 122888 | tf_op jit(solution)/shard_map/ppermute | solution.py:29
  62.7 9.9 %collective-permute-start.13 = (f32[8,1280]{1,0:T(8,128)S(1)}, f32[8,1280]{1,0:T(8,128)S(1)}, u32[]{:S(2)}, u32[]{:S(2)}) collective-permute-start(f32[8,1280]{1,0:T(8,128)S(1)} %add_add_fusion.1), channel_id=1, source_target_pairs={{0,128},{64,192},{128,0},{192,64},{16,144},{80,208},{144,16},{208,... | collective-permute-start | bytes 122888 | tf_op jit(solution)/shard_map/ppermute | solution.py:29
  68.4 5.1 %collective-permute-start.16 = (f32[32,64]{1,0:T(8,128)S(1)}, f32[32,64]{1,0:T(8,128)S(1)}, u32[]{:S(2)}, u32[]{:S(2)}) collective-permute-start(f32[32,64]{1,0:T(8,128)S(1)} %get-tuple-element.30), channel_id=1, source_target_pairs={{0,1},{1,0},{2,3},{3,2},{4,5},{5,4},{6,7},{7,6},{8,9},{9,8},{10,11... | collective-permute-start | bytes 24584 | tf_op jit(solution)/shard_map/ppermute | solution.py:297
  82.6 4.0 %collective-permute-start.17 = (f32[64,1280]{1,0:T(8,128)S(1)}, f32[64,1280]{1,0:T(8,128)S(1)}, u32[]{:S(2)}, u32[]{:S(2)}) collective-permute-start(f32[64,1280]{1,0:T(8,128)S(1)} %bitcast.13), channel_id=1, source_target_pairs={{0,1},{1,0},{2,3},{3,2},{4,5},{5,4},{6,7},{7,6},{8,9},{9,8},{10,11... | collective-permute-start | bytes 983048 | tf_op jit(solution)/shard_map/ppermute | solution.py:304

commit v2 on v1

--- a/solution.py
+++ b/solution.py
@@ -239,17 +239,17 @@
     return copies
 
 
-def last_mine_kernel(replicas, right_half, factor, weights, momentum, left, inverse, *refs):
+def last_mine_kernel(right_half, factor, weights, momentum, *refs):
     core = lax.rem(lax.axis_index("tp"), 2)
-    copies = last_kernel(core, right_half, factor, weights, momentum, refs[:3], refs[4:])
-    solve_left(replicas, inverse, left, 1 - core, refs[3])
-    for copy in copies:
+    for copy in last_kernel(core, right_half, factor, weights, momentum, refs[:3], refs[3:]):
         copy.wait()
 
 
-def last_other_kernel(right_half, factor, weights, momentum, *refs):
-    core = lax.rem(lax.axis_index("tp"), 2)
-    for copy in last_kernel(1 - core, right_half, factor, weights, momentum, refs[3:6], refs[6:]):
+def last_other_kernel(replicas, right_half, inverse, weights, momentum, left, *refs):
+    other = 1 - lax.rem(lax.axis_index("tp"), 2)
+    factor = refs[-1]
+    solve_left(replicas, inverse, left, other, factor)
+    for copy in last_kernel(other, right_half, factor, weights, momentum, refs[3:6], refs[6:-1]):
         copy.wait()
 
 
@@ -260,19 +260,20 @@
     width = right_half.shape[1]
     whole = jax.ShapeDtypeStruct(weights.shape, jnp.float32)
     basis = jax.ShapeDtypeStruct((LAYERS, RANK, width), jnp.float32)
-    extra = [jax.ShapeDtypeStruct(factor.shape, jnp.float32)] * bool(more)
+    extra = [pltpu.VMEM((HALF, rows), jnp.float32)] * bool(more)
     return pl.pallas_call(
         kernel,
-        out_shape=[whole, basis, whole] + extra,
+        out_shape=[whole, basis, whole],
         in_specs=[block] * (4 + len(more)) + [anywhere] * len(outs),
-        out_specs=[anywhere] * 3 + [block] * len(extra),
+        out_specs=[anywhere] * 3,
         scratch_shapes=[
             pltpu.VMEM((2, columns, rows), jnp.float32),
             pltpu.VMEM((2, RANK, width), jnp.float32),
             pltpu.VMEM((2, columns, rows), jnp.float32),
             pltpu.SemaphoreType.DMA((6,)),
-        ],
-        input_output_aliases={4 + k: k for k in range(len(outs))},
+        ]
+        + extra,
+        input_output_aliases={4 + len(more) + k: k for k in range(len(outs))},
         cost_estimate=pl.CostEstimate(flops=20_000_000, bytes_accessed=1_000_000, transcendentals=0),
         compiler_params=SMALL,
     )(right_half, factor, weights, momentum, *more, *outs)
@@ -294,23 +295,23 @@
     packet = jnp.sum(packet, axis=0)
     replicas = lax.axis_size("dp")
     mine_inverse, mine_factor = inverses(replicas, packet[:, width:], left)
-    other_inverse = lax.ppermute(mine_inverse, "tp", CORE_PAIRS)
     share = sum_of_ring(packet[:, :width], X_RINGS)
     share = sum_of_ring(share, Z_RINGS)
-    share, other_inverse = lax.optimization_barrier((share, other_inverse))
     mine = lax.all_to_all(
         jnp.broadcast_to(share[None], (8, 8, width)), "tp", 0, 0, tiled=True, axis_index_groups=CHIP_GROUPS
     ).reshape(HALF, width)
     other = lax.ppermute(mine, "tp", CORE_PAIRS)
+    other_inverse = lax.ppermute(mine_inverse, "tp", CORE_PAIRS)
     state = jnp.swapaxes(weights_before, 1, 2), jnp.swapaxes(momentum, 1, 2)
-    *outs, other_factor = last_half(
-        lambda *refs: last_mine_kernel(replicas, *refs),
-        mine,
-        mine_factor,
+    outs = last_half(last_mine_kernel, mine, mine_factor, *state)
+    outs = last_half(
+        lambda *refs: last_other_kernel(replicas, *refs),
+        other,
+        other_inverse,
         *state,
-        more=(left, other_inverse),
+        more=(left,),
+        outs=outs,
     )
-    outs = last_half(last_other_kernel, other, other_factor, *state, outs=outs)
     return tuple(jnp.swapaxes(array, 1, 2) for array in outs)
 
 

time: 88.5 us -> 91.8 us (1.037)
  waiting for transfers between devices: 14.8 us -> 18.4 us
    ppermute x15, waiting for transfers between devices: 13 us -> 17.4 us  [to_ring(): got.append(lax.ppermute(array, 'dp', hop(rings, k)))]
    ppermute x1, starting transfers between devices: 4.22 us -> 0.09 us  [one_step(): other_inverse = lax.ppermute(mine_inverse, 'tp', CORE_PAIRS)]
    ppermute x1, starting transfers between devices: 2.33 us -> 5.72 us  [one_step(): other = lax.ppermute(mine, 'tp', CORE_PAIRS)]
  transfers between devices with their start and end apart: 18 -> 18, of which waited for: 9 -> 10; matrix products, arithmetic and copies ran while one was open for 0% -> 0% of each run, Pallas kernels for 6% -> 6%
where the time goes in v2:
time: 91.8 us; the launch traced here: 91.7 us
  starting transfers between devices  39.6 us (43%)
  blocking collectives  21.5 us (23%)
  waiting for transfers between devices  18.4 us (20%)
  Pallas kernels  11.1 us (12%)
  between operations  0.94 us (1%)
    ppermute x15, starting transfers between devices, to_ring(): got.append(lax.ppermute(array, 'dp', hop(rings, k)))  28.2 us
    ppermute x15, waiting for transfers between devices, to_ring(): got.append(lax.ppermute(array, 'dp', hop(rings, k)))  17.4 us
    all_to_all x1, blocking collectives, one_step(): lax.all_to_all(packet, 'tp', 0, 0, tiled=True, axis_index_groups=CHIP_GRO...  11.9 us
    all_to_all x1, blocking collectives, one_step(): lax.all_to_all(jnp.broadcast_to(share[None], (8, 8, width)), 'tp', 0, 0,...  9.54 us
    ppermute x1, starting transfers between devices, one_step(): other = lax.ppermute(mine, 'tp', CORE_PAIRS)  5.72 us
    ppermute x1, starting transfers between devices, one_step(): came = lax.ppermute(send, 'tp', CORE_PAIRS)  5.55 us
    pallas_call x1, Pallas kernels, left_parts(): pl.pallas_call(left_kernel, out_shape=[piece] * 4, in_specs=[pl.BlockSpec...  3.4 us
    pallas_call x1, Pallas kernels, inverses(): pl.pallas_call(lambda *refs: inverse_kernel(replicas, *refs), out_shape=[...  3.34 us
  transfers between devices with their start and end apart: 18, of which 10 were waited for; matrix products, arithmetic and copies ran while one was open for 0% of the time, Pallas kernels for 6%

profile of v2, /device:TPU:1, one launch (start us, length us, event | category | flops | bytes accessed | tf_op | source)
XLA Modules:
  0.0 91.7 jit_solution(12080397507421230992)
XLA Ops:
  0.6 0.0 copy-start
  0.6 3.4 %left_parts.1 = (f32[80,128]{1,0:T(8,128)S(1)}, f32[80,128]{1,0:T(8,128)S(1)}, f32[80,128]{1,0:T(8,128)S(1)}, f32[80,128]{1,0:T(8,128)S(1)}) custom-call(bf16[1,4,320,1280]{3,2,1,0:T(8,128)(2,1)} %grads.5, f32[4,32,1280]{2,1,0:T(8,128)} %bitcast.16), custom_call_target="tpu_custom_call" | custom-call | tf_op jit(solution)/shard_map/left_parts/pallas_call | solution.py:71
  4.1 3.6 %collective-permute-start = (f32[80,128]{1,0:T(8,128)S(1)}, f32[80,128]{1,0:T(8,128)S(1)}, u32[]{:S(2)}, u32[]{:S(2)}) collective-permute-start(f32[80,128]{1,0:T(8,128)S(1)} %get-tuple-element.20), channel_id=1, source_target_pairs={{0,32},{16,48},{32,0},{48,16},{64,96},{80,112},{96,64},{112,80},{1... | collective-permute-start | bytes 122888 | tf_op jit(solution)/shard_map/ppermute | solution.py:29
  7.7 0.3 collective-permute-start.1
  8.0 2.4 %collective-permute-start.2 = (f32[80,128]{1,0:T(8,128)S(1)}, f32[80,128]{1,0:T(8,128)S(1)}, u32[]{:S(2)}, u32[]{:S(2)}) collective-permute-start(f32[80,128]{1,0:T(8,128)S(1)} %get-tuple-element.22), channel_id=1, source_target_pairs={{0,48},{16,0},{32,16},{48,32},{64,112},{80,64},{96,80},{112,96},{1... | collective-permute-start | bytes 122888 | tf_op jit(solution)/shard_map/ppermute | solution.py:29
  10.4 0.0 collective-permute-done
  10.4 1.7 %collective-permute-done.1 = f32[80,128]{1,0:T(8,128)S(1)} collective-permute-done((f32[80,128]{1,0:T(8,128)S(1)}, f32[80,128]{1,0:T(8,128)S(1)}, u32[]{:S(2)}, u32[]{:S(2)}) %collective-permute-start.1) | collective-permute-done | bytes 40992 | tf_op jit(solution)/shard_map/ppermute | solution.py:29
  12.1 0.0 collective-permute-done.2
  12.1 5.8 %collective-permute-start.5 = (f32[80,128]{1,0:T(8,128)S(1)}, f32[80,128]{1,0:T(8,128)S(1)}, u32[]{:S(2)}, u32[]{:S(2)}) collective-permute-start(f32[80,128]{1,0:T(8,128)S(1)} %add_add_fusion.3), channel_id=1, source_target_pairs={{0,192},{64,0},{128,64},{192,128},{16,208},{80,16},{144,80},{208,1... | collective-permute-start | bytes 122888 | tf_op jit(solution)/shard_map/ppermute | solution.py:29
  17.9 0.0 collective-permute-start.4
  17.9 3.3 %collective-permute-start.3 = (f32[80,128]{1,0:T(8,128)S(1)}, f32[80,128]{1,0:T(8,128)S(1)}, u32[]{:S(2)}, u32[]{:S(2)}) collective-permute-start(f32[80,128]{1,0:T(8,128)S(1)} %add_add_fusion.3), channel_id=1, source_target_pairs={{0,128},{64,192},{128,0},{192,64},{16,144},{80,208},{144,16},{208,... | collective-permute-start | bytes 122888 | tf_op jit(solution)/shard_map/ppermute | solution.py:29
  21.1 0.0 collective-permute-done.5
  21.1 1.7 %collective-permute-done.4 = f32[80,128]{1,0:T(8,128)S(1)} collective-permute-done((f32[80,128]{1,0:T(8,128)S(1)}, f32[80,128]{1,0:T(8,128)S(1)}, u32[]{:S(2)}, u32[]{:S(2)}) %collective-permute-start.4) | collective-permute-done | bytes 40992 | tf_op jit(solution)/shard_map/ppermute | solution.py:29
  22.8 1.8 %collective-permute-done.3 = f32[80,128]{1,0:T(8,128)S(1)} collective-permute-done((f32[80,128]{1,0:T(8,128)S(1)}, f32[80,128]{1,0:T(8,128)S(1)}, u32[]{:S(2)}, u32[]{:S(2)}) %collective-permute-start.3) | collective-permute-done | bytes 40992 | tf_op jit(solution)/shard_map/ppermute | solution.py:29
  24.7 2.7 %collective-permute-start.8 = (f32[80,128]{1,0:T(8,128)S(1)}, f32[80,128]{1,0:T(8,128)S(1)}, u32[]{:S(2)}, u32[]{:S(2)}) collective-permute-start(f32[80,128]{1,0:T(8,128)S(1)} %add_add_fusion.2.own), channel_id=1, source_target_pairs={{0,48},{16,0},{32,16},{48,32},{64,112},{80,64},{96,80},{112,96},{1... | collective-permute-start | bytes 122888 | tf_op jit(solution)/shard_map/ppermute | solution.py:29
  27.4 0.0 collective-permute-start.7
  27.4 0.7 collective-permute-start.6
  28.1 0.4 collective-permute-done.8.three
  28.5 3.4 %collective-permute-done.7.two = f32[80,128]{1,0:T(8,128)S(1)} collective-permute-done((f32[80,128]{1,0:T(8,128)S(1)}, f32[80,128]{1,0:T(8,128)S(1)}, u32[]{:S(2)}, u32[]{:S(2)}) %collective-permute-start.7) | collective-permute-done | bytes 40992 | tf_op jit(solution)/shard_map/ppermute | solution.py:29
  31.9 0.0 collective-permute-done.6.one
  31.9 0.0 copy-done
  31.9 0.8 right_send.1
  32.7 5.5 %collective-permute-start.9 = (f32[72,1280]{1,0:T(8,128)S(1)}, f32[72,1280]{1,0:T(8,128)S(1)}, u32[]{:S(2)}, u32[]{:S(2)}) collective-permute-start(f32[72,1280]{1,0:T(8,128)S(1)} %get-tuple-element.24), channel_id=1, source_target_pairs={{0,1},{1,0},{2,3},{3,2},{4,5},{5,4},{6,7},{7,6},{8,9},{9,8},{10,11... | collective-permute-start | bytes 1105928 | tf_op jit(solution)/shard_map/ppermute | solution.py:290
  38.3 0.4 right_keep.1
  38.6 0.0 copy-start.1
  38.6 0.0 copy-start.2
  38.7 0.9 %collective-permute-done.9 = f32[72,1280]{1,0:T(8,128)S(1)} collective-permute-done((f32[72,1280]{1,0:T(8,128)S(1)}, f32[72,1280]{1,0:T(8,128)S(1)}, u32[]{:S(2)}, u32[]{:S(2)}) %collective-permute-start.9) | collective-permute-done | bytes 368672 | tf_op jit(solution)/shard_map/ppermute | solution.py:290
  39.6 0.1 fusion
  39.7 11.9 %all_to_all.10 = f32[8,8,1536]{2,1,0:T(8,128)S(1)} all-to-all(f32[8,8,1536]{2,1,0:T(8,128)S(1)} %pad_maximum_fusion), channel_id=1, replica_groups={{0,2,4,6,8,10,12,14},{1,3,5,7,9,11,13,15},{16,18,20,22,24,26,28,30},{17..., dimensions={0} | all-to-all | bytes 786432 | tf_op jit(solution)/shard_map/all_to_all | solution.py:294
  51.7 0.1 collective-permute-start.11
  51.8 2.7 %collective-permute-start.12 = (f32[8,1280]{1,0:T(8,128)S(1)}, f32[8,1280]{1,0:T(8,128)S(1)}, u32[]{:S(2)}, u32[]{:S(2)}) collective-permute-start(f32[8,1280]{1,0:T(8,128)S(1)} %slice.18), channel_id=1, source_target_pairs={{0,48},{16,0},{32,16},{48,32},{64,112},{80,64},{96,80},{112,96},{1... | collective-permute-start | bytes 122888 | tf_op jit(solution)/shard_map/ppermute | solution.py:29
  54.4 0.4 collective-permute-start.10
  54.8 1.0 %collective-permute-done.11 = f32[8,1280]{1,0:T(8,128)S(1)} collective-permute-done((f32[8,1280]{1,0:T(8,128)S(1)}, f32[8,1280]{1,0:T(8,128)S(1)}, u32[]{:S(2)}, u32[]{:S(2)}) %collective-permute-start.11) | collective-permute-done | bytes 40992 | tf_op jit(solution)/shard_map/ppermute | solution.py:29
  55.8 0.0 collective-permute-done.12
  55.8 3.0 %collective-permute-done.10 = f32[8,1280]{1,0:T(8,128)S(1)} collective-permute-done((f32[8,1280]{1,0:T(8,128)S(1)}, f32[8,1280]{1,0:T(8,128)S(1)}, u32[]{:S(2)}, u32[]{:S(2)}) %collective-permute-start.10) | collective-permute-done | bytes 40992 | tf_op jit(solution)/shard_map/ppermute | solution.py:29
  58.8 3.9 %collective-permute-start.15 = (f32[8,1280]{1,0:T(8,128)S(1)}, f32[8,1280]{1,0:T(8,128)S(1)}, u32[]{:S(2)}, u32[]{:S(2)}) collective-permute-start(f32[8,1280]{1,0:T(8,128)S(1)} %add_add_fusion.1), channel_id=1, source_target_pairs={{0,192},{64,0},{128,64},{192,128},{16,208},{80,16},{144,80},{208,1... | collective-permute-start | bytes 122888 | tf_op jit(solution)/shard_map/ppermute | solution.py:29
  62.7 0.0 collective-permute-start.14
  62.7 2.3 %collective-permute-start.13 = (f32[8,1280]{1,0:T(8,128)S(1)}, f32[8,1280]{1,0:T(8,128)S(1)}, u32[]{:S(2)}, u32[]{:S(2)}) collective-permute-start(f32[8,1280]{1,0:T(8,128)S(1)} %add_add_fusion.1), channel_id=1, source_target_pairs={{0,128},{64,192},{128,0},{192,64},{16,144},{80,208},{144,16},{208,... | collective-permute-start | bytes 122888 | tf_op jit(solution)/shard_map/ppermute | solution.py:29
  65.1 0.0 collective-permute-done.15
  65.1 2.6 %collective-permute-done.14 = f32[8,1280]{1,0:T(8,128)S(1)} collective-permute-done((f32[8,1280]{1,0:T(8,128)S(1)}, f32[8,1280]{1,0:T(8,128)S(1)}, u32[]{:S(2)}, u32[]{:S(2)}) %collective-permute-start.14) | collective-permute-done | bytes 40992 | tf_op jit(solution)/shard_map/ppermute | solution.py:29
  67.7 1.8 %collective-permute-done.13 = f32[8,1280]{1,0:T(8,128)S(1)} collective-permute-done((f32[8,1280]{1,0:T(8,128)S(1)}, f32[8,1280]{1,0:T(8,128)S(1)}, u32[]{:S(2)}, u32[]{:S(2)}) %collective-permute-start.13) | collective-permute-done | bytes 40992 | tf_op jit(solution)/shard_map/ppermute | solution.py:29
  69.5 9.5 %all_to_all.11 = f32[8,8,1280]{2,1,0:T(8,128)S(1)} all-to-all(f32[8,8,1280]{2,1,0:T(8,128)S(1)} %broadcast_in_dim.5), channel_id=1, replica_groups={{0,2,4,6,8,10,12,14},{1,3,5,7,9,11,13,15},{16,18,20,22,24,26,28,30},{17..., dimensions={0} | all-to-all | bytes 655360 | tf_op jit(solution)/shard_map/all_to_all | solution.py:300
  79.1 5.7 %collective-permute-start.16 = (f32[64,1280]{1,0:T(8,128)S(1)}, f32[64,1280]{1,0:T(8,128)S(1)}, u32[]{:S(2)}, u32[]{:S(2)}) collective-permute-start(f32[64,1280]{1,0:T(8,128)S(1)} %bitcast.13), channel_id=1, source_target_pairs={{0,1},{1,0},{2,3},{3,2},{4,5},{5,4},{6,7},{7,6},{8,9},{9,8},{10,11... | collective-permute-start | bytes 983048 | tf_op jit(solution)/shard_map/ppermute | solution.py:303
  84.8 3.3 %inverses.1 = (f32[32,64]{1,0:T(8,128)S(1)}, f32[64,320]{1,0:T(8,128)S(1)}) custom-call(f32[8,256]{1,0:T(8,128)S(1)} %slice.19.refs_0_, f32[320,128]{1,0:T(8,128)S(1)} %get-tuple-element.26.refs_1_.refs_4_), custom_call_target="tpu_custom_call" | custom-call | flops 20000000 | bytes 32768 | tf_op jit(solution)/shard_map/inverses/pallas_call | solution.py:198
  88.2 0.1 collective-permute-start.17
  88.3 0.0 copy-done.1
  88.3 0.0 copy-done.2
  88.3 1.5 %shard_map.67 = (f32[4,80,320]{2,1,0:T(8,128)}, f32[4,32,1280]{2,1,0:T(8,128)}, f32[4,80,320]{2,1,0:T(8,128)}) custom-call(f32[64,1280]{1,0:T(8,128)S(1)} %bitcast.14, f32[64,320]{1,0:T(8,128)S(1)} %get-tuple-element.28.factor, f32[4,80,320]{2,1,0:T(8,128)S(1)} %bitcast.9, f32[4,80,320]{2,1,0:T(8,128)S(1)} %bitcast.11), custom_call_target="tpu_custom_call" | custom-call | flops 20000000 | bytes 1000000 | tf_op jit(solution)/shard_map/pallas_call | solution.py:264
  89.8 0.0 collective-permute-done.17.refs_1_
  89.8 0.0 collective-permute-done.16.refs_0_
  89.8 1.7 %shard_map.68 = (f32[4,80,320]{2,1,0:T(8,128)}, f32[4,32,1280]{2,1,0:T(8,128)}, f32[4,80,320]{2,1,0:T(8,128)}) custom-call(f32[64,1280]{1,0:T(8,128)S(1)} %collective-permute-done.16.refs_0_, f32[32,64]{1,0:T(8,128)S(1)} %collective-permute-done.17.refs_1_, f32[4,80,320]{2,1,0:T(8,128)S(1)} %bitcast.10, ...), custom_call_target="tpu_custom_call", output_to_operand_aliasing={{0}: (5, {}), {1}: (6, {}), {2}: (7, {})} | custom-call | flops 20000000 | bytes 1000000 | tf_op jit(solution)/shard_map/pallas_call | solution.py:264
  (11 shorter events, 0.1 us)
Async XLA Ops:
  0.6 31.3 %copy-start = (bf16[1,4,320,1280]{3,2,1,0:T(8,128)(2,1)S(1)}, bf16[1,4,320,1280]{3,2,1,0:T(8,128)(2,1)}, u32[]{:S(2)}) copy-start(bf16[1,4,320,1280]{3,2,1,0:T(8,128)(2,1)} %grads.5) | copy-start | bytes 9830404
  4.1 6.3 %collective-permute-start = (f32[80,128]{1,0:T(8,128)S(1)}, f32[80,128]{1,0:T(8,128)S(1)}, u32[]{:S(2)}, u32[]{:S(2)}) collective-permute-start(f32[80,128]{1,0:T(8,128)S(1)} %get-tuple-element.20), channel_id=1, source_target_pairs={{0,32},{16,48},{32,0},{48,16},{64,96},{80,112},{96,64},{112,80},{1... | collective-permute-start | bytes 122888 | tf_op jit(solution)/shard_map/ppermute | solution.py:29
  7.7 4.4 %collective-permute-start.1 = (f32[80,128]{1,0:T(8,128)S(1)}, f32[80,128]{1,0:T(8,128)S(1)}, u32[]{:S(2)}, u32[]{:S(2)}) collective-permute-start(f32[80,128]{1,0:T(8,128)S(1)} %get-tuple-element.21), channel_id=1, source_target_pairs={{0,16},{16,32},{32,48},{48,0},{64,80},{80,96},{96,112},{112,64},{1... | collective-permute-start | bytes 122888 | tf_op jit(solution)/shard_map/ppermute | solution.py:29
  8.0 4.1 %collective-permute-start.2 = (f32[80,128]{1,0:T(8,128)S(1)}, f32[80,128]{1,0:T(8,128)S(1)}, u32[]{:S(2)}, u32[]{:S(2)}) collective-permute-start(f32[80,128]{1,0:T(8,128)S(1)} %get-tuple-element.22), channel_id=1, source_target_pairs={{0,48},{16,0},{32,16},{48,32},{64,112},{80,64},{96,80},{112,96},{1... | collective-permute-start | bytes 122888 | tf_op jit(solution)/shard_map/ppermute | solution.py:29
  12.1 9.1 %collective-permute-start.5 = (f32[80,128]{1,0:T(8,128)S(1)}, f32[80,128]{1,0:T(8,128)S(1)}, u32[]{:S(2)}, u32[]{:S(2)}) collective-permute-start(f32[80,128]{1,0:T(8,128)S(1)} %add_add_fusion.3), channel_id=1, source_target_pairs={{0,192},{64,0},{128,64},{192,128},{16,208},{80,16},{144,80},{208,1... | collective-permute-start | bytes 122888 | tf_op jit(solution)/shard_map/ppermute | solution.py:29
  17.9 5.0 %collective-permute-start.4 = (f32[80,128]{1,0:T(8,128)S(1)}, f32[80,128]{1,0:T(8,128)S(1)}, u32[]{:S(2)}, u32[]{:S(2)}) collective-permute-start(f32[80,128]{1,0:T(8,128)S(1)} %add_add_fusion.3), channel_id=1, source_target_pairs={{0,64},{64,128},{128,192},{192,0},{16,80},{80,144},{144,208},{208,... | collective-permute-start | bytes 122888 | tf_op jit(solution)/shard_map/ppermute | solution.py:29
  17.9 6.8 %collective-permute-start.3 = (f32[80,128]{1,0:T(8,128)S(1)}, f32[80,128]{1,0:T(8,128)S(1)}, u32[]{:S(2)}, u32[]{:S(2)}) collective-permute-start(f32[80,128]{1,0:T(8,128)S(1)} %add_add_fusion.3), channel_id=1, source_target_pairs={{0,128},{64,192},{128,0},{192,64},{16,144},{80,208},{144,16},{208,... | collective-permute-start | bytes 122888 | tf_op jit(solution)/shard_map/ppermute | solution.py:29
  24.7 3.8 %collective-permute-start.8 = (f32[80,128]{1,0:T(8,128)S(1)}, f32[80,128]{1,0:T(8,128)S(1)}, u32[]{:S(2)}, u32[]{:S(2)}) collective-permute-start(f32[80,128]{1,0:T(8,128)S(1)} %add_add_fusion.2.own), channel_id=1, source_target_pairs={{0,48},{16,0},{32,16},{48,32},{64,112},{80,64},{96,80},{112,96},{1... | collective-permute-start | bytes 122888 | tf_op jit(solution)/shard_map/ppermute | solution.py:29
  27.4 4.5 %collective-permute-start.7 = (f32[80,128]{1,0:T(8,128)S(1)}, f32[80,128]{1,0:T(8,128)S(1)}, u32[]{:S(2)}, u32[]{:S(2)}) collective-permute-start(f32[80,128]{1,0:T(8,128)S(1)} %add_add_fusion.2.own), channel_id=1, source_target_pairs={{0,32},{16,48},{32,0},{48,16},{64,96},{80,112},{96,64},{112,80},{1... | collective-permute-start | bytes 122888 | tf_op jit(solution)/shard_map/ppermute | solution.py:29
  27.4 4.5 %collective-permute-start.6 = (f32[80,128]{1,0:T(8,128)S(1)}, f32[80,128]{1,0:T(8,128)S(1)}, u32[]{:S(2)}, u32[]{:S(2)}) collective-permute-start(f32[80,128]{1,0:T(8,128)S(1)} %add_add_fusion.2.own), channel_id=1, source_target_pairs={{0,16},{16,32},{32,48},{48,0},{64,80},{80,96},{96,112},{112,64},{1... | collective-permute-start | bytes 122888 | tf_op jit(solution)/shard_map/ppermute | solution.py:29
  32.7 6.9 %collective-permute-start.9 = (f32[72,1280]{1,0:T(8,128)S(1)}, f32[72,1280]{1,0:T(8,128)S(1)}, u32[]{:S(2)}, u32[]{:S(2)}) collective-permute-start(f32[72,1280]{1,0:T(8,128)S(1)} %get-tuple-element.24), channel_id=1, source_target_pairs={{0,1},{1,0},{2,3},{3,2},{4,5},{5,4},{6,7},{7,6},{8,9},{9,8},{10,11... | collective-permute-start | bytes 1105928 | tf_op jit(solution)/shard_map/ppermute | solution.py:290
  38.6 49.6 %copy-start.1 = (f32[4,320,80]{1,2,0:T(8,128)S(1)}, f32[4,320,80]{1,2,0:T(8,128)}, u32[]{:S(2)}) copy-start(f32[4,320,80]{1,2,0:T(8,128)} %param.6) | copy-start | bytes 1228804
  38.6 49.6 %copy-start.2 = (f32[4,320,80]{1,2,0:T(8,128)S(1)}, f32[4,320,80]{1,2,0:T(8,128)}, u32[]{:S(2)}) copy-start(f32[4,320,80]{1,2,0:T(8,128)} %param.7) | copy-start | bytes 1228804
  51.7 4.1 %collective-permute-start.11 = (f32[8,1280]{1,0:T(8,128)S(1)}, f32[8,1280]{1,0:T(8,128)S(1)}, u32[]{:S(2)}, u32[]{:S(2)}) collective-permute-start(f32[8,1280]{1,0:T(8,128)S(1)} %slice.18), channel_id=1, source_target_pairs={{0,16},{16,32},{32,48},{48,0},{64,80},{80,96},{96,112},{112,64},{1... | collective-permute-start | bytes 122888 | tf_op jit(solution)/shard_map/ppermute | solution.py:29
  51.8 4.1 %collective-permute-start.12 = (f32[8,1280]{1,0:T(8,128)S(1)}, f32[8,1280]{1,0:T(8,128)S(1)}, u32[]{:S(2)}, u32[]{:S(2)}) collective-permute-start(f32[8,1280]{1,0:T(8,128)S(1)} %slice.18), channel_id=1, source_target_pairs={{0,48},{16,0},{32,16},{48,32},{64,112},{80,64},{96,80},{112,96},{1... | collective-permute-start | bytes 122888 | tf_op jit(solution)/shard_map/ppermute | solution.py:29
  54.4 4.4 %collective-permute-start.10 = (f32[8,1280]{1,0:T(8,128)S(1)}, f32[8,1280]{1,0:T(8,128)S(1)}, u32[]{:S(2)}, u32[]{:S(2)}) collective-permute-start(f32[8,1280]{1,0:T(8,128)S(1)} %slice.18), channel_id=1, source_target_pairs={{0,32},{16,48},{32,0},{48,16},{64,96},{80,112},{96,64},{112,80},{1... | collective-permute-start | bytes 122888 | tf_op jit(solution)/shard_map/ppermute | solution.py:29
  58.8 6.3 %collective-permute-start.15 = (f32[8,1280]{1,0:T(8,128)S(1)}, f32[8,1280]{1,0:T(8,128)S(1)}, u32[]{:S(2)}, u32[]{:S(2)}) collective-permute-start(f32[8,1280]{1,0:T(8,128)S(1)} %add_add_fusion.1), channel_id=1, source_target_pairs={{0,192},{64,0},{128,64},{192,128},{16,208},{80,16},{144,80},{208,1... | collective-permute-start | bytes 122888 | tf_op jit(solution)/shard_map/ppermute | solution.py:29
  62.7 5.0 %collective-permute-start.14 = (f32[8,1280]{1,0:T(8,128)S(1)}, f32[8,1280]{1,0:T(8,128)S(1)}, u32[]{:S(2)}, u32[]{:S(2)}) collective-permute-start(f32[8,1280]{1,0:T(8,128)S(1)} %add_add_fusion.1), channel_id=1, source_target_pairs={{0,64},{64,128},{128,192},{192,0},{16,80},{80,144},{144,208},{208,... | collective-permute-start | bytes 122888 | tf_op jit(solution)/shard_map/ppermute | solution.py:29
  62.7 6.8 %collective-permute-start.13 = (f32[8,1280]{1,0:T(8,128)S(1)}, f32[8,1280]{1,0:T(8,128)S(1)}, u32[]{:S(2)}, u32[]{:S(2)}) collective-permute-start(f32[8,1280]{1,0:T(8,128)S(1)} %add_add_fusion.1), channel_id=1, source_target_pairs={{0,128},{64,192},{128,0},{192,64},{16,144},{80,208},{144,16},{208,... | collective-permute-start | bytes 122888 | tf_op jit(solution)/shard_map/ppermute | solution.py:29
  79.1 10.7 %collective-permute-start.16 = (f32[64,1280]{1,0:T(8,128)S(1)}, f32[64,1280]{1,0:T(8,128)S(1)}, u32[]{:S(2)}, u32[]{:S(2)}) collective-permute-start(f32[64,1280]{1,0:T(8,128)S(1)} %bitcast.13), channel_id=1, source_target_pairs={{0,1},{1,0},{2,3},{3,2},{4,5},{5,4},{6,7},{7,6},{8,9},{9,8},{10,11... | collective-permute-start | bytes 983048 | tf_op jit(solution)/shard_map/ppermute | solution.py:303
  88.2 1.6 %collective-permute-start.17 = (f32[32,64]{1,0:T(8,128)S(1)}, f32[32,64]{1,0:T(8,128)S(1)}, u32[]{:S(2)}, u32[]{:S(2)}) collective-permute-start(f32[32,64]{1,0:T(8,128)S(1)} %get-tuple-element.27), channel_id=1, source_target_pairs={{0,1},{1,0},{2,3},{3,2},{4,5},{5,4},{6,7},{7,6},{8,9},{9,8},{10,11... | collective-permute-start | bytes 24584 | tf_op jit(solution)/shard_map/ppermute | solution.py:304

commit v3 on v2

--- a/solution.py
+++ b/solution.py
@@ -35,34 +35,23 @@
     return (array + two) + (one + three)
 
 
-def left_kernel(grads, basis, own, one, two, three, total_t, total, held, small, sems):
-    layers = held.shape[0]
-    copies = []
+def left_kernel(grads, basis, own, one, two, three, total_t, total):
+    step = pl.program_id(0)
+    layers = grads.shape[0]
     for l in range(layers):
-        copies.append(
-            (
-                pltpu.make_async_copy(basis.at[l], small.at[l], sems.at[l]),
-                pltpu.make_async_copy(grads.at[0, l], held.at[l], sems.at[layers + l]),
-            )
+        start = pl.multiple_of((step * layers + l) * RANK, RANK)
+        total_t[pl.ds(start, RANK), :] = lax.dot_general(
+            basis[l].astype(jnp.bfloat16), grads[l], (((1,), (1,)), ((), ())), preferred_element_type=jnp.float32
         )
-    for pair in copies:
-        for copy in pair:
-            copy.start()
-    for l, pair in enumerate(copies):
-        for copy in pair:
-            copy.wait()
-        total_t[l * RANK : (l + 1) * RANK, :] = lax.dot_general(
-            small[l].astype(jnp.bfloat16),
-            held[l],
-            (((1,), (1,)), ((), ())),
-            preferred_element_type=jnp.float32,
-        )
-    total[...] = total_t[...].T
-    rows = own.shape[0]
-    x = lax.rem(lax.axis_index("dp"), 4)
-    for step, out in enumerate((own, one, two, three)):
-        start = lax.rem(x + step, 4) * rows
-        out[...] = total[pl.ds(pl.multiple_of(start, 8), rows), :]
+
+    @pl.when(step == pl.num_programs(0) - 1)
+    def _():
+        total[...] = total_t[...].T
+        rows = own.shape[0]
+        x = lax.rem(lax.axis_index("dp"), 4)
+        for back, out in enumerate((own, one, two, three)):
+            start = lax.rem(x + back, 4) * rows
+            out[...] = total[pl.ds(pl.multiple_of(start, 8), rows), :]
 
 
 def left_parts(grads, basis_t):
@@ -71,15 +60,13 @@
     return pl.pallas_call(
         left_kernel,
         out_shape=[piece] * 4,
-        in_specs=[pl.BlockSpec(memory_space=pl.ANY)] * 2,
-        out_specs=[pl.BlockSpec(memory_space=pltpu.VMEM)] * 4,
-        scratch_shapes=[
-            pltpu.VMEM((LR, rows), jnp.float32),
-            pltpu.VMEM((rows, LR), jnp.float32),
-            pltpu.VMEM((layers, rows, width), jnp.bfloat16),
-            pltpu.VMEM((layers, RANK, width), jnp.float32),
-            pltpu.SemaphoreType.DMA((2 * layers,)),
+        grid=(2,),
+        in_specs=[
+            pl.BlockSpec((None, layers // 2, rows, width), lambda l: (0, l, 0, 0)),
+            pl.BlockSpec((layers // 2, RANK, width), lambda l: (l, 0, 0)),
         ],
+        out_specs=[pl.BlockSpec((rows // 4, LR), lambda l: (0, 0))] * 4,
+        scratch_shapes=[pltpu.VMEM((LR, rows), jnp.float32), pltpu.VMEM((rows, LR), jnp.float32)],
         compiler_params=pltpu.CompilerParams(vmem_limit_bytes=54772 * 2**10),
         name="left_parts",
     )(grads, basis_t)
@@ -156,6 +143,10 @@
     )(grads, small)
 
 
+def unpacked(packed):
+    return jnp.concatenate([packed[:, k * HALF : (k + 1) * HALF] for k in range(4)], axis=0)
+
+
 def solve_left(replicas, inverse, left, group, out):
     factor = jnp.where(group == 0, left[:, :HALF], left[:, HALF:])
     for t in range(2):
@@ -173,7 +164,7 @@
 
 
 def inverse_kernel(replicas, packed, left, out, factor):
-    gram = jnp.concatenate([packed[:, k * HALF : (k + 1) * HALF] for k in range(4)], axis=0)
+    gram = unpacked(packed)
     row = lax.broadcasted_iota(jnp.int32, (RANK, HALF), 0)
     lane = lax.broadcasted_iota(jnp.int32, (RANK, HALF), 1)
     inner = lane % RANK
@@ -190,7 +181,8 @@
         pivot = 1.0 / column[k : k + 1, :]
         scaled = jnp.where(inner[:1] == k, 1.0, m[k : k + 1, :]) * pivot
         m = jnp.where(row == k, scaled, jnp.where(inner == k, 0.0, m) - column * scaled)
-    out[...] = m
+    for k in range(4):
+        out[:, k * HALF : (k + 1) * HALF] = m[8 * k : 8 * k + 8, :]
     solve_left(replicas, m, left, lax.rem(lax.axis_index("tp"), 2), factor)
 
 
@@ -198,7 +190,7 @@
     return pl.pallas_call(
         lambda *refs: inverse_kernel(replicas, *refs),
         out_shape=[
-            jax.ShapeDtypeStruct((RANK, HALF), jnp.float32),
+            jax.ShapeDtypeStruct((8, 4 * HALF), jnp.float32),
             jax.ShapeDtypeStruct((HALF, left.shape[0]), jnp.float32),
         ],
         in_specs=[pl.BlockSpec(memory_space=pltpu.VMEM)] * 2,
@@ -245,26 +237,26 @@
         copy.wait()
 
 
-def last_other_kernel(replicas, right_half, inverse, weights, momentum, left, *refs):
+def last_other_kernel(replicas, right_half, left, weights, momentum, *refs):
     other = 1 - lax.rem(lax.axis_index("tp"), 2)
     factor = refs[-1]
-    solve_left(replicas, inverse, left, other, factor)
+    solve_left(replicas, unpacked(right_half[HALF:, : 4 * HALF]), left, other, factor)
     for copy in last_kernel(other, right_half, factor, weights, momentum, refs[3:6], refs[6:-1]):
         copy.wait()
 
 
-def last_half(kernel, right_half, factor, weights, momentum, *, more=(), outs=()):
+def last_half(kernel, right_half, factor, weights, momentum, outs=()):
     block = pl.BlockSpec(memory_space=pltpu.VMEM)
     anywhere = pl.BlockSpec(memory_space=pl.ANY)
     columns, rows = weights.shape[1:]
     width = right_half.shape[1]
     whole = jax.ShapeDtypeStruct(weights.shape, jnp.float32)
     basis = jax.ShapeDtypeStruct((LAYERS, RANK, width), jnp.float32)
-    extra = [pltpu.VMEM((HALF, rows), jnp.float32)] * bool(more)
+    extra = [pltpu.VMEM((HALF, rows), jnp.float32)] * bool(outs)
     return pl.pallas_call(
         kernel,
         out_shape=[whole, basis, whole],
-        in_specs=[block] * (4 + len(more)) + [anywhere] * len(outs),
+        in_specs=[block] * 4 + [anywhere] * len(outs),
         out_specs=[anywhere] * 3,
         scratch_shapes=[
             pltpu.VMEM((2, columns, rows), jnp.float32),
@@ -273,10 +265,10 @@
             pltpu.SemaphoreType.DMA((6,)),
         ]
         + extra,
-        input_output_aliases={4 + len(more) + k: k for k in range(len(outs))},
+        input_output_aliases={4 + k: k for k in range(len(outs))},
         cost_estimate=pl.CostEstimate(flops=20_000_000, bytes_accessed=1_000_000, transcendentals=0),
         compiler_params=SMALL,
-    )(right_half, factor, weights, momentum, *more, *outs)
+    )(right_half, factor, weights, momentum, *outs)
 
 
 def one_step(gradients, right_factor, weights_before, momentum):
@@ -300,18 +292,11 @@
     mine = lax.all_to_all(
         jnp.broadcast_to(share[None], (8, 8, width)), "tp", 0, 0, tiled=True, axis_index_groups=CHIP_GROUPS
     ).reshape(HALF, width)
-    other = lax.ppermute(mine, "tp", CORE_PAIRS)
-    other_inverse = lax.ppermute(mine_inverse, "tp", CORE_PAIRS)
+    going = jnp.concatenate([mine, jnp.pad(mine_inverse, ((0, 0), (0, width - 4 * HALF)))], axis=0)
+    other = lax.ppermute(going, "tp", CORE_PAIRS)
     state = jnp.swapaxes(weights_before, 1, 2), jnp.swapaxes(momentum, 1, 2)
     outs = last_half(last_mine_kernel, mine, mine_factor, *state)
-    outs = last_half(
-        lambda *refs: last_other_kernel(replicas, *refs),
-        other,
-        other_inverse,
-        *state,
-        more=(left,),
-        outs=outs,
-    )
+    outs = last_half(lambda *refs: last_other_kernel(replicas, *refs), other, left, *state, outs)
     return tuple(jnp.swapaxes(array, 1, 2) for array in outs)
 
 

time: 91.8 us -> 89.4 us (0.974)
  blocking collectives: 21.5 us -> 11.9 us
  starting transfers between devices: 39.6 us -> 43.3 us
  waiting for transfers between devices: 18.4 us -> 21.5 us
    all_to_all x1 -> x0, blocking collectives: 9.54 us -> none  [one_step(): lax.all_to_all(jnp.broadcast_to(share[None], (8, 8, width)), 'tp', 0, 0,...]
    all_to_all x0 -> x1, starting transfers between devices: none -> 3.43 us  [one_step(): lax.all_to_all(jnp.broadcast_to(share[None], (8, 8, width)), 'tp', 0, 0,...]
    all_to_all x0 -> x1, waiting for transfers between devices: none -> 2.92 us  [one_step(): lax.all_to_all(jnp.broadcast_to(share[None], (8, 8, width)), 'tp', 0, 0,...]
    ppermute x2 -> x1, starting transfers between devices: 5.81 us -> 6.3 us  [one_step(): other = lax.ppermute(going, 'tp', CORE_PAIRS)]
  transfers between devices with their start and end apart: 18 -> 18, of which waited for: 10 -> 11; matrix products, arithmetic and copies ran while one was open for 0% -> 0% of each run, Pallas kernels for 6% -> 6%
where the time goes in v3:
time: 89.4 us; the launch traced here: 89.2 us
  starting transfers between devices  43.3 us (48%)
  waiting for transfers between devices  21.5 us (24%)
  blocking collectives  11.9 us (13%)
  Pallas kernels  10.6 us (12%)
  between operations  0.92 us (1%)
    ppermute x15, starting transfers between devices, to_ring(): got.append(lax.ppermute(array, 'dp', hop(rings, k)))  28 us
    ppermute x15, waiting for transfers between devices, to_ring(): got.append(lax.ppermute(array, 'dp', hop(rings, k)))  17.6 us
    all_to_all x1, blocking collectives, one_step(): lax.all_to_all(packet, 'tp', 0, 0, tiled=True, axis_index_groups=CHIP_GRO...  11.9 us
    ppermute x1, starting transfers between devices, one_step(): other = lax.ppermute(going, 'tp', CORE_PAIRS)  6.3 us
    ppermute x1, starting transfers between devices, one_step(): came = lax.ppermute(send, 'tp', CORE_PAIRS)  5.55 us
    all_to_all x1, starting transfers between devices, one_step(): lax.all_to_all(jnp.broadcast_to(share[None], (8, 8, width)), 'tp', 0, 0,...  3.43 us
    pallas_call x1, Pallas kernels, inverses(): pl.pallas_call(lambda *refs: inverse_kernel(replicas, *refs), out_shape=[...  3.33 us
    pallas_call x2, Pallas kernels, last_half(): pl.pallas_call(kernel, out_shape=[whole, basis, whole], in_specs=[block]...  3.2 us
  transfers between devices with their start and end apart: 18, of which 11 were waited for; matrix products, arithmetic and copies ran while one was open for 0% of the time, Pallas kernels for 6%

profile of v3, /device:TPU:1, one launch (start us, length us, event | category | flops | bytes accessed | tf_op | source)
XLA Modules:
  0.0 89.2 jit_solution(10077843531212824656)
XLA Ops:
  0.6 0.0 copy-start
  0.6 2.9 %left_parts.1 = (f32[80,128]{1,0:T(8,128)S(1)}, f32[80,128]{1,0:T(8,128)S(1)}, f32[80,128]{1,0:T(8,128)S(1)}, f32[80,128]{1,0:T(8,128)S(1)}) custom-call(bf16[1,4,320,1280]{3,2,1,0:T(8,128)(2,1)} %grads.5, f32[4,32,1280]{2,1,0:T(8,128)} %bitcast.16), custom_call_target="tpu_custom_call" | custom-call | tf_op jit(solution)/shard_map/left_parts/pallas_call | solution.py:60
  3.6 3.6 %collective-permute-start = (f32[80,128]{1,0:T(8,128)S(1)}, f32[80,128]{1,0:T(8,128)S(1)}, u32[]{:S(2)}, u32[]{:S(2)}) collective-permute-start(f32[80,128]{1,0:T(8,128)S(1)} %get-tuple-element.20), channel_id=1, source_target_pairs={{0,32},{16,48},{32,0},{48,16},{64,96},{80,112},{96,64},{112,80},{1... | collective-permute-start | bytes 122888 | tf_op jit(solution)/shard_map/ppermute | solution.py:29
  7.2 0.3 collective-permute-start.1
  7.5 2.4 %collective-permute-start.2 = (f32[80,128]{1,0:T(8,128)S(1)}, f32[80,128]{1,0:T(8,128)S(1)}, u32[]{:S(2)}, u32[]{:S(2)}) collective-permute-start(f32[80,128]{1,0:T(8,128)S(1)} %get-tuple-element.22), channel_id=1, source_target_pairs={{0,48},{16,0},{32,16},{48,32},{64,112},{80,64},{96,80},{112,96},{1... | collective-permute-start | bytes 122888 | tf_op jit(solution)/shard_map/ppermute | solution.py:29
  9.9 0.0 collective-permute-done
  9.9 1.7 %collective-permute-done.1 = f32[80,128]{1,0:T(8,128)S(1)} collective-permute-done((f32[80,128]{1,0:T(8,128)S(1)}, f32[80,128]{1,0:T(8,128)S(1)}, u32[]{:S(2)}, u32[]{:S(2)}) %collective-permute-start.1) | collective-permute-done | bytes 40992 | tf_op jit(solution)/shard_map/ppermute | solution.py:29
  11.6 0.0 collective-permute-done.2
  11.6 5.8 %collective-permute-start.5 = (f32[80,128]{1,0:T(8,128)S(1)}, f32[80,128]{1,0:T(8,128)S(1)}, u32[]{:S(2)}, u32[]{:S(2)}) collective-permute-start(f32[80,128]{1,0:T(8,128)S(1)} %add_add_fusion.3), channel_id=1, source_target_pairs={{0,192},{64,0},{128,64},{192,128},{16,208},{80,16},{144,80},{208,1... | collective-permute-start | bytes 122888 | tf_op jit(solution)/shard_map/ppermute | solution.py:29
  17.4 0.0 collective-permute-start.4
  17.4 3.3 %collective-permute-start.3 = (f32[80,128]{1,0:T(8,128)S(1)}, f32[80,128]{1,0:T(8,128)S(1)}, u32[]{:S(2)}, u32[]{:S(2)}) collective-permute-start(f32[80,128]{1,0:T(8,128)S(1)} %add_add_fusion.3), channel_id=1, source_target_pairs={{0,128},{64,192},{128,0},{192,64},{16,144},{80,208},{144,16},{208,... | collective-permute-start | bytes 122888 | tf_op jit(solution)/shard_map/ppermute | solution.py:29
  20.6 0.0 collective-permute-done.5
  20.6 1.7 %collective-permute-done.4 = f32[80,128]{1,0:T(8,128)S(1)} collective-permute-done((f32[80,128]{1,0:T(8,128)S(1)}, f32[80,128]{1,0:T(8,128)S(1)}, u32[]{:S(2)}, u32[]{:S(2)}) %collective-permute-start.4) | collective-permute-done | bytes 40992 | tf_op jit(solution)/shard_map/ppermute | solution.py:29
  22.4 1.8 %collective-permute-done.3 = f32[80,128]{1,0:T(8,128)S(1)} collective-permute-done((f32[80,128]{1,0:T(8,128)S(1)}, f32[80,128]{1,0:T(8,128)S(1)}, u32[]{:S(2)}, u32[]{:S(2)}) %collective-permute-start.3) | collective-permute-done | bytes 40992 | tf_op jit(solution)/shard_map/ppermute | solution.py:29
  24.2 2.7 %collective-permute-start.8 = (f32[80,128]{1,0:T(8,128)S(1)}, f32[80,128]{1,0:T(8,128)S(1)}, u32[]{:S(2)}, u32[]{:S(2)}) collective-permute-start(f32[80,128]{1,0:T(8,128)S(1)} %add_add_fusion.2.own), channel_id=1, source_target_pairs={{0,48},{16,0},{32,16},{48,32},{64,112},{80,64},{96,80},{112,96},{1... | collective-permute-start | bytes 122888 | tf_op jit(solution)/shard_map/ppermute | solution.py:29
  26.9 0.0 collective-permute-start.7
  26.9 0.7 collective-permute-start.6
  27.6 0.4 collective-permute-done.8.three
  28.0 3.4 %collective-permute-done.7.two = f32[80,128]{1,0:T(8,128)S(1)} collective-permute-done((f32[80,128]{1,0:T(8,128)S(1)}, f32[80,128]{1,0:T(8,128)S(1)}, u32[]{:S(2)}, u32[]{:S(2)}) %collective-permute-start.7) | collective-permute-done | bytes 40992 | tf_op jit(solution)/shard_map/ppermute | solution.py:29
  31.4 0.0 collective-permute-done.6.one
  31.4 0.0 copy-done
  31.4 0.8 right_send.1
  32.2 5.6 %collective-permute-start.9 = (f32[72,1280]{1,0:T(8,128)S(1)}, f32[72,1280]{1,0:T(8,128)S(1)}, u32[]{:S(2)}, u32[]{:S(2)}) collective-permute-start(f32[72,1280]{1,0:T(8,128)S(1)} %get-tuple-element.24), channel_id=1, source_target_pairs={{0,1},{1,0},{2,3},{3,2},{4,5},{5,4},{6,7},{7,6},{8,9},{9,8},{10,11... | collective-permute-start | bytes 1105928 | tf_op jit(solution)/shard_map/ppermute | solution.py:282
  37.8 0.4 right_keep.1
  38.1 0.0 copy-start.1
  38.2 0.0 copy-start.2
  38.2 0.9 %collective-permute-done.9 = f32[72,1280]{1,0:T(8,128)S(1)} collective-permute-done((f32[72,1280]{1,0:T(8,128)S(1)}, f32[72,1280]{1,0:T(8,128)S(1)}, u32[]{:S(2)}, u32[]{:S(2)}) %collective-permute-start.9) | collective-permute-done | bytes 368672 | tf_op jit(solution)/shard_map/ppermute | solution.py:282
  39.1 0.1 fusion
  39.2 11.9 %all_to_all.10 = f32[8,8,1536]{2,1,0:T(8,128)S(1)} all-to-all(f32[8,8,1536]{2,1,0:T(8,128)S(1)} %pad_maximum_fusion), channel_id=1, replica_groups={{0,2,4,6,8,10,12,14},{1,3,5,7,9,11,13,15},{16,18,20,22,24,26,28,30},{17..., dimensions={0} | all-to-all | bytes 786432 | tf_op jit(solution)/shard_map/all_to_all | solution.py:286
  51.2 0.1 collective-permute-start.11
  51.3 2.7 %collective-permute-start.12 = (f32[8,1280]{1,0:T(8,128)S(1)}, f32[8,1280]{1,0:T(8,128)S(1)}, u32[]{:S(2)}, u32[]{:S(2)}) collective-permute-start(f32[8,1280]{1,0:T(8,128)S(1)} %slice.18), channel_id=1, source_target_pairs={{0,48},{16,0},{32,16},{48,32},{64,112},{80,64},{96,80},{112,96},{1... | collective-permute-start | bytes 122888 | tf_op jit(solution)/shard_map/ppermute | solution.py:29
  53.9 0.4 collective-permute-start.10
  54.3 1.0 %collective-permute-done.11 = f32[8,1280]{1,0:T(8,128)S(1)} collective-permute-done((f32[8,1280]{1,0:T(8,128)S(1)}, f32[8,1280]{1,0:T(8,128)S(1)}, u32[]{:S(2)}, u32[]{:S(2)}) %collective-permute-start.11) | collective-permute-done | bytes 40992 | tf_op jit(solution)/shard_map/ppermute | solution.py:29
  55.3 0.0 collective-permute-done.12
  55.3 3.0 %collective-permute-done.10 = f32[8,1280]{1,0:T(8,128)S(1)} collective-permute-done((f32[8,1280]{1,0:T(8,128)S(1)}, f32[8,1280]{1,0:T(8,128)S(1)}, u32[]{:S(2)}, u32[]{:S(2)}) %collective-permute-start.10) | collective-permute-done | bytes 40992 | tf_op jit(solution)/shard_map/ppermute | solution.py:29
  58.3 3.9 %collective-permute-start.15 = (f32[8,1280]{1,0:T(8,128)S(1)}, f32[8,1280]{1,0:T(8,128)S(1)}, u32[]{:S(2)}, u32[]{:S(2)}) collective-permute-start(f32[8,1280]{1,0:T(8,128)S(1)} %add_add_fusion.1), channel_id=1, source_target_pairs={{0,192},{64,0},{128,64},{192,128},{16,208},{80,16},{144,80},{208,1... | collective-permute-start | bytes 122888 | tf_op jit(solution)/shard_map/ppermute | solution.py:29
  62.2 0.0 collective-permute-start.14
  62.2 2.2 %collective-permute-start.13 = (f32[8,1280]{1,0:T(8,128)S(1)}, f32[8,1280]{1,0:T(8,128)S(1)}, u32[]{:S(2)}, u32[]{:S(2)}) collective-permute-start(f32[8,1280]{1,0:T(8,128)S(1)} %add_add_fusion.1), channel_id=1, source_target_pairs={{0,128},{64,192},{128,0},{192,64},{16,144},{80,208},{144,16},{208,... | collective-permute-start | bytes 122888 | tf_op jit(solution)/shard_map/ppermute | solution.py:29
  64.4 0.0 collective-permute-done.15
  64.4 2.8 %collective-permute-done.14 = f32[8,1280]{1,0:T(8,128)S(1)} collective-permute-done((f32[8,1280]{1,0:T(8,128)S(1)}, f32[8,1280]{1,0:T(8,128)S(1)}, u32[]{:S(2)}, u32[]{:S(2)}) %collective-permute-start.14) | collective-permute-done | bytes 40992 | tf_op jit(solution)/shard_map/ppermute | solution.py:29
  67.2 1.8 %collective-permute-done.13 = f32[8,1280]{1,0:T(8,128)S(1)} collective-permute-done((f32[8,1280]{1,0:T(8,128)S(1)}, f32[8,1280]{1,0:T(8,128)S(1)}, u32[]{:S(2)}, u32[]{:S(2)}) %collective-permute-start.13) | collective-permute-done | bytes 40992 | tf_op jit(solution)/shard_map/ppermute | solution.py:29
  69.0 0.7 broadcast_in_dim.5
  69.8 3.4 %all-to-all-start.1 = ((f32[8,8,1280]{2,1,0:T(8,128)}), f32[8,8,1280]{2,1,0:T(8,128)S(1)}, u32[]{:S(2)}, u32[]{:S(2)}) async-start(f32[8,8,1280]{2,1,0:T(8,128)} %broadcast_in_dim.5), calls=%async_computation.1 | async-start | bytes 655360 | tf_op jit(solution)/shard_map/all_to_all | solution.py:292
  73.2 3.3 %inverses.1 = (f32[8,256]{1,0:T(8,128)S(1)}, f32[64,320]{1,0:T(8,128)S(1)}) custom-call(f32[8,256]{1,0:T(8,128)S(1)} %slice.19.refs_0_, f32[320,128]{1,0:T(8,128)S(1)} %get-tuple-element.26.refs_1_), custom_call_target="tpu_custom_call" | custom-call | flops 20000000 | bytes 32768 | tf_op jit(solution)/shard_map/inverses/pallas_call | solution.py:190
  76.6 2.9 %all-to-all-done.1 = f32[8,8,1280]{2,1,0:T(8,128)S(1)} async-done(((f32[8,8,1280]{2,1,0:T(8,128)}), f32[8,8,1280]{2,1,0:T(8,128)S(1)}, u32[]{:S(2)}, u32[]{:S(2)}) %all-to-all-start.1) | async-done | bytes 327712 | tf_op jit(solution)/shard_map/all_to_all | solution.py:292
  79.5 6.3 %collective-permute-start.16 = (f32[72,1280]{1,0:T(8,128)S(1)}, f32[72,1280]{1,0:T(8,128)S(1)}, u32[]{:S(2)}, u32[]{:S(2)}) collective-permute-start(f32[72,1280]{1,0:T(8,128)S(1)} %select_maximum_fusion), channel_id=1, source_target_pairs={{0,1},{1,0},{2,3},{3,2},{4,5},{5,4},{6,7},{7,6},{8,9},{9,8},{10,11... | collective-permute-start | bytes 1105928 | tf_op jit(solution)/shard_map/ppermute | solution.py:296
  85.8 0.0 copy-done.1
  85.8 0.0 copy-done.2
  85.8 1.5 %shard_map.67 = (f32[4,80,320]{2,1,0:T(8,128)}, f32[4,32,1280]{2,1,0:T(8,128)}, f32[4,80,320]{2,1,0:T(8,128)}) custom-call(f32[64,1280]{1,0:T(8,128)S(1)} %bitcast.10, f32[64,320]{1,0:T(8,128)S(1)} %get-tuple-element.28.factor, f32[4,80,320]{2,1,0:T(8,128)S(1)} %bitcast.11, f32[4,80,320]{2,1,0:T(8,128)S(1)} %bitcast.13), custom_call_target="tpu_custom_call" | custom-call | flops 20000000 | bytes 1000000 | tf_op jit(solution)/shard_map/pallas_call | solution.py:256
  87.3 0.0 collective-permute-done.16.refs_0_
  87.3 1.7 %shard_map.68 = (f32[4,80,320]{2,1,0:T(8,128)}, f32[4,32,1280]{2,1,0:T(8,128)}, f32[4,80,320]{2,1,0:T(8,128)}) custom-call(f32[72,1280]{1,0:T(8,128)S(1)} %collective-permute-done.16.refs_0_, f32[320,128]{1,0:T(8,128)S(1)} %get-tuple-element.26.refs_1_, f32[4,80,320]{2,1,0:T(8,128)S(1)} %bitcast.12, ...), custom_call_target="tpu_custom_call", output_to_operand_aliasing={{0}: (4, {}), {1}: (5, {}), {2}: (6, {})} | custom-call | flops 20000000 | bytes 1000000 | tf_op jit(solution)/shard_map/pallas_call | solution.py:256
  (11 shorter events, 0.1 us)
Async XLA Ops:
  0.6 30.8 %copy-start = (bf16[1,4,320,1280]{3,2,1,0:T(8,128)(2,1)S(1)}, bf16[1,4,320,1280]{3,2,1,0:T(8,128)(2,1)}, u32[]{:S(2)}) copy-start(bf16[1,4,320,1280]{3,2,1,0:T(8,128)(2,1)} %grads.5) | copy-start | bytes 9830404
  3.6 6.3 %collective-permute-start = (f32[80,128]{1,0:T(8,128)S(1)}, f32[80,128]{1,0:T(8,128)S(1)}, u32[]{:S(2)}, u32[]{:S(2)}) collective-permute-start(f32[80,128]{1,0:T(8,128)S(1)} %get-tuple-element.20), channel_id=1, source_target_pairs={{0,32},{16,48},{32,0},{48,16},{64,96},{80,112},{96,64},{112,80},{1... | collective-permute-start | bytes 122888 | tf_op jit(solution)/shard_map/ppermute | solution.py:29
  7.2 4.4 %collective-permute-start.1 = (f32[80,128]{1,0:T(8,128)S(1)}, f32[80,128]{1,0:T(8,128)S(1)}, u32[]{:S(2)}, u32[]{:S(2)}) collective-permute-start(f32[80,128]{1,0:T(8,128)S(1)} %get-tuple-element.21), channel_id=1, source_target_pairs={{0,16},{16,32},{32,48},{48,0},{64,80},{80,96},{96,112},{112,64},{1... | collective-permute-start | bytes 122888 | tf_op jit(solution)/shard_map/ppermute | solution.py:29
  7.5 4.1 %collective-permute-start.2 = (f32[80,128]{1,0:T(8,128)S(1)}, f32[80,128]{1,0:T(8,128)S(1)}, u32[]{:S(2)}, u32[]{:S(2)}) collective-permute-start(f32[80,128]{1,0:T(8,128)S(1)} %get-tuple-element.22), channel_id=1, source_target_pairs={{0,48},{16,0},{32,16},{48,32},{64,112},{80,64},{96,80},{112,96},{1... | collective-permute-start | bytes 122888 | tf_op jit(solution)/shard_map/ppermute | solution.py:29
  11.6 9.1 %collective-permute-start.5 = (f32[80,128]{1,0:T(8,128)S(1)}, f32[80,128]{1,0:T(8,128)S(1)}, u32[]{:S(2)}, u32[]{:S(2)}) collective-permute-start(f32[80,128]{1,0:T(8,128)S(1)} %add_add_fusion.3), channel_id=1, source_target_pairs={{0,192},{64,0},{128,64},{192,128},{16,208},{80,16},{144,80},{208,1... | collective-permute-start | bytes 122888 | tf_op jit(solution)/shard_map/ppermute | solution.py:29
  17.4 5.0 %collective-permute-start.4 = (f32[80,128]{1,0:T(8,128)S(1)}, f32[80,128]{1,0:T(8,128)S(1)}, u32[]{:S(2)}, u32[]{:S(2)}) collective-permute-start(f32[80,128]{1,0:T(8,128)S(1)} %add_add_fusion.3), channel_id=1, source_target_pairs={{0,64},{64,128},{128,192},{192,0},{16,80},{80,144},{144,208},{208,... | collective-permute-start | bytes 122888 | tf_op jit(solution)/shard_map/ppermute | solution.py:29
  17.4 6.8 %collective-permute-start.3 = (f32[80,128]{1,0:T(8,128)S(1)}, f32[80,128]{1,0:T(8,128)S(1)}, u32[]{:S(2)}, u32[]{:S(2)}) collective-permute-start(f32[80,128]{1,0:T(8,128)S(1)} %add_add_fusion.3), channel_id=1, source_target_pairs={{0,128},{64,192},{128,0},{192,64},{16,144},{80,208},{144,16},{208,... | collective-permute-start | bytes 122888 | tf_op jit(solution)/shard_map/ppermute | solution.py:29
  24.2 3.8 %collective-permute-start.8 = (f32[80,128]{1,0:T(8,128)S(1)}, f32[80,128]{1,0:T(8,128)S(1)}, u32[]{:S(2)}, u32[]{:S(2)}) collective-permute-start(f32[80,128]{1,0:T(8,128)S(1)} %add_add_fusion.2.own), channel_id=1, source_target_pairs={{0,48},{16,0},{32,16},{48,32},{64,112},{80,64},{96,80},{112,96},{1... | collective-permute-start | bytes 122888 | tf_op jit(solution)/shard_map/ppermute | solution.py:29
  26.9 4.5 %collective-permute-start.7 = (f32[80,128]{1,0:T(8,128)S(1)}, f32[80,128]{1,0:T(8,128)S(1)}, u32[]{:S(2)}, u32[]{:S(2)}) collective-permute-start(f32[80,128]{1,0:T(8,128)S(1)} %add_add_fusion.2.own), channel_id=1, source_target_pairs={{0,32},{16,48},{32,0},{48,16},{64,96},{80,112},{96,64},{112,80},{1... | collective-permute-start | bytes 122888 | tf_op jit(solution)/shard_map/ppermute | solution.py:29
  26.9 4.5 %collective-permute-start.6 = (f32[80,128]{1,0:T(8,128)S(1)}, f32[80,128]{1,0:T(8,128)S(1)}, u32[]{:S(2)}, u32[]{:S(2)}) collective-permute-start(f32[80,128]{1,0:T(8,128)S(1)} %add_add_fusion.2.own), channel_id=1, source_target_pairs={{0,16},{16,32},{32,48},{48,0},{64,80},{80,96},{96,112},{112,64},{1... | collective-permute-start | bytes 122888 | tf_op jit(solution)/shard_map/ppermute | solution.py:29
  32.2 6.9 %collective-permute-start.9 = (f32[72,1280]{1,0:T(8,128)S(1)}, f32[72,1280]{1,0:T(8,128)S(1)}, u32[]{:S(2)}, u32[]{:S(2)}) collective-permute-start(f32[72,1280]{1,0:T(8,128)S(1)} %get-tuple-element.24), channel_id=1, source_target_pairs={{0,1},{1,0},{2,3},{3,2},{4,5},{5,4},{6,7},{7,6},{8,9},{9,8},{10,11... | collective-permute-start | bytes 1105928 | tf_op jit(solution)/shard_map/ppermute | solution.py:282
  38.1 47.7 %copy-start.1 = (f32[4,320,80]{1,2,0:T(8,128)S(1)}, f32[4,320,80]{1,2,0:T(8,128)}, u32[]{:S(2)}) copy-start(f32[4,320,80]{1,2,0:T(8,128)} %param.6) | copy-start | bytes 1228804
  38.2 47.7 %copy-start.2 = (f32[4,320,80]{1,2,0:T(8,128)S(1)}, f32[4,320,80]{1,2,0:T(8,128)}, u32[]{:S(2)}) copy-start(f32[4,320,80]{1,2,0:T(8,128)} %param.7) | copy-start | bytes 1228804
  51.2 4.1 %collective-permute-start.11 = (f32[8,1280]{1,0:T(8,128)S(1)}, f32[8,1280]{1,0:T(8,128)S(1)}, u32[]{:S(2)}, u32[]{:S(2)}) collective-permute-start(f32[8,1280]{1,0:T(8,128)S(1)} %slice.18), channel_id=1, source_target_pairs={{0,16},{16,32},{32,48},{48,0},{64,80},{80,96},{96,112},{112,64},{1... | collective-permute-start | bytes 122888 | tf_op jit(solution)/shard_map/ppermute | solution.py:29
  51.3 4.1 %collective-permute-start.12 = (f32[8,1280]{1,0:T(8,128)S(1)}, f32[8,1280]{1,0:T(8,128)S(1)}, u32[]{:S(2)}, u32[]{:S(2)}) collective-permute-start(f32[8,1280]{1,0:T(8,128)S(1)} %slice.18), channel_id=1, source_target_pairs={{0,48},{16,0},{32,16},{48,32},{64,112},{80,64},{96,80},{112,96},{1... | collective-permute-start | bytes 122888 | tf_op jit(solution)/shard_map/ppermute | solution.py:29
  53.9 4.4 %collective-permute-start.10 = (f32[8,1280]{1,0:T(8,128)S(1)}, f32[8,1280]{1,0:T(8,128)S(1)}, u32[]{:S(2)}, u32[]{:S(2)}) collective-permute-start(f32[8,1280]{1,0:T(8,128)S(1)} %slice.18), channel_id=1, source_target_pairs={{0,32},{16,48},{32,0},{48,16},{64,96},{80,112},{96,64},{112,80},{1... | collective-permute-start | bytes 122888 | tf_op jit(solution)/shard_map/ppermute | solution.py:29
  58.3 6.1 %collective-permute-start.15 = (f32[8,1280]{1,0:T(8,128)S(1)}, f32[8,1280]{1,0:T(8,128)S(1)}, u32[]{:S(2)}, u32[]{:S(2)}) collective-permute-start(f32[8,1280]{1,0:T(8,128)S(1)} %add_add_fusion.1), channel_id=1, source_target_pairs={{0,192},{64,0},{128,64},{192,128},{16,208},{80,16},{144,80},{208,1... | collective-permute-start | bytes 122888 | tf_op jit(solution)/shard_map/ppermute | solution.py:29
  62.2 5.0 %collective-permute-start.14 = (f32[8,1280]{1,0:T(8,128)S(1)}, f32[8,1280]{1,0:T(8,128)S(1)}, u32[]{:S(2)}, u32[]{:S(2)}) collective-permute-start(f32[8,1280]{1,0:T(8,128)S(1)} %add_add_fusion.1), channel_id=1, source_target_pairs={{0,64},{64,128},{128,192},{192,0},{16,80},{80,144},{144,208},{208,... | collective-permute-start | bytes 122888 | tf_op jit(solution)/shard_map/ppermute | solution.py:29
  62.2 6.8 %collective-permute-start.13 = (f32[8,1280]{1,0:T(8,128)S(1)}, f32[8,1280]{1,0:T(8,128)S(1)}, u32[]{:S(2)}, u32[]{:S(2)}) collective-permute-start(f32[8,1280]{1,0:T(8,128)S(1)} %add_add_fusion.1), channel_id=1, source_target_pairs={{0,128},{64,192},{128,0},{192,64},{16,144},{80,208},{144,16},{208,... | collective-permute-start | bytes 122888 | tf_op jit(solution)/shard_map/ppermute | solution.py:29
  69.8 9.7 %all-to-all-start.1 = ((f32[8,8,1280]{2,1,0:T(8,128)}), f32[8,8,1280]{2,1,0:T(8,128)S(1)}, u32[]{:S(2)}, u32[]{:S(2)}) async-start(f32[8,8,1280]{2,1,0:T(8,128)} %broadcast_in_dim.5), calls=%async_computation.1 | async-start | bytes 655360 | tf_op jit(solution)/shard_map/all_to_all | solution.py:292
  79.5 7.8 %collective-permute-start.16 = (f32[72,1280]{1,0:T(8,128)S(1)}, f32[72,1280]{1,0:T(8,128)S(1)}, u32[]{:S(2)}, u32[]{:S(2)}) collective-permute-start(f32[72,1280]{1,0:T(8,128)S(1)} %select_maximum_fusion), channel_id=1, source_target_pairs={{0,1},{1,0},{2,3},{3,2},{4,5},{5,4},{6,7},{7,6},{8,9},{9,8},{10,11... | collective-permute-start | bytes 1105928 | tf_op jit(solution)/shard_map/ppermute | solution.py:296

commit v4 on v3

--- a/solution.py
+++ b/solution.py
@@ -147,13 +147,13 @@
     return jnp.concatenate([packed[:, k * HALF : (k + 1) * HALF] for k in range(4)], axis=0)
 
 
-def solve_left(replicas, inverse, left, group, out):
+def solve_left(replicas, root, left, group, out):
     factor = jnp.where(group == 0, left[:, :HALF], left[:, HALF:])
     for t in range(2):
         lanes = slice(t * RANK, (t + 1) * RANK)
         out[lanes, :] = (
             lax.dot_general(
-                inverse[:, lanes],
+                root[:, lanes],
                 factor[:, lanes],
                 (((1,), (1,)), ((), ())),
                 precision=HIGH,
@@ -163,32 +163,38 @@
         )
 
 
-def inverse_kernel(replicas, packed, left, out, factor):
+def root_kernel(replicas, packed, left, out, factor):
     gram = unpacked(packed)
-    row = lax.broadcasted_iota(jnp.int32, (RANK, HALF), 0)
-    lane = lax.broadcasted_iota(jnp.int32, (RANK, HALF), 1)
-    inner = lane % RANK
-    on_diagonal = inner == row
-    picked = jnp.sum(jnp.where(on_diagonal, gram, 0.0), axis=0, keepdims=True)
-    ridge = jnp.zeros((1, HALF), jnp.float32)
+    row = lax.broadcasted_iota(jnp.int32, (RANK, LR), 0)
+    lane = lax.broadcasted_iota(jnp.int32, (RANK, LR), 1)
+    first = (lane // RANK) % 2 == 0
+    one = jnp.where(lane % RANK == row, 1.0, 0.0)
+    ridge = jnp.zeros((RANK, HALF), jnp.float32)
     for l in range(2):
-        mine = lane[:1] // RANK == l
-        mean = jnp.sum(jnp.where(mine, picked, 0.0), axis=1, keepdims=True) / RANK
-        ridge = jnp.where(mine, mean, ridge)
-    m = gram + jnp.where(on_diagonal, 0.001 * ridge, 0.0)
-    for k in range(RANK):
-        column = jnp.where(lane < RANK, m[:, k : k + 1], m[:, RANK + k : RANK + k + 1])
-        pivot = 1.0 / column[k : k + 1, :]
-        scaled = jnp.where(inner[:1] == k, 1.0, m[k : k + 1, :]) * pivot
-        m = jnp.where(row == k, scaled, jnp.where(inner == k, 0.0, m) - column * scaled)
+        mine = lane[:, :HALF] // RANK == l
+        on_diagonal = mine & (lane[:, :HALF] % RANK == row[:, :HALF])
+        mean = jnp.sum(jnp.where(on_diagonal, gram, 0.0)) / RANK
+        ridge = jnp.where(on_diagonal, 0.001 * mean, ridge)
+    m = jnp.concatenate([gram + ridge, one[:, HALF:]], axis=1)
+    for k in range(RANK - 1):
+        column = jnp.where(first, m[:, k : k + 1], m[:, RANK + k : RANK + k + 1])
+        scale = jnp.where(row > k, column * (1.0 / column[k : k + 1, :]), 0.0)
+        m = m - scale * m[k : k + 1, :]
+    pivots = [
+        jnp.sum(jnp.where(lane == row + l * RANK, m, 0.0), axis=1, keepdims=True) for l in range(2)
+    ]
+    pivot = jnp.where(first, pivots[0], pivots[1])[:, HALF:]
+    shrink = lax.rsqrt(pivot)
+    shrink = shrink * (1.5 - 0.5 * (pivot * shrink) * shrink)
+    root = m[:, HALF:] * shrink
     for k in range(4):
-        out[:, k * HALF : (k + 1) * HALF] = m[8 * k : 8 * k + 8, :]
-    solve_left(replicas, m, left, lax.rem(lax.axis_index("tp"), 2), factor)
-
-
-def inverses(replicas, packed, left):
-    return pl.pallas_call(
-        lambda *refs: inverse_kernel(replicas, *refs),
+        out[:, k * HALF : (k + 1) * HALF] = root[8 * k : 8 * k + 8, :]
+    solve_left(replicas, root, left, lax.rem(lax.axis_index("tp"), 2), factor)
+
+
+def inverse_roots(replicas, packed, left):
+    return pl.pallas_call(
+        lambda *refs: root_kernel(replicas, *refs),
         out_shape=[
             jax.ShapeDtypeStruct((8, 4 * HALF), jnp.float32),
             jax.ShapeDtypeStruct((HALF, left.shape[0]), jnp.float32),
@@ -197,11 +203,11 @@
         out_specs=[pl.BlockSpec(memory_space=pltpu.VMEM)] * 2,
         cost_estimate=pl.CostEstimate(flops=20_000_000, bytes_accessed=32768, transcendentals=0),
         compiler_params=SMALL,
-        name="inverses",
+        name="inverse_roots",
     )(packed, left)
 
 
-def last_kernel(group, right_half, factor, weights, momentum, outs, scratch):
+def last_kernel(group, right_half, root, factor, weights, momentum, outs, scratch):
     new_w, new_b, new_m = outs
     buf_w, buf_b, buf_m, sems = scratch
     columns = weights.shape[1]
@@ -212,7 +218,12 @@
         layer = 2 * group + t
         rows = slice(t * RANK, (t + 1) * RANK)
         right = right_half[rows, :]
-        turned = pltpu.roll(right, lax.rem(width - start, width), 1)[:, :LR]
+        turned = jnp.dot(
+            root[:, rows],
+            pltpu.roll(right, lax.rem(width - start, width), 1)[:, :LR],
+            precision=HIGH,
+            preferred_element_type=jnp.float32,
+        )
         change = lax.dot_general(
             turned,
             factor[rows, :],
@@ -231,32 +242,35 @@
     return copies
 
 
-def last_mine_kernel(right_half, factor, weights, momentum, *refs):
+def last_mine_kernel(right_half, root, factor, weights, momentum, *refs):
     core = lax.rem(lax.axis_index("tp"), 2)
-    for copy in last_kernel(core, right_half, factor, weights, momentum, refs[:3], refs[3:]):
+    root = unpacked(root)
+    for copy in last_kernel(core, right_half, root, factor, weights, momentum, refs[:3], refs[3:]):
         copy.wait()
 
 
 def last_other_kernel(replicas, right_half, left, weights, momentum, *refs):
     other = 1 - lax.rem(lax.axis_index("tp"), 2)
     factor = refs[-1]
-    solve_left(replicas, unpacked(right_half[HALF:, : 4 * HALF]), left, other, factor)
-    for copy in last_kernel(other, right_half, factor, weights, momentum, refs[3:6], refs[6:-1]):
+    root = unpacked(right_half[HALF:, : 4 * HALF])
+    solve_left(replicas, root, left, other, factor)
+    for copy in last_kernel(other, right_half, root, factor, weights, momentum, refs[3:6], refs[6:-1]):
         copy.wait()
 
 
-def last_half(kernel, right_half, factor, weights, momentum, outs=()):
+def last_half(kernel, right_half, operands, weights, momentum, outs=()):
     block = pl.BlockSpec(memory_space=pltpu.VMEM)
     anywhere = pl.BlockSpec(memory_space=pl.ANY)
     columns, rows = weights.shape[1:]
     width = right_half.shape[1]
     whole = jax.ShapeDtypeStruct(weights.shape, jnp.float32)
     basis = jax.ShapeDtypeStruct((LAYERS, RANK, width), jnp.float32)
-    extra = [pltpu.VMEM((HALF, rows), jnp.float32)] * bool(outs)
+    inputs = (right_half, *operands, weights, momentum)
+    factor = [pltpu.VMEM((HALF, rows), jnp.float32)] * bool(outs)
     return pl.pallas_call(
         kernel,
         out_shape=[whole, basis, whole],
-        in_specs=[block] * 4 + [anywhere] * len(outs),
+        in_specs=[block] * len(inputs) + [anywhere] * len(outs),
         out_specs=[anywhere] * 3,
         scratch_shapes=[
             pltpu.VMEM((2, columns, rows), jnp.float32),
@@ -264,11 +278,11 @@
             pltpu.VMEM((2, columns, rows), jnp.float32),
             pltpu.SemaphoreType.DMA((6,)),
         ]
-        + extra,
-        input_output_aliases={4 + k: k for k in range(len(outs))},
+        + factor,
+        input_output_aliases={len(inputs) + k: k for k in range(len(outs))},
         cost_estimate=pl.CostEstimate(flops=20_000_000, bytes_accessed=1_000_000, transcendentals=0),
         compiler_params=SMALL,
-    )(right_half, factor, weights, momentum, *outs)
+    )(*inputs, *outs)
 
 
 def one_step(gradients, right_factor, weights_before, momentum):
@@ -286,17 +300,17 @@
     packet = lax.all_to_all(packet, "tp", 0, 0, tiled=True, axis_index_groups=CHIP_GROUPS)
     packet = jnp.sum(packet, axis=0)
     replicas = lax.axis_size("dp")
-    mine_inverse, mine_factor = inverses(replicas, packet[:, width:], left)
+    root, factor = inverse_roots(replicas, packet[:, width:], left)
     share = sum_of_ring(packet[:, :width], X_RINGS)
     share = sum_of_ring(share, Z_RINGS)
     mine = lax.all_to_all(
         jnp.broadcast_to(share[None], (8, 8, width)), "tp", 0, 0, tiled=True, axis_index_groups=CHIP_GROUPS
     ).reshape(HALF, width)
-    going = jnp.concatenate([mine, jnp.pad(mine_inverse, ((0, 0), (0, width - 4 * HALF)))], axis=0)
+    going = jnp.concatenate([mine, jnp.pad(root, ((0, 0), (0, width - 4 * HALF)))], axis=0)
     other = lax.ppermute(going, "tp", CORE_PAIRS)
     state = jnp.swapaxes(weights_before, 1, 2), jnp.swapaxes(momentum, 1, 2)
-    outs = last_half(last_mine_kernel, mine, mine_factor, *state)
-    outs = last_half(lambda *refs: last_other_kernel(replicas, *refs), other, left, *state, outs)
+    outs = last_half(last_mine_kernel, mine, (root, factor), *state)
+    outs = last_half(lambda *refs: last_other_kernel(replicas, *refs), other, (left,), *state, outs)
     return tuple(jnp.swapaxes(array, 1, 2) for array in outs)
 
 

time: 89.4 us -> 90.2 us (level)
  no operation moved by 1% of the time
where the time goes in v4:
time: 90.2 us; the launch traced here: 89.9 us
  starting transfers between devices  43.3 us (48%)
  waiting for transfers between devices  21.5 us (24%)
  blocking collectives  11.9 us (13%)
  Pallas kernels  11.4 us (13%)
  between operations  0.92 us (1%)
    ppermute x15, starting transfers between devices, to_ring(): got.append(lax.ppermute(array, 'dp', hop(rings, k)))  28 us
    ppermute x15, waiting for transfers between devices, to_ring(): got.append(lax.ppermute(array, 'dp', hop(rings, k)))  17.6 us
    all_to_all x1, blocking collectives, one_step(): lax.all_to_all(packet, 'tp', 0, 0, tiled=True, axis_index_groups=CHIP_GRO...  11.9 us
    ppermute x1, starting transfers between devices, one_step(): other = lax.ppermute(going, 'tp', CORE_PAIRS)  6.3 us
    ppermute x1, starting transfers between devices, one_step(): came = lax.ppermute(send, 'tp', CORE_PAIRS)  5.55 us
    pallas_call x2, Pallas kernels, last_half(): pl.pallas_call(kernel, out_shape=[whole, basis, whole], in_specs=[block]...  3.94 us
    all_to_all x1, starting transfers between devices, one_step(): lax.all_to_all(jnp.broadcast_to(share[None], (8, 8, width)), 'tp', 0, 0,...  3.43 us
    pallas_call x1, Pallas kernels, inverse_roots(): pl.pallas_call(lambda *refs: root_kernel(replicas, *refs), out_shape=[jax...  3.34 us
  transfers between devices with their start and end apart: 18, of which 11 were waited for; matrix products, arithmetic and copies ran while one was open for 0% of the time, Pallas kernels for 6%

profile of v4, /device:TPU:1, one launch (start us, length us, event | category | flops | bytes accessed | tf_op | source)
XLA Modules:
  0.0 89.9 jit_solution(8391631842312197164)
XLA Ops:
  0.6 0.0 copy-start
  0.6 2.9 %left_parts.1 = (f32[80,128]{1,0:T(8,128)S(1)}, f32[80,128]{1,0:T(8,128)S(1)}, f32[80,128]{1,0:T(8,128)S(1)}, f32[80,128]{1,0:T(8,128)S(1)}) custom-call(bf16[1,4,320,1280]{3,2,1,0:T(8,128)(2,1)} %grads.5, f32[4,32,1280]{2,1,0:T(8,128)} %bitcast.16), custom_call_target="tpu_custom_call" | custom-call | tf_op jit(solution)/shard_map/left_parts/pallas_call | solution.py:60
  3.6 3.6 %collective-permute-start = (f32[80,128]{1,0:T(8,128)S(1)}, f32[80,128]{1,0:T(8,128)S(1)}, u32[]{:S(2)}, u32[]{:S(2)}) collective-permute-start(f32[80,128]{1,0:T(8,128)S(1)} %get-tuple-element.20), channel_id=1, source_target_pairs={{0,32},{16,48},{32,0},{48,16},{64,96},{80,112},{96,64},{112,80},{1... | collective-permute-start | bytes 122888 | tf_op jit(solution)/shard_map/ppermute | solution.py:29
  7.2 0.3 collective-permute-start.1
  7.5 2.4 %collective-permute-start.2 = (f32[80,128]{1,0:T(8,128)S(1)}, f32[80,128]{1,0:T(8,128)S(1)}, u32[]{:S(2)}, u32[]{:S(2)}) collective-permute-start(f32[80,128]{1,0:T(8,128)S(1)} %get-tuple-element.22), channel_id=1, source_target_pairs={{0,48},{16,0},{32,16},{48,32},{64,112},{80,64},{96,80},{112,96},{1... | collective-permute-start | bytes 122888 | tf_op jit(solution)/shard_map/ppermute | solution.py:29
  9.9 0.0 collective-permute-done
  9.9 1.7 %collective-permute-done.1 = f32[80,128]{1,0:T(8,128)S(1)} collective-permute-done((f32[80,128]{1,0:T(8,128)S(1)}, f32[80,128]{1,0:T(8,128)S(1)}, u32[]{:S(2)}, u32[]{:S(2)}) %collective-permute-start.1) | collective-permute-done | bytes 40992 | tf_op jit(solution)/shard_map/ppermute | solution.py:29
  11.6 0.0 collective-permute-done.2
  11.6 5.8 %collective-permute-start.5 = (f32[80,128]{1,0:T(8,128)S(1)}, f32[80,128]{1,0:T(8,128)S(1)}, u32[]{:S(2)}, u32[]{:S(2)}) collective-permute-start(f32[80,128]{1,0:T(8,128)S(1)} %add_add_fusion.3), channel_id=1, source_target_pairs={{0,192},{64,0},{128,64},{192,128},{16,208},{80,16},{144,80},{208,1... | collective-permute-start | bytes 122888 | tf_op jit(solution)/shard_map/ppermute | solution.py:29
  17.4 0.0 collective-permute-start.4
  17.4 3.3 %collective-permute-start.3 = (f32[80,128]{1,0:T(8,128)S(1)}, f32[80,128]{1,0:T(8,128)S(1)}, u32[]{:S(2)}, u32[]{:S(2)}) collective-permute-start(f32[80,128]{1,0:T(8,128)S(1)} %add_add_fusion.3), channel_id=1, source_target_pairs={{0,128},{64,192},{128,0},{192,64},{16,144},{80,208},{144,16},{208,... | collective-permute-start | bytes 122888 | tf_op jit(solution)/shard_map/ppermute | solution.py:29
  20.6 0.0 collective-permute-done.5
  20.6 1.7 %collective-permute-done.4 = f32[80,128]{1,0:T(8,128)S(1)} collective-permute-done((f32[80,128]{1,0:T(8,128)S(1)}, f32[80,128]{1,0:T(8,128)S(1)}, u32[]{:S(2)}, u32[]{:S(2)}) %collective-permute-start.4) | collective-permute-done | bytes 40992 | tf_op jit(solution)/shard_map/ppermute | solution.py:29
  22.4 1.8 %collective-permute-done.3 = f32[80,128]{1,0:T(8,128)S(1)} collective-permute-done((f32[80,128]{1,0:T(8,128)S(1)}, f32[80,128]{1,0:T(8,128)S(1)}, u32[]{:S(2)}, u32[]{:S(2)}) %collective-permute-start.3) | collective-permute-done | bytes 40992 | tf_op jit(solution)/shard_map/ppermute | solution.py:29
  24.2 2.7 %collective-permute-start.8 = (f32[80,128]{1,0:T(8,128)S(1)}, f32[80,128]{1,0:T(8,128)S(1)}, u32[]{:S(2)}, u32[]{:S(2)}) collective-permute-start(f32[80,128]{1,0:T(8,128)S(1)} %add_add_fusion.2.own), channel_id=1, source_target_pairs={{0,48},{16,0},{32,16},{48,32},{64,112},{80,64},{96,80},{112,96},{1... | collective-permute-start | bytes 122888 | tf_op jit(solution)/shard_map/ppermute | solution.py:29
  26.9 0.0 collective-permute-start.7
  26.9 0.7 collective-permute-start.6
  27.6 0.4 collective-permute-done.8.three
  28.0 3.4 %collective-permute-done.7.two = f32[80,128]{1,0:T(8,128)S(1)} collective-permute-done((f32[80,128]{1,0:T(8,128)S(1)}, f32[80,128]{1,0:T(8,128)S(1)}, u32[]{:S(2)}, u32[]{:S(2)}) %collective-permute-start.7) | collective-permute-done | bytes 40992 | tf_op jit(solution)/shard_map/ppermute | solution.py:29
  31.4 0.0 collective-permute-done.6.one
  31.4 0.0 copy-done
  31.4 0.8 right_send.1
  32.2 5.6 %collective-permute-start.9 = (f32[72,1280]{1,0:T(8,128)S(1)}, f32[72,1280]{1,0:T(8,128)S(1)}, u32[]{:S(2)}, u32[]{:S(2)}) collective-permute-start(f32[72,1280]{1,0:T(8,128)S(1)} %get-tuple-element.24), channel_id=1, source_target_pairs={{0,1},{1,0},{2,3},{3,2},{4,5},{5,4},{6,7},{7,6},{8,9},{9,8},{10,11... | collective-permute-start | bytes 1105928 | tf_op jit(solution)/shard_map/ppermute | solution.py:296
  37.8 0.4 right_keep.1
  38.1 0.0 copy-start.1
  38.2 0.0 copy-start.2
  38.2 0.9 %collective-permute-done.9 = f32[72,1280]{1,0:T(8,128)S(1)} collective-permute-done((f32[72,1280]{1,0:T(8,128)S(1)}, f32[72,1280]{1,0:T(8,128)S(1)}, u32[]{:S(2)}, u32[]{:S(2)}) %collective-permute-start.9) | collective-permute-done | bytes 368672 | tf_op jit(solution)/shard_map/ppermute | solution.py:296
  39.1 0.1 fusion
  39.2 11.9 %all_to_all.10 = f32[8,8,1536]{2,1,0:T(8,128)S(1)} all-to-all(f32[8,8,1536]{2,1,0:T(8,128)S(1)} %pad_maximum_fusion), channel_id=1, replica_groups={{0,2,4,6,8,10,12,14},{1,3,5,7,9,11,13,15},{16,18,20,22,24,26,28,30},{17..., dimensions={0} | all-to-all | bytes 786432 | tf_op jit(solution)/shard_map/all_to_all | solution.py:300
  51.2 0.1 collective-permute-start.11
  51.3 2.7 %collective-permute-start.12 = (f32[8,1280]{1,0:T(8,128)S(1)}, f32[8,1280]{1,0:T(8,128)S(1)}, u32[]{:S(2)}, u32[]{:S(2)}) collective-permute-start(f32[8,1280]{1,0:T(8,128)S(1)} %slice.18), channel_id=1, source_target_pairs={{0,48},{16,0},{32,16},{48,32},{64,112},{80,64},{96,80},{112,96},{1... | collective-permute-start | bytes 122888 | tf_op jit(solution)/shard_map/ppermute | solution.py:29
  53.9 0.4 collective-permute-start.10
  54.3 1.0 %collective-permute-done.11 = f32[8,1280]{1,0:T(8,128)S(1)} collective-permute-done((f32[8,1280]{1,0:T(8,128)S(1)}, f32[8,1280]{1,0:T(8,128)S(1)}, u32[]{:S(2)}, u32[]{:S(2)}) %collective-permute-start.11) | collective-permute-done | bytes 40992 | tf_op jit(solution)/shard_map/ppermute | solution.py:29
  55.3 0.0 collective-permute-done.12
  55.3 3.0 %collective-permute-done.10 = f32[8,1280]{1,0:T(8,128)S(1)} collective-permute-done((f32[8,1280]{1,0:T(8,128)S(1)}, f32[8,1280]{1,0:T(8,128)S(1)}, u32[]{:S(2)}, u32[]{:S(2)}) %collective-permute-start.10) | collective-permute-done | bytes 40992 | tf_op jit(solution)/shard_map/ppermute | solution.py:29
  58.3 3.9 %collective-permute-start.15 = (f32[8,1280]{1,0:T(8,128)S(1)}, f32[8,1280]{1,0:T(8,128)S(1)}, u32[]{:S(2)}, u32[]{:S(2)}) collective-permute-start(f32[8,1280]{1,0:T(8,128)S(1)} %add_add_fusion.1), channel_id=1, source_target_pairs={{0,192},{64,0},{128,64},{192,128},{16,208},{80,16},{144,80},{208,1... | collective-permute-start | bytes 122888 | tf_op jit(solution)/shard_map/ppermute | solution.py:29
  62.2 0.0 collective-permute-start.14
  62.2 2.2 %collective-permute-start.13 = (f32[8,1280]{1,0:T(8,128)S(1)}, f32[8,1280]{1,0:T(8,128)S(1)}, u32[]{:S(2)}, u32[]{:S(2)}) collective-permute-start(f32[8,1280]{1,0:T(8,128)S(1)} %add_add_fusion.1), channel_id=1, source_target_pairs={{0,128},{64,192},{128,0},{192,64},{16,144},{80,208},{144,16},{208,... | collective-permute-start | bytes 122888 | tf_op jit(solution)/shard_map/ppermute | solution.py:29
  64.4 0.0 collective-permute-done.15
  64.4 2.8 %collective-permute-done.14 = f32[8,1280]{1,0:T(8,128)S(1)} collective-permute-done((f32[8,1280]{1,0:T(8,128)S(1)}, f32[8,1280]{1,0:T(8,128)S(1)}, u32[]{:S(2)}, u32[]{:S(2)}) %collective-permute-start.14) | collective-permute-done | bytes 40992 | tf_op jit(solution)/shard_map/ppermute | solution.py:29
  67.2 1.8 %collective-permute-done.13 = f32[8,1280]{1,0:T(8,128)S(1)} collective-permute-done((f32[8,1280]{1,0:T(8,128)S(1)}, f32[8,1280]{1,0:T(8,128)S(1)}, u32[]{:S(2)}, u32[]{:S(2)}) %collective-permute-start.13) | collective-permute-done | bytes 40992 | tf_op jit(solution)/shard_map/ppermute | solution.py:29
  69.0 0.7 broadcast_in_dim.5
  69.8 3.4 %all-to-all-start.1 = ((f32[8,8,1280]{2,1,0:T(8,128)}), f32[8,8,1280]{2,1,0:T(8,128)S(1)}, u32[]{:S(2)}, u32[]{:S(2)}) async-start(f32[8,8,1280]{2,1,0:T(8,128)} %broadcast_in_dim.5), calls=%async_computation.1 | async-start | bytes 655360 | tf_op jit(solution)/shard_map/all_to_all | solution.py:306
  73.2 3.3 %inverse_roots.1 = (f32[8,256]{1,0:T(8,128)S(1)}, f32[64,320]{1,0:T(8,128)S(1)}) custom-call(f32[8,256]{1,0:T(8,128)S(1)} %slice.19.refs_0_, f32[320,128]{1,0:T(8,128)S(1)} %get-tuple-element.26.refs_1_), custom_call_target="tpu_custom_call" | custom-call | flops 20000000 | bytes 32768 | tf_op jit(solution)/shard_map/inverse_roots/pallas_call | solution.py:196
  76.6 2.9 %all-to-all-done.1 = f32[8,8,1280]{2,1,0:T(8,128)S(1)} async-done(((f32[8,8,1280]{2,1,0:T(8,128)}), f32[8,8,1280]{2,1,0:T(8,128)S(1)}, u32[]{:S(2)}, u32[]{:S(2)}) %all-to-all-start.1) | async-done | bytes 327712 | tf_op jit(solution)/shard_map/all_to_all | solution.py:306
  79.5 6.3 %collective-permute-start.16 = (f32[72,1280]{1,0:T(8,128)S(1)}, f32[72,1280]{1,0:T(8,128)S(1)}, u32[]{:S(2)}, u32[]{:S(2)}) collective-permute-start(f32[72,1280]{1,0:T(8,128)S(1)} %select_maximum_fusion), channel_id=1, source_target_pairs={{0,1},{1,0},{2,3},{3,2},{4,5},{5,4},{6,7},{7,6},{8,9},{9,8},{10,11... | collective-permute-start | bytes 1105928 | tf_op jit(solution)/shard_map/ppermute | solution.py:310
  85.8 0.0 copy-done.1
  85.8 0.0 copy-done.2
  85.8 1.8 %shard_map.67 = (f32[4,80,320]{2,1,0:T(8,128)}, f32[4,32,1280]{2,1,0:T(8,128)}, f32[4,80,320]{2,1,0:T(8,128)}) custom-call(f32[64,1280]{1,0:T(8,128)S(1)} %bitcast.10, f32[8,256]{1,0:T(8,128)S(1)} %get-tuple-element.27.root, f32[64,320]{1,0:T(8,128)S(1)} %get-tuple-element.28.factor, f32[4,80,320]{2,1,0:T(8,128)S(1)} %bitcast.11, f32[4,80,320]{2,1,0:T(8,128)S(1)} %bitcast.13), custom_call_target="tpu_custom_call" | custom-call | flops 20000000 | bytes 1000000 | tf_op jit(solution)/shard_map/pallas_call | solution.py:270
  87.7 0.0 collective-permute-done.16.refs_0_
  87.7 2.1 %shard_map.68 = (f32[4,80,320]{2,1,0:T(8,128)}, f32[4,32,1280]{2,1,0:T(8,128)}, f32[4,80,320]{2,1,0:T(8,128)}) custom-call(f32[72,1280]{1,0:T(8,128)S(1)} %collective-permute-done.16.refs_0_, f32[320,128]{1,0:T(8,128)S(1)} %get-tuple-element.26.refs_1_, f32[4,80,320]{2,1,0:T(8,128)S(1)} %bitcast.12, ...), custom_call_target="tpu_custom_call", output_to_operand_aliasing={{0}: (4, {}), {1}: (5, {}), {2}: (6, {})} | custom-call | flops 20000000 | bytes 1000000 | tf_op jit(solution)/shard_map/pallas_call | solution.py:270
  (11 shorter events, 0.1 us)
Async XLA Ops:
  0.6 30.8 %copy-start = (bf16[1,4,320,1280]{3,2,1,0:T(8,128)(2,1)S(1)}, bf16[1,4,320,1280]{3,2,1,0:T(8,128)(2,1)}, u32[]{:S(2)}) copy-start(bf16[1,4,320,1280]{3,2,1,0:T(8,128)(2,1)} %grads.5) | copy-start | bytes 9830404
  3.6 6.3 %collective-permute-start = (f32[80,128]{1,0:T(8,128)S(1)}, f32[80,128]{1,0:T(8,128)S(1)}, u32[]{:S(2)}, u32[]{:S(2)}) collective-permute-start(f32[80,128]{1,0:T(8,128)S(1)} %get-tuple-element.20), channel_id=1, source_target_pairs={{0,32},{16,48},{32,0},{48,16},{64,96},{80,112},{96,64},{112,80},{1... | collective-permute-start | bytes 122888 | tf_op jit(solution)/shard_map/ppermute | solution.py:29
  7.2 4.4 %collective-permute-start.1 = (f32[80,128]{1,0:T(8,128)S(1)}, f32[80,128]{1,0:T(8,128)S(1)}, u32[]{:S(2)}, u32[]{:S(2)}) collective-permute-start(f32[80,128]{1,0:T(8,128)S(1)} %get-tuple-element.21), channel_id=1, source_target_pairs={{0,16},{16,32},{32,48},{48,0},{64,80},{80,96},{96,112},{112,64},{1... | collective-permute-start | bytes 122888 | tf_op jit(solution)/shard_map/ppermute | solution.py:29
  7.5 4.1 %collective-permute-start.2 = (f32[80,128]{1,0:T(8,128)S(1)}, f32[80,128]{1,0:T(8,128)S(1)}, u32[]{:S(2)}, u32[]{:S(2)}) collective-permute-start(f32[80,128]{1,0:T(8,128)S(1)} %get-tuple-element.22), channel_id=1, source_target_pairs={{0,48},{16,0},{32,16},{48,32},{64,112},{80,64},{96,80},{112,96},{1... | collective-permute-start | bytes 122888 | tf_op jit(solution)/shard_map/ppermute | solution.py:29
  11.6 9.1 %collective-permute-start.5 = (f32[80,128]{1,0:T(8,128)S(1)}, f32[80,128]{1,0:T(8,128)S(1)}, u32[]{:S(2)}, u32[]{:S(2)}) collective-permute-start(f32[80,128]{1,0:T(8,128)S(1)} %add_add_fusion.3), channel_id=1, source_target_pairs={{0,192},{64,0},{128,64},{192,128},{16,208},{80,16},{144,80},{208,1... | collective-permute-start | bytes 122888 | tf_op jit(solution)/shard_map/ppermute | solution.py:29
  17.4 5.0 %collective-permute-start.4 = (f32[80,128]{1,0:T(8,128)S(1)}, f32[80,128]{1,0:T(8,128)S(1)}, u32[]{:S(2)}, u32[]{:S(2)}) collective-permute-start(f32[80,128]{1,0:T(8,128)S(1)} %add_add_fusion.3), channel_id=1, source_target_pairs={{0,64},{64,128},{128,192},{192,0},{16,80},{80,144},{144,208},{208,... | collective-permute-start | bytes 122888 | tf_op jit(solution)/shard_map/ppermute | solution.py:29
  17.4 6.8 %collective-permute-start.3 = (f32[80,128]{1,0:T(8,128)S(1)}, f32[80,128]{1,0:T(8,128)S(1)}, u32[]{:S(2)}, u32[]{:S(2)}) collective-permute-start(f32[80,128]{1,0:T(8,128)S(1)} %add_add_fusion.3), channel_id=1, source_target_pairs={{0,128},{64,192},{128,0},{192,64},{16,144},{80,208},{144,16},{208,... | collective-permute-start | bytes 122888 | tf_op jit(solution)/shard_map/ppermute | solution.py:29
  24.2 3.8 %collective-permute-start.8 = (f32[80,128]{1,0:T(8,128)S(1)}, f32[80,128]{1,0:T(8,128)S(1)}, u32[]{:S(2)}, u32[]{:S(2)}) collective-permute-start(f32[80,128]{1,0:T(8,128)S(1)} %add_add_fusion.2.own), channel_id=1, source_target_pairs={{0,48},{16,0},{32,16},{48,32},{64,112},{80,64},{96,80},{112,96},{1... | collective-permute-start | bytes 122888 | tf_op jit(solution)/shard_map/ppermute | solution.py:29
  26.9 4.5 %collective-permute-start.7 = (f32[80,128]{1,0:T(8,128)S(1)}, f32[80,128]{1,0:T(8,128)S(1)}, u32[]{:S(2)}, u32[]{:S(2)}) collective-permute-start(f32[80,128]{1,0:T(8,128)S(1)} %add_add_fusion.2.own), channel_id=1, source_target_pairs={{0,32},{16,48},{32,0},{48,16},{64,96},{80,112},{96,64},{112,80},{1... | collective-permute-start | bytes 122888 | tf_op jit(solution)/shard_map/ppermute | solution.py:29
  26.9 4.5 %collective-permute-start.6 = (f32[80,128]{1,0:T(8,128)S(1)}, f32[80,128]{1,0:T(8,128)S(1)}, u32[]{:S(2)}, u32[]{:S(2)}) collective-permute-start(f32[80,128]{1,0:T(8,128)S(1)} %add_add_fusion.2.own), channel_id=1, source_target_pairs={{0,16},{16,32},{32,48},{48,0},{64,80},{80,96},{96,112},{112,64},{1... | collective-permute-start | bytes 122888 | tf_op jit(solution)/shard_map/ppermute | solution.py:29
  32.2 6.9 %collective-permute-start.9 = (f32[72,1280]{1,0:T(8,128)S(1)}, f32[72,1280]{1,0:T(8,128)S(1)}, u32[]{:S(2)}, u32[]{:S(2)}) collective-permute-start(f32[72,1280]{1,0:T(8,128)S(1)} %get-tuple-element.24), channel_id=1, source_target_pairs={{0,1},{1,0},{2,3},{3,2},{4,5},{5,4},{6,7},{7,6},{8,9},{9,8},{10,11... | collective-permute-start | bytes 1105928 | tf_op jit(solution)/shard_map/ppermute | solution.py:296
  38.1 47.7 %copy-start.1 = (f32[4,320,80]{1,2,0:T(8,128)S(1)}, f32[4,320,80]{1,2,0:T(8,128)}, u32[]{:S(2)}) copy-start(f32[4,320,80]{1,2,0:T(8,128)} %param.6) | copy-start | bytes 1228804
  38.2 47.7 %copy-start.2 = (f32[4,320,80]{1,2,0:T(8,128)S(1)}, f32[4,320,80]{1,2,0:T(8,128)}, u32[]{:S(2)}) copy-start(f32[4,320,80]{1,2,0:T(8,128)} %param.7) | copy-start | bytes 1228804
  51.2 4.1 %collective-permute-start.11 = (f32[8,1280]{1,0:T(8,128)S(1)}, f32[8,1280]{1,0:T(8,128)S(1)}, u32[]{:S(2)}, u32[]{:S(2)}) collective-permute-start(f32[8,1280]{1,0:T(8,128)S(1)} %slice.18), channel_id=1, source_target_pairs={{0,16},{16,32},{32,48},{48,0},{64,80},{80,96},{96,112},{112,64},{1... | collective-permute-start | bytes 122888 | tf_op jit(solution)/shard_map/ppermute | solution.py:29
  51.3 4.1 %collective-permute-start.12 = (f32[8,1280]{1,0:T(8,128)S(1)}, f32[8,1280]{1,0:T(8,128)S(1)}, u32[]{:S(2)}, u32[]{:S(2)}) collective-permute-start(f32[8,1280]{1,0:T(8,128)S(1)} %slice.18), channel_id=1, source_target_pairs={{0,48},{16,0},{32,16},{48,32},{64,112},{80,64},{96,80},{112,96},{1... | collective-permute-start | bytes 122888 | tf_op jit(solution)/shard_map/ppermute | solution.py:29
  53.9 4.4 %collective-permute-start.10 = (f32[8,1280]{1,0:T(8,128)S(1)}, f32[8,1280]{1,0:T(8,128)S(1)}, u32[]{:S(2)}, u32[]{:S(2)}) collective-permute-start(f32[8,1280]{1,0:T(8,128)S(1)} %slice.18), channel_id=1, source_target_pairs={{0,32},{16,48},{32,0},{48,16},{64,96},{80,112},{96,64},{112,80},{1... | collective-permute-start | bytes 122888 | tf_op jit(solution)/shard_map/ppermute | solution.py:29
  58.3 6.1 %collective-permute-start.15 = (f32[8,1280]{1,0:T(8,128)S(1)}, f32[8,1280]{1,0:T(8,128)S(1)}, u32[]{:S(2)}, u32[]{:S(2)}) collective-permute-start(f32[8,1280]{1,0:T(8,128)S(1)} %add_add_fusion.1), channel_id=1, source_target_pairs={{0,192},{64,0},{128,64},{192,128},{16,208},{80,16},{144,80},{208,1... | collective-permute-start | bytes 122888 | tf_op jit(solution)/shard_map/ppermute | solution.py:29
  62.2 5.0 %collective-permute-start.14 = (f32[8,1280]{1,0:T(8,128)S(1)}, f32[8,1280]{1,0:T(8,128)S(1)}, u32[]{:S(2)}, u32[]{:S(2)}) collective-permute-start(f32[8,1280]{1,0:T(8,128)S(1)} %add_add_fusion.1), channel_id=1, source_target_pairs={{0,64},{64,128},{128,192},{192,0},{16,80},{80,144},{144,208},{208,... | collective-permute-start | bytes 122888 | tf_op jit(solution)/shard_map/ppermute | solution.py:29
  62.2 6.8 %collective-permute-start.13 = (f32[8,1280]{1,0:T(8,128)S(1)}, f32[8,1280]{1,0:T(8,128)S(1)}, u32[]{:S(2)}, u32[]{:S(2)}) collective-permute-start(f32[8,1280]{1,0:T(8,128)S(1)} %add_add_fusion.1), channel_id=1, source_target_pairs={{0,128},{64,192},{128,0},{192,64},{16,144},{80,208},{144,16},{208,... | collective-permute-start | bytes 122888 | tf_op jit(solution)/shard_map/ppermute | solution.py:29
  69.8 9.7 %all-to-all-start.1 = ((f32[8,8,1280]{2,1,0:T(8,128)}), f32[8,8,1280]{2,1,0:T(8,128)S(1)}, u32[]{:S(2)}, u32[]{:S(2)}) async-start(f32[8,8,1280]{2,1,0:T(8,128)} %broadcast_in_dim.5), calls=%async_computation.1 | async-start | bytes 655360 | tf_op jit(solution)/shard_map/all_to_all | solution.py:306
  79.5 8.2 %collective-permute-start.16 = (f32[72,1280]{1,0:T(8,128)S(1)}, f32[72,1280]{1,0:T(8,128)S(1)}, u32[]{:S(2)}, u32[]{:S(2)}) collective-permute-start(f32[72,1280]{1,0:T(8,128)S(1)} %select_maximum_fusion), channel_id=1, source_target_pairs={{0,1},{1,0},{2,3},{3,2},{4,5},{5,4},{6,7},{7,6},{8,9},{9,8},{10,11... | collective-permute-start | bytes 1105928 | tf_op jit(solution)/shard_map/ppermute | solution.py:310

commit v5 on v4

--- a/solution.py
+++ b/solution.py
@@ -207,54 +207,80 @@
     )(packed, left)
 
 
-def last_kernel(group, right_half, root, factor, weights, momentum, outs, scratch):
-    new_w, new_b, new_m = outs
-    buf_w, buf_b, buf_m, sems = scratch
-    columns = weights.shape[1]
+def start_copy(copies, buf, out, layer, t, sem):
+    copies.append(pltpu.make_async_copy(buf.at[t], out.at[layer], sem))
+    copies[-1].start()
+
+
+def basis_part(group, right_half, new_b, buf_b, sems):
+    copies = []
+    width = right_half.shape[1]
+    for t in range(2):
+        right = right_half[t * RANK : (t + 1) * RANK, :]
+        square = jnp.sum(right * right) / (RANK * width)
+        buf_b[t] = right * lax.rsqrt(jnp.full((1, 1), square, jnp.float32) + 1e-12)
+        start_copy(copies, buf_b, new_b, 2 * group + t, t, sems.at[t])
+    return copies
+
+
+def reduced_right(right_half, root, columns):
     width = right_half.shape[1]
     start = lax.axis_index("dp") * columns
-    copies = []
-    for t in range(2):
-        layer = 2 * group + t
-        rows = slice(t * RANK, (t + 1) * RANK)
-        right = right_half[rows, :]
-        turned = jnp.dot(
-            root[:, rows],
-            pltpu.roll(right, lax.rem(width - start, width), 1)[:, :LR],
+    turned = pltpu.roll(right_half[:HALF, :], lax.rem(width - start, width), 1)[:, :LR]
+    return [
+        jnp.dot(
+            root[:, t * RANK : (t + 1) * RANK],
+            turned[t * RANK : (t + 1) * RANK, :],
             precision=HIGH,
             preferred_element_type=jnp.float32,
         )
-        change = lax.dot_general(
-            turned,
-            factor[rows, :],
+        for t in range(2)
+    ]
+
+
+def state_part(group, reduced, factor, weights, momentum, new_w, new_m, buf_w, buf_m, sems):
+    copies = []
+    columns = weights.shape[1]
+    changes = [
+        lax.dot_general(
+            reduced[t][:, :columns],
+            factor[t * RANK : (t + 1) * RANK, :],
             (((0,), (0,)), ((), ())),
             precision=HIGH,
             preferred_element_type=jnp.float32,
-        )[:columns, :]
-        square = jnp.sum(right * right) / (RANK * width)
-        buf_b[t] = right * lax.rsqrt(jnp.full((1, 1), square, jnp.float32) + 1e-12)
+        )
+        for t in range(2)
+    ]
+    for t, change in enumerate(changes):
+        layer = 2 * group + t
         momentum_now = 0.8 * momentum[layer] + change
         buf_m[t] = momentum_now
+        start_copy(copies, buf_m, new_m, layer, t, sems.at[2 + t])
         buf_w[t] = weights[layer] - 0.05 * momentum_now
-        for k, (buf, out) in enumerate(((buf_b, new_b), (buf_m, new_m), (buf_w, new_w))):
-            copies.append(pltpu.make_async_copy(buf.at[t], out.at[layer], sems.at[3 * t + k]))
-            copies[-1].start()
+        start_copy(copies, buf_w, new_w, layer, t, sems.at[4 + t])
     return copies
 
 
-def last_mine_kernel(right_half, root, factor, weights, momentum, *refs):
+def last_mine_kernel(
+    right_half, root, factor, weights, momentum, new_w, new_b, new_m, buf_w, buf_b, buf_m, sems
+):
     core = lax.rem(lax.axis_index("tp"), 2)
-    root = unpacked(root)
-    for copy in last_kernel(core, right_half, root, factor, weights, momentum, refs[:3], refs[3:]):
+    reduced = reduced_right(right_half, unpacked(root), weights.shape[1])
+    copies = basis_part(core, right_half, new_b, buf_b, sems)
+    copies += state_part(core, reduced, factor, weights, momentum, new_w, new_m, buf_w, buf_m, sems)
+    for copy in copies:
         copy.wait()
 
 
 def last_other_kernel(replicas, right_half, left, weights, momentum, *refs):
+    new_w, new_b, new_m, buf_w, buf_b, buf_m, sems, factor = refs[3:]
     other = 1 - lax.rem(lax.axis_index("tp"), 2)
-    factor = refs[-1]
     root = unpacked(right_half[HALF:, : 4 * HALF])
+    reduced = reduced_right(right_half, root, weights.shape[1])
     solve_left(replicas, root, left, other, factor)
-    for copy in last_kernel(other, right_half, root, factor, weights, momentum, refs[3:6], refs[6:-1]):
+    copies = basis_part(other, right_half, new_b, buf_b, sems)
+    copies += state_part(other, reduced, factor, weights, momentum, new_w, new_m, buf_w, buf_m, sems)
+    for copy in copies:
         copy.wait()
 
 

time: 90.2 us -> 89.5 us (level)
  no operation moved by 1% of the time
where the time goes in v5:
time: 89.5 us; the launch traced here: 89.3 us
  starting transfers between devices  43.3 us (48%)
  waiting for transfers between devices  21.5 us (24%)
  blocking collectives  11.9 us (13%)
  Pallas kernels  10.8 us (12%)
  between operations  0.92 us (1%)
    ppermute x15, starting transfers between devices, to_ring(): got.append(lax.ppermute(array, 'dp', hop(rings, k)))  28 us
    ppermute x15, waiting for transfers between devices, to_ring(): got.append(lax.ppermute(array, 'dp', hop(rings, k)))  17.6 us
    all_to_all x1, blocking collectives, one_step(): lax.all_to_all(packet, 'tp', 0, 0, tiled=True, axis_index_groups=CHIP_GRO...  11.9 us
    ppermute x1, starting transfers between devices, one_step(): other = lax.ppermute(going, 'tp', CORE_PAIRS)  6.3 us
    ppermute x1, starting transfers between devices, one_step(): came = lax.ppermute(send, 'tp', CORE_PAIRS)  5.55 us
    all_to_all x1, starting transfers between devices, one_step(): lax.all_to_all(jnp.broadcast_to(share[None], (8, 8, width)), 'tp', 0, 0,...  3.43 us
    pallas_call x1, Pallas kernels, inverse_roots(): pl.pallas_call(lambda *refs: root_kernel(replicas, *refs), out_shape=[jax...  3.34 us
    pallas_call x2, Pallas kernels, last_half(): pl.pallas_call(kernel, out_shape=[whole, basis, whole], in_specs=[block]...  3.33 us
  transfers between devices with their start and end apart: 18, of which 11 were waited for; matrix products, arithmetic and copies ran while one was open for 0% of the time, Pallas kernels for 6%

profile of v5, /device:TPU:1, one launch (start us, length us, event | category | flops | bytes accessed | tf_op | source)
XLA Modules:
  0.0 89.3 jit_solution(7439441967178982470)
XLA Ops:
  0.6 0.0 copy-start
  0.6 2.9 %left_parts.1 = (f32[80,128]{1,0:T(8,128)S(1)}, f32[80,128]{1,0:T(8,128)S(1)}, f32[80,128]{1,0:T(8,128)S(1)}, f32[80,128]{1,0:T(8,128)S(1)}) custom-call(bf16[1,4,320,1280]{3,2,1,0:T(8,128)(2,1)} %grads.5, f32[4,32,1280]{2,1,0:T(8,128)} %bitcast.16), custom_call_target="tpu_custom_call" | custom-call | tf_op jit(solution)/shard_map/left_parts/pallas_call | solution.py:60
  3.6 3.6 %collective-permute-start = (f32[80,128]{1,0:T(8,128)S(1)}, f32[80,128]{1,0:T(8,128)S(1)}, u32[]{:S(2)}, u32[]{:S(2)}) collective-permute-start(f32[80,128]{1,0:T(8,128)S(1)} %get-tuple-element.20), channel_id=1, source_target_pairs={{0,32},{16,48},{32,0},{48,16},{64,96},{80,112},{96,64},{112,80},{1... | collective-permute-start | bytes 122888 | tf_op jit(solution)/shard_map/ppermute | solution.py:29
  7.2 0.3 collective-permute-start.1
  7.5 2.4 %collective-permute-start.2 = (f32[80,128]{1,0:T(8,128)S(1)}, f32[80,128]{1,0:T(8,128)S(1)}, u32[]{:S(2)}, u32[]{:S(2)}) collective-permute-start(f32[80,128]{1,0:T(8,128)S(1)} %get-tuple-element.22), channel_id=1, source_target_pairs={{0,48},{16,0},{32,16},{48,32},{64,112},{80,64},{96,80},{112,96},{1... | collective-permute-start | bytes 122888 | tf_op jit(solution)/shard_map/ppermute | solution.py:29
  9.9 0.0 collective-permute-done
  9.9 1.7 %collective-permute-done.1 = f32[80,128]{1,0:T(8,128)S(1)} collective-permute-done((f32[80,128]{1,0:T(8,128)S(1)}, f32[80,128]{1,0:T(8,128)S(1)}, u32[]{:S(2)}, u32[]{:S(2)}) %collective-permute-start.1) | collective-permute-done | bytes 40992 | tf_op jit(solution)/shard_map/ppermute | solution.py:29
  11.6 0.0 collective-permute-done.2
  11.6 5.8 %collective-permute-start.5 = (f32[80,128]{1,0:T(8,128)S(1)}, f32[80,128]{1,0:T(8,128)S(1)}, u32[]{:S(2)}, u32[]{:S(2)}) collective-permute-start(f32[80,128]{1,0:T(8,128)S(1)} %add_add_fusion.3), channel_id=1, source_target_pairs={{0,192},{64,0},{128,64},{192,128},{16,208},{80,16},{144,80},{208,1... | collective-permute-start | bytes 122888 | tf_op jit(solution)/shard_map/ppermute | solution.py:29
  17.4 0.0 collective-permute-start.4
  17.4 3.3 %collective-permute-start.3 = (f32[80,128]{1,0:T(8,128)S(1)}, f32[80,128]{1,0:T(8,128)S(1)}, u32[]{:S(2)}, u32[]{:S(2)}) collective-permute-start(f32[80,128]{1,0:T(8,128)S(1)} %add_add_fusion.3), channel_id=1, source_target_pairs={{0,128},{64,192},{128,0},{192,64},{16,144},{80,208},{144,16},{208,... | collective-permute-start | bytes 122888 | tf_op jit(solution)/shard_map/ppermute | solution.py:29
  20.6 0.0 collective-permute-done.5
  20.6 1.7 %collective-permute-done.4 = f32[80,128]{1,0:T(8,128)S(1)} collective-permute-done((f32[80,128]{1,0:T(8,128)S(1)}, f32[80,128]{1,0:T(8,128)S(1)}, u32[]{:S(2)}, u32[]{:S(2)}) %collective-permute-start.4) | collective-permute-done | bytes 40992 | tf_op jit(solution)/shard_map/ppermute | solution.py:29
  22.4 1.8 %collective-permute-done.3 = f32[80,128]{1,0:T(8,128)S(1)} collective-permute-done((f32[80,128]{1,0:T(8,128)S(1)}, f32[80,128]{1,0:T(8,128)S(1)}, u32[]{:S(2)}, u32[]{:S(2)}) %collective-permute-start.3) | collective-permute-done | bytes 40992 | tf_op jit(solution)/shard_map/ppermute | solution.py:29
  24.2 2.7 %collective-permute-start.8 = (f32[80,128]{1,0:T(8,128)S(1)}, f32[80,128]{1,0:T(8,128)S(1)}, u32[]{:S(2)}, u32[]{:S(2)}) collective-permute-start(f32[80,128]{1,0:T(8,128)S(1)} %add_add_fusion.2.own), channel_id=1, source_target_pairs={{0,48},{16,0},{32,16},{48,32},{64,112},{80,64},{96,80},{112,96},{1... | collective-permute-start | bytes 122888 | tf_op jit(solution)/shard_map/ppermute | solution.py:29
  26.9 0.0 collective-permute-start.7
  26.9 0.7 collective-permute-start.6
  27.6 0.4 collective-permute-done.8.three
  28.0 3.4 %collective-permute-done.7.two = f32[80,128]{1,0:T(8,128)S(1)} collective-permute-done((f32[80,128]{1,0:T(8,128)S(1)}, f32[80,128]{1,0:T(8,128)S(1)}, u32[]{:S(2)}, u32[]{:S(2)}) %collective-permute-start.7) | collective-permute-done | bytes 40992 | tf_op jit(solution)/shard_map/ppermute | solution.py:29
  31.4 0.0 collective-permute-done.6.one
  31.4 0.0 copy-done
  31.4 0.8 right_send.1
  32.2 5.6 %collective-permute-start.9 = (f32[72,1280]{1,0:T(8,128)S(1)}, f32[72,1280]{1,0:T(8,128)S(1)}, u32[]{:S(2)}, u32[]{:S(2)}) collective-permute-start(f32[72,1280]{1,0:T(8,128)S(1)} %get-tuple-element.24), channel_id=1, source_target_pairs={{0,1},{1,0},{2,3},{3,2},{4,5},{5,4},{6,7},{7,6},{8,9},{9,8},{10,11... | collective-permute-start | bytes 1105928 | tf_op jit(solution)/shard_map/ppermute | solution.py:322
  37.8 0.4 right_keep.1
  38.1 0.0 copy-start.1
  38.2 0.0 copy-start.2
  38.2 0.9 %collective-permute-done.9 = f32[72,1280]{1,0:T(8,128)S(1)} collective-permute-done((f32[72,1280]{1,0:T(8,128)S(1)}, f32[72,1280]{1,0:T(8,128)S(1)}, u32[]{:S(2)}, u32[]{:S(2)}) %collective-permute-start.9) | collective-permute-done | bytes 368672 | tf_op jit(solution)/shard_map/ppermute | solution.py:322
  39.1 0.1 fusion
  39.2 11.9 %all_to_all.10 = f32[8,8,1536]{2,1,0:T(8,128)S(1)} all-to-all(f32[8,8,1536]{2,1,0:T(8,128)S(1)} %pad_maximum_fusion), channel_id=1, replica_groups={{0,2,4,6,8,10,12,14},{1,3,5,7,9,11,13,15},{16,18,20,22,24,26,28,30},{17..., dimensions={0} | all-to-all | bytes 786432 | tf_op jit(solution)/shard_map/all_to_all | solution.py:326
  51.2 0.1 collective-permute-start.11
  51.3 2.7 %collective-permute-start.12 = (f32[8,1280]{1,0:T(8,128)S(1)}, f32[8,1280]{1,0:T(8,128)S(1)}, u32[]{:S(2)}, u32[]{:S(2)}) collective-permute-start(f32[8,1280]{1,0:T(8,128)S(1)} %slice.18), channel_id=1, source_target_pairs={{0,48},{16,0},{32,16},{48,32},{64,112},{80,64},{96,80},{112,96},{1... | collective-permute-start | bytes 122888 | tf_op jit(solution)/shard_map/ppermute | solution.py:29
  53.9 0.4 collective-permute-start.10
  54.3 1.0 %collective-permute-done.11 = f32[8,1280]{1,0:T(8,128)S(1)} collective-permute-done((f32[8,1280]{1,0:T(8,128)S(1)}, f32[8,1280]{1,0:T(8,128)S(1)}, u32[]{:S(2)}, u32[]{:S(2)}) %collective-permute-start.11) | collective-permute-done | bytes 40992 | tf_op jit(solution)/shard_map/ppermute | solution.py:29
  55.3 0.0 collective-permute-done.12
  55.3 3.0 %collective-permute-done.10 = f32[8,1280]{1,0:T(8,128)S(1)} collective-permute-done((f32[8,1280]{1,0:T(8,128)S(1)}, f32[8,1280]{1,0:T(8,128)S(1)}, u32[]{:S(2)}, u32[]{:S(2)}) %collective-permute-start.10) | collective-permute-done | bytes 40992 | tf_op jit(solution)/shard_map/ppermute | solution.py:29
  58.3 3.9 %collective-permute-start.15 = (f32[8,1280]{1,0:T(8,128)S(1)}, f32[8,1280]{1,0:T(8,128)S(1)}, u32[]{:S(2)}, u32[]{:S(2)}) collective-permute-start(f32[8,1280]{1,0:T(8,128)S(1)} %add_add_fusion.1), channel_id=1, source_target_pairs={{0,192},{64,0},{128,64},{192,128},{16,208},{80,16},{144,80},{208,1... | collective-permute-start | bytes 122888 | tf_op jit(solution)/shard_map/ppermute | solution.py:29
  62.2 0.0 collective-permute-start.14
  62.2 2.2 %collective-permute-start.13 = (f32[8,1280]{1,0:T(8,128)S(1)}, f32[8,1280]{1,0:T(8,128)S(1)}, u32[]{:S(2)}, u32[]{:S(2)}) collective-permute-start(f32[8,1280]{1,0:T(8,128)S(1)} %add_add_fusion.1), channel_id=1, source_target_pairs={{0,128},{64,192},{128,0},{192,64},{16,144},{80,208},{144,16},{208,... | collective-permute-start | bytes 122888 | tf_op jit(solution)/shard_map/ppermute | solution.py:29
  64.4 0.0 collective-permute-done.15
  64.4 2.8 %collective-permute-done.14 = f32[8,1280]{1,0:T(8,128)S(1)} collective-permute-done((f32[8,1280]{1,0:T(8,128)S(1)}, f32[8,1280]{1,0:T(8,128)S(1)}, u32[]{:S(2)}, u32[]{:S(2)}) %collective-permute-start.14) | collective-permute-done | bytes 40992 | tf_op jit(solution)/shard_map/ppermute | solution.py:29
  67.2 1.8 %collective-permute-done.13 = f32[8,1280]{1,0:T(8,128)S(1)} collective-permute-done((f32[8,1280]{1,0:T(8,128)S(1)}, f32[8,1280]{1,0:T(8,128)S(1)}, u32[]{:S(2)}, u32[]{:S(2)}) %collective-permute-start.13) | collective-permute-done | bytes 40992 | tf_op jit(solution)/shard_map/ppermute | solution.py:29
  69.0 0.7 broadcast_in_dim.5
  69.8 3.4 %all-to-all-start.1 = ((f32[8,8,1280]{2,1,0:T(8,128)}), f32[8,8,1280]{2,1,0:T(8,128)S(1)}, u32[]{:S(2)}, u32[]{:S(2)}) async-start(f32[8,8,1280]{2,1,0:T(8,128)} %broadcast_in_dim.5), calls=%async_computation.1 | async-start | bytes 655360 | tf_op jit(solution)/shard_map/all_to_all | solution.py:332
  73.2 3.3 %inverse_roots.1 = (f32[8,256]{1,0:T(8,128)S(1)}, f32[64,320]{1,0:T(8,128)S(1)}) custom-call(f32[8,256]{1,0:T(8,128)S(1)} %slice.19.refs_0_, f32[320,128]{1,0:T(8,128)S(1)} %get-tuple-element.26.refs_1_), custom_call_target="tpu_custom_call" | custom-call | flops 20000000 | bytes 32768 | tf_op jit(solution)/shard_map/inverse_roots/pallas_call | solution.py:196
  76.6 2.9 %all-to-all-done.1 = f32[8,8,1280]{2,1,0:T(8,128)S(1)} async-done(((f32[8,8,1280]{2,1,0:T(8,128)}), f32[8,8,1280]{2,1,0:T(8,128)S(1)}, u32[]{:S(2)}, u32[]{:S(2)}) %all-to-all-start.1) | async-done | bytes 327712 | tf_op jit(solution)/shard_map/all_to_all | solution.py:332
  79.5 6.3 %collective-permute-start.16 = (f32[72,1280]{1,0:T(8,128)S(1)}, f32[72,1280]{1,0:T(8,128)S(1)}, u32[]{:S(2)}, u32[]{:S(2)}) collective-permute-start(f32[72,1280]{1,0:T(8,128)S(1)} %select_maximum_fusion), channel_id=1, source_target_pairs={{0,1},{1,0},{2,3},{3,2},{4,5},{5,4},{6,7},{7,6},{8,9},{9,8},{10,11... | collective-permute-start | bytes 1105928 | tf_op jit(solution)/shard_map/ppermute | solution.py:336
  85.8 0.0 copy-done.1
  85.8 0.0 copy-done.2
  85.8 1.5 %shard_map.67 = (f32[4,80,320]{2,1,0:T(8,128)}, f32[4,32,1280]{2,1,0:T(8,128)}, f32[4,80,320]{2,1,0:T(8,128)}) custom-call(f32[64,1280]{1,0:T(8,128)S(1)} %bitcast.10, f32[8,256]{1,0:T(8,128)S(1)} %get-tuple-element.27.root, f32[64,320]{1,0:T(8,128)S(1)} %get-tuple-element.28.factor, f32[4,80,320]{2,1,0:T(8,128)S(1)} %bitcast.11, f32[4,80,320]{2,1,0:T(8,128)S(1)} %bitcast.13), custom_call_target="tpu_custom_call" | custom-call | flops 20000000 | bytes 1000000 | tf_op jit(solution)/shard_map/pallas_call | solution.py:296
  87.4 0.0 collective-permute-done.16.refs_0_
  87.4 1.8 %shard_map.68 = (f32[4,80,320]{2,1,0:T(8,128)}, f32[4,32,1280]{2,1,0:T(8,128)}, f32[4,80,320]{2,1,0:T(8,128)}) custom-call(f32[72,1280]{1,0:T(8,128)S(1)} %collective-permute-done.16.refs_0_, f32[320,128]{1,0:T(8,128)S(1)} %get-tuple-element.26.refs_1_, f32[4,80,320]{2,1,0:T(8,128)S(1)} %bitcast.12, ...), custom_call_target="tpu_custom_call", output_to_operand_aliasing={{0}: (4, {}), {1}: (5, {}), {2}: (6, {})} | custom-call | flops 20000000 | bytes 1000000 | tf_op jit(solution)/shard_map/pallas_call | solution.py:296
  (11 shorter events, 0.1 us)
Async XLA Ops:
  0.6 30.8 %copy-start = (bf16[1,4,320,1280]{3,2,1,0:T(8,128)(2,1)S(1)}, bf16[1,4,320,1280]{3,2,1,0:T(8,128)(2,1)}, u32[]{:S(2)}) copy-start(bf16[1,4,320,1280]{3,2,1,0:T(8,128)(2,1)} %grads.5) | copy-start | bytes 9830404
  3.6 6.3 %collective-permute-start = (f32[80,128]{1,0:T(8,128)S(1)}, f32[80,128]{1,0:T(8,128)S(1)}, u32[]{:S(2)}, u32[]{:S(2)}) collective-permute-start(f32[80,128]{1,0:T(8,128)S(1)} %get-tuple-element.20), channel_id=1, source_target_pairs={{0,32},{16,48},{32,0},{48,16},{64,96},{80,112},{96,64},{112,80},{1... | collective-permute-start | bytes 122888 | tf_op jit(solution)/shard_map/ppermute | solution.py:29
  7.2 4.4 %collective-permute-start.1 = (f32[80,128]{1,0:T(8,128)S(1)}, f32[80,128]{1,0:T(8,128)S(1)}, u32[]{:S(2)}, u32[]{:S(2)}) collective-permute-start(f32[80,128]{1,0:T(8,128)S(1)} %get-tuple-element.21), channel_id=1, source_target_pairs={{0,16},{16,32},{32,48},{48,0},{64,80},{80,96},{96,112},{112,64},{1... | collective-permute-start | bytes 122888 | tf_op jit(solution)/shard_map/ppermute | solution.py:29
  7.5 4.1 %collective-permute-start.2 = (f32[80,128]{1,0:T(8,128)S(1)}, f32[80,128]{1,0:T(8,128)S(1)}, u32[]{:S(2)}, u32[]{:S(2)}) collective-permute-start(f32[80,128]{1,0:T(8,128)S(1)} %get-tuple-element.22), channel_id=1, source_target_pairs={{0,48},{16,0},{32,16},{48,32},{64,112},{80,64},{96,80},{112,96},{1... | collective-permute-start | bytes 122888 | tf_op jit(solution)/shard_map/ppermute | solution.py:29
  11.6 9.1 %collective-permute-start.5 = (f32[80,128]{1,0:T(8,128)S(1)}, f32[80,128]{1,0:T(8,128)S(1)}, u32[]{:S(2)}, u32[]{:S(2)}) collective-permute-start(f32[80,128]{1,0:T(8,128)S(1)} %add_add_fusion.3), channel_id=1, source_target_pairs={{0,192},{64,0},{128,64},{192,128},{16,208},{80,16},{144,80},{208,1... | collective-permute-start | bytes 122888 | tf_op jit(solution)/shard_map/ppermute | solution.py:29
  17.4 5.0 %collective-permute-start.4 = (f32[80,128]{1,0:T(8,128)S(1)}, f32[80,128]{1,0:T(8,128)S(1)}, u32[]{:S(2)}, u32[]{:S(2)}) collective-permute-start(f32[80,128]{1,0:T(8,128)S(1)} %add_add_fusion.3), channel_id=1, source_target_pairs={{0,64},{64,128},{128,192},{192,0},{16,80},{80,144},{144,208},{208,... | collective-permute-start | bytes 122888 | tf_op jit(solution)/shard_map/ppermute | solution.py:29
  17.4 6.8 %collective-permute-start.3 = (f32[80,128]{1,0:T(8,128)S(1)}, f32[80,128]{1,0:T(8,128)S(1)}, u32[]{:S(2)}, u32[]{:S(2)}) collective-permute-start(f32[80,128]{1,0:T(8,128)S(1)} %add_add_fusion.3), channel_id=1, source_target_pairs={{0,128},{64,192},{128,0},{192,64},{16,144},{80,208},{144,16},{208,... | collective-permute-start | bytes 122888 | tf_op jit(solution)/shard_map/ppermute | solution.py:29
  24.2 3.8 %collective-permute-start.8 = (f32[80,128]{1,0:T(8,128)S(1)}, f32[80,128]{1,0:T(8,128)S(1)}, u32[]{:S(2)}, u32[]{:S(2)}) collective-permute-start(f32[80,128]{1,0:T(8,128)S(1)} %add_add_fusion.2.own), channel_id=1, source_target_pairs={{0,48},{16,0},{32,16},{48,32},{64,112},{80,64},{96,80},{112,96},{1... | collective-permute-start | bytes 122888 | tf_op jit(solution)/shard_map/ppermute | solution.py:29
  26.9 4.5 %collective-permute-start.7 = (f32[80,128]{1,0:T(8,128)S(1)}, f32[80,128]{1,0:T(8,128)S(1)}, u32[]{:S(2)}, u32[]{:S(2)}) collective-permute-start(f32[80,128]{1,0:T(8,128)S(1)} %add_add_fusion.2.own), channel_id=1, source_target_pairs={{0,32},{16,48},{32,0},{48,16},{64,96},{80,112},{96,64},{112,80},{1... | collective-permute-start | bytes 122888 | tf_op jit(solution)/shard_map/ppermute | solution.py:29
  26.9 4.5 %collective-permute-start.6 = (f32[80,128]{1,0:T(8,128)S(1)}, f32[80,128]{1,0:T(8,128)S(1)}, u32[]{:S(2)}, u32[]{:S(2)}) collective-permute-start(f32[80,128]{1,0:T(8,128)S(1)} %add_add_fusion.2.own), channel_id=1, source_target_pairs={{0,16},{16,32},{32,48},{48,0},{64,80},{80,96},{96,112},{112,64},{1... | collective-permute-start | bytes 122888 | tf_op jit(solution)/shard_map/ppermute | solution.py:29
  32.2 6.9 %collective-permute-start.9 = (f32[72,1280]{1,0:T(8,128)S(1)}, f32[72,1280]{1,0:T(8,128)S(1)}, u32[]{:S(2)}, u32[]{:S(2)}) collective-permute-start(f32[72,1280]{1,0:T(8,128)S(1)} %get-tuple-element.24), channel_id=1, source_target_pairs={{0,1},{1,0},{2,3},{3,2},{4,5},{5,4},{6,7},{7,6},{8,9},{9,8},{10,11... | collective-permute-start | bytes 1105928 | tf_op jit(solution)/shard_map/ppermute | solution.py:322
  38.1 47.7 %copy-start.1 = (f32[4,320,80]{1,2,0:T(8,128)S(1)}, f32[4,320,80]{1,2,0:T(8,128)}, u32[]{:S(2)}) copy-start(f32[4,320,80]{1,2,0:T(8,128)} %param.6) | copy-start | bytes 1228804
  38.2 47.7 %copy-start.2 = (f32[4,320,80]{1,2,0:T(8,128)S(1)}, f32[4,320,80]{1,2,0:T(8,128)}, u32[]{:S(2)}) copy-start(f32[4,320,80]{1,2,0:T(8,128)} %param.7) | copy-start | bytes 1228804
  51.2 4.1 %collective-permute-start.11 = (f32[8,1280]{1,0:T(8,128)S(1)}, f32[8,1280]{1,0:T(8,128)S(1)}, u32[]{:S(2)}, u32[]{:S(2)}) collective-permute-start(f32[8,1280]{1,0:T(8,128)S(1)} %slice.18), channel_id=1, source_target_pairs={{0,16},{16,32},{32,48},{48,0},{64,80},{80,96},{96,112},{112,64},{1... | collective-permute-start | bytes 122888 | tf_op jit(solution)/shard_map/ppermute | solution.py:29
  51.3 4.1 %collective-permute-start.12 = (f32[8,1280]{1,0:T(8,128)S(1)}, f32[8,1280]{1,0:T(8,128)S(1)}, u32[]{:S(2)}, u32[]{:S(2)}) collective-permute-start(f32[8,1280]{1,0:T(8,128)S(1)} %slice.18), channel_id=1, source_target_pairs={{0,48},{16,0},{32,16},{48,32},{64,112},{80,64},{96,80},{112,96},{1... | collective-permute-start | bytes 122888 | tf_op jit(solution)/shard_map/ppermute | solution.py:29
  53.9 4.4 %collective-permute-start.10 = (f32[8,1280]{1,0:T(8,128)S(1)}, f32[8,1280]{1,0:T(8,128)S(1)}, u32[]{:S(2)}, u32[]{:S(2)}) collective-permute-start(f32[8,1280]{1,0:T(8,128)S(1)} %slice.18), channel_id=1, source_target_pairs={{0,32},{16,48},{32,0},{48,16},{64,96},{80,112},{96,64},{112,80},{1... | collective-permute-start | bytes 122888 | tf_op jit(solution)/shard_map/ppermute | solution.py:29
  58.3 6.1 %collective-permute-start.15 = (f32[8,1280]{1,0:T(8,128)S(1)}, f32[8,1280]{1,0:T(8,128)S(1)}, u32[]{:S(2)}, u32[]{:S(2)}) collective-permute-start(f32[8,1280]{1,0:T(8,128)S(1)} %add_add_fusion.1), channel_id=1, source_target_pairs={{0,192},{64,0},{128,64},{192,128},{16,208},{80,16},{144,80},{208,1... | collective-permute-start | bytes 122888 | tf_op jit(solution)/shard_map/ppermute | solution.py:29
  62.2 5.0 %collective-permute-start.14 = (f32[8,1280]{1,0:T(8,128)S(1)}, f32[8,1280]{1,0:T(8,128)S(1)}, u32[]{:S(2)}, u32[]{:S(2)}) collective-permute-start(f32[8,1280]{1,0:T(8,128)S(1)} %add_add_fusion.1), channel_id=1, source_target_pairs={{0,64},{64,128},{128,192},{192,0},{16,80},{80,144},{144,208},{208,... | collective-permute-start | bytes 122888 | tf_op jit(solution)/shard_map/ppermute | solution.py:29
  62.2 6.8 %collective-permute-start.13 = (f32[8,1280]{1,0:T(8,128)S(1)}, f32[8,1280]{1,0:T(8,128)S(1)}, u32[]{:S(2)}, u32[]{:S(2)}) collective-permute-start(f32[8,1280]{1,0:T(8,128)S(1)} %add_add_fusion.1), channel_id=1, source_target_pairs={{0,128},{64,192},{128,0},{192,64},{16,144},{80,208},{144,16},{208,... | collective-permute-start | bytes 122888 | tf_op jit(solution)/shard_map/ppermute | solution.py:29
  69.8 9.7 %all-to-all-start.1 = ((f32[8,8,1280]{2,1,0:T(8,128)}), f32[8,8,1280]{2,1,0:T(8,128)S(1)}, u32[]{:S(2)}, u32[]{:S(2)}) async-start(f32[8,8,1280]{2,1,0:T(8,128)} %broadcast_in_dim.5), calls=%async_computation.1 | async-start | bytes 655360 | tf_op jit(solution)/shard_map/all_to_all | solution.py:332
  79.5 7.9 %collective-permute-start.16 = (f32[72,1280]{1,0:T(8,128)S(1)}, f32[72,1280]{1,0:T(8,128)S(1)}, u32[]{:S(2)}, u32[]{:S(2)}) collective-permute-start(f32[72,1280]{1,0:T(8,128)S(1)} %select_maximum_fusion), channel_id=1, source_target_pairs={{0,1},{1,0},{2,3},{3,2},{4,5},{5,4},{6,7},{7,6},{8,9},{9,8},{10,11... | collective-permute-start | bytes 1105928 | tf_op jit(solution)/shard_map/ppermute | solution.py:336

commit v6 on v5

--- a/solution.py
+++ b/solution.py
@@ -238,19 +238,26 @@
     ]
 
 
+def halves(array):
+    high = array.astype(jnp.bfloat16)
+    return high, (array - high.astype(jnp.float32)).astype(jnp.bfloat16)
+
+
 def state_part(group, reduced, factor, weights, momentum, new_w, new_m, buf_w, buf_m, sems):
     copies = []
     columns = weights.shape[1]
-    changes = [
-        lax.dot_general(
-            reduced[t][:, :columns],
-            factor[t * RANK : (t + 1) * RANK, :],
-            (((0,), (0,)), ((), ())),
-            precision=HIGH,
-            preferred_element_type=jnp.float32,
-        )
-        for t in range(2)
-    ]
+    changes = []
+    for t in range(2):
+        right_high, right_low = halves(reduced[t][:, :columns])
+        left_high, left_low = halves(factor[t * RANK : (t + 1) * RANK, :])
+        changes.append(
+            lax.dot_general(
+                jnp.concatenate([right_high, right_high, right_low], axis=0),
+                jnp.concatenate([left_high, left_low, left_high], axis=0),
+                (((0,), (0,)), ((), ())),
+                preferred_element_type=jnp.float32,
+            )
+        )
     for t, change in enumerate(changes):
         layer = 2 * group + t
         momentum_now = 0.8 * momentum[layer] + change

time: 89.5 us -> 89.3 us (level)
  no operation moved by 1% of the time
where the time goes in v6:
time: 89.3 us; the launch traced here: 89.1 us
  starting transfers between devices  43.3 us (48%)
  waiting for transfers between devices  21.5 us (24%)
  blocking collectives  11.9 us (13%)
  Pallas kernels  10.5 us (12%)
  between operations  0.92 us (1%)
    ppermute x15, starting transfers between devices, to_ring(): got.append(lax.ppermute(array, 'dp', hop(rings, k)))  28 us
    ppermute x15, waiting for transfers between devices, to_ring(): got.append(lax.ppermute(array, 'dp', hop(rings, k)))  17.6 us
    all_to_all x1, blocking collectives, one_step(): lax.all_to_all(packet, 'tp', 0, 0, tiled=True, axis_index_groups=CHIP_GRO...  11.9 us
    ppermute x1, starting transfers between devices, one_step(): other = lax.ppermute(going, 'tp', CORE_PAIRS)  6.3 us
    ppermute x1, starting transfers between devices, one_step(): came = lax.ppermute(send, 'tp', CORE_PAIRS)  5.55 us
    all_to_all x1, starting transfers between devices, one_step(): lax.all_to_all(jnp.broadcast_to(share[None], (8, 8, width)), 'tp', 0, 0,...  3.43 us
    pallas_call x1, Pallas kernels, inverse_roots(): pl.pallas_call(lambda *refs: root_kernel(replicas, *refs), out_shape=[jax...  3.34 us
    pallas_call x2, Pallas kernels, last_half(): pl.pallas_call(kernel, out_shape=[whole, basis, whole], in_specs=[block]...  3.09 us
  transfers between devices with their start and end apart: 18, of which 11 were waited for; matrix products, arithmetic and copies ran while one was open for 0% of the time, Pallas kernels for 6%

profile of v6, /device:TPU:1, one launch (start us, length us, event | category | flops | bytes accessed | tf_op | source)
XLA Modules:
  0.0 89.1 jit_solution(12766553256962153567)
XLA Ops:
  0.6 0.0 copy-start
  0.6 2.9 %left_parts.1 = (f32[80,128]{1,0:T(8,128)S(1)}, f32[80,128]{1,0:T(8,128)S(1)}, f32[80,128]{1,0:T(8,128)S(1)}, f32[80,128]{1,0:T(8,128)S(1)}) custom-call(bf16[1,4,320,1280]{3,2,1,0:T(8,128)(2,1)} %grads.5, f32[4,32,1280]{2,1,0:T(8,128)} %bitcast.16), custom_call_target="tpu_custom_call" | custom-call | tf_op jit(solution)/shard_map/left_parts/pallas_call | solution.py:60
  3.6 3.6 %collective-permute-start = (f32[80,128]{1,0:T(8,128)S(1)}, f32[80,128]{1,0:T(8,128)S(1)}, u32[]{:S(2)}, u32[]{:S(2)}) collective-permute-start(f32[80,128]{1,0:T(8,128)S(1)} %get-tuple-element.20), channel_id=1, source_target_pairs={{0,32},{16,48},{32,0},{48,16},{64,96},{80,112},{96,64},{112,80},{1... | collective-permute-start | bytes 122888 | tf_op jit(solution)/shard_map/ppermute | solution.py:29
  7.2 0.3 collective-permute-start.1
  7.5 2.4 %collective-permute-start.2 = (f32[80,128]{1,0:T(8,128)S(1)}, f32[80,128]{1,0:T(8,128)S(1)}, u32[]{:S(2)}, u32[]{:S(2)}) collective-permute-start(f32[80,128]{1,0:T(8,128)S(1)} %get-tuple-element.22), channel_id=1, source_target_pairs={{0,48},{16,0},{32,16},{48,32},{64,112},{80,64},{96,80},{112,96},{1... | collective-permute-start | bytes 122888 | tf_op jit(solution)/shard_map/ppermute | solution.py:29
  9.9 0.0 collective-permute-done
  9.9 1.7 %collective-permute-done.1 = f32[80,128]{1,0:T(8,128)S(1)} collective-permute-done((f32[80,128]{1,0:T(8,128)S(1)}, f32[80,128]{1,0:T(8,128)S(1)}, u32[]{:S(2)}, u32[]{:S(2)}) %collective-permute-start.1) | collective-permute-done | bytes 40992 | tf_op jit(solution)/shard_map/ppermute | solution.py:29
  11.6 0.0 collective-permute-done.2
  11.6 5.8 %collective-permute-start.5 = (f32[80,128]{1,0:T(8,128)S(1)}, f32[80,128]{1,0:T(8,128)S(1)}, u32[]{:S(2)}, u32[]{:S(2)}) collective-permute-start(f32[80,128]{1,0:T(8,128)S(1)} %add_add_fusion.3), channel_id=1, source_target_pairs={{0,192},{64,0},{128,64},{192,128},{16,208},{80,16},{144,80},{208,1... | collective-permute-start | bytes 122888 | tf_op jit(solution)/shard_map/ppermute | solution.py:29
  17.4 0.0 collective-permute-start.4
  17.4 3.3 %collective-permute-start.3 = (f32[80,128]{1,0:T(8,128)S(1)}, f32[80,128]{1,0:T(8,128)S(1)}, u32[]{:S(2)}, u32[]{:S(2)}) collective-permute-start(f32[80,128]{1,0:T(8,128)S(1)} %add_add_fusion.3), channel_id=1, source_target_pairs={{0,128},{64,192},{128,0},{192,64},{16,144},{80,208},{144,16},{208,... | collective-permute-start | bytes 122888 | tf_op jit(solution)/shard_map/ppermute | solution.py:29
  20.6 0.0 collective-permute-done.5
  20.6 1.7 %collective-permute-done.4 = f32[80,128]{1,0:T(8,128)S(1)} collective-permute-done((f32[80,128]{1,0:T(8,128)S(1)}, f32[80,128]{1,0:T(8,128)S(1)}, u32[]{:S(2)}, u32[]{:S(2)}) %collective-permute-start.4) | collective-permute-done | bytes 40992 | tf_op jit(solution)/shard_map/ppermute | solution.py:29
  22.4 1.8 %collective-permute-done.3 = f32[80,128]{1,0:T(8,128)S(1)} collective-permute-done((f32[80,128]{1,0:T(8,128)S(1)}, f32[80,128]{1,0:T(8,128)S(1)}, u32[]{:S(2)}, u32[]{:S(2)}) %collective-permute-start.3) | collective-permute-done | bytes 40992 | tf_op jit(solution)/shard_map/ppermute | solution.py:29
  24.2 2.7 %collective-permute-start.8 = (f32[80,128]{1,0:T(8,128)S(1)}, f32[80,128]{1,0:T(8,128)S(1)}, u32[]{:S(2)}, u32[]{:S(2)}) collective-permute-start(f32[80,128]{1,0:T(8,128)S(1)} %add_add_fusion.2.own), channel_id=1, source_target_pairs={{0,48},{16,0},{32,16},{48,32},{64,112},{80,64},{96,80},{112,96},{1... | collective-permute-start | bytes 122888 | tf_op jit(solution)/shard_map/ppermute | solution.py:29
  26.9 0.0 collective-permute-start.7
  26.9 0.7 collective-permute-start.6
  27.6 0.4 collective-permute-done.8.three
  28.0 3.4 %collective-permute-done.7.two = f32[80,128]{1,0:T(8,128)S(1)} collective-permute-done((f32[80,128]{1,0:T(8,128)S(1)}, f32[80,128]{1,0:T(8,128)S(1)}, u32[]{:S(2)}, u32[]{:S(2)}) %collective-permute-start.7) | collective-permute-done | bytes 40992 | tf_op jit(solution)/shard_map/ppermute | solution.py:29
  31.4 0.0 collective-permute-done.6.one
  31.4 0.0 copy-done
  31.4 0.8 right_send.1
  32.2 5.6 %collective-permute-start.9 = (f32[72,1280]{1,0:T(8,128)S(1)}, f32[72,1280]{1,0:T(8,128)S(1)}, u32[]{:S(2)}, u32[]{:S(2)}) collective-permute-start(f32[72,1280]{1,0:T(8,128)S(1)} %get-tuple-element.24), channel_id=1, source_target_pairs={{0,1},{1,0},{2,3},{3,2},{4,5},{5,4},{6,7},{7,6},{8,9},{9,8},{10,11... | collective-permute-start | bytes 1105928 | tf_op jit(solution)/shard_map/ppermute | solution.py:329
  37.8 0.4 right_keep.1
  38.1 0.0 copy-start.1
  38.2 0.0 copy-start.2
  38.2 0.9 %collective-permute-done.9 = f32[72,1280]{1,0:T(8,128)S(1)} collective-permute-done((f32[72,1280]{1,0:T(8,128)S(1)}, f32[72,1280]{1,0:T(8,128)S(1)}, u32[]{:S(2)}, u32[]{:S(2)}) %collective-permute-start.9) | collective-permute-done | bytes 368672 | tf_op jit(solution)/shard_map/ppermute | solution.py:329
  39.1 0.1 fusion
  39.2 11.9 %all_to_all.10 = f32[8,8,1536]{2,1,0:T(8,128)S(1)} all-to-all(f32[8,8,1536]{2,1,0:T(8,128)S(1)} %pad_maximum_fusion), channel_id=1, replica_groups={{0,2,4,6,8,10,12,14},{1,3,5,7,9,11,13,15},{16,18,20,22,24,26,28,30},{17..., dimensions={0} | all-to-all | bytes 786432 | tf_op jit(solution)/shard_map/all_to_all | solution.py:333
  51.2 0.1 collective-permute-start.11
  51.3 2.7 %collective-permute-start.12 = (f32[8,1280]{1,0:T(8,128)S(1)}, f32[8,1280]{1,0:T(8,128)S(1)}, u32[]{:S(2)}, u32[]{:S(2)}) collective-permute-start(f32[8,1280]{1,0:T(8,128)S(1)} %slice.18), channel_id=1, source_target_pairs={{0,48},{16,0},{32,16},{48,32},{64,112},{80,64},{96,80},{112,96},{1... | collective-permute-start | bytes 122888 | tf_op jit(solution)/shard_map/ppermute | solution.py:29
  53.9 0.4 collective-permute-start.10
  54.3 1.0 %collective-permute-done.11 = f32[8,1280]{1,0:T(8,128)S(1)} collective-permute-done((f32[8,1280]{1,0:T(8,128)S(1)}, f32[8,1280]{1,0:T(8,128)S(1)}, u32[]{:S(2)}, u32[]{:S(2)}) %collective-permute-start.11) | collective-permute-done | bytes 40992 | tf_op jit(solution)/shard_map/ppermute | solution.py:29
  55.3 0.0 collective-permute-done.12
  55.3 3.0 %collective-permute-done.10 = f32[8,1280]{1,0:T(8,128)S(1)} collective-permute-done((f32[8,1280]{1,0:T(8,128)S(1)}, f32[8,1280]{1,0:T(8,128)S(1)}, u32[]{:S(2)}, u32[]{:S(2)}) %collective-permute-start.10) | collective-permute-done | bytes 40992 | tf_op jit(solution)/shard_map/ppermute | solution.py:29
  58.3 3.9 %collective-permute-start.15 = (f32[8,1280]{1,0:T(8,128)S(1)}, f32[8,1280]{1,0:T(8,128)S(1)}, u32[]{:S(2)}, u32[]{:S(2)}) collective-permute-start(f32[8,1280]{1,0:T(8,128)S(1)} %add_add_fusion.1), channel_id=1, source_target_pairs={{0,192},{64,0},{128,64},{192,128},{16,208},{80,16},{144,80},{208,1... | collective-permute-start | bytes 122888 | tf_op jit(solution)/shard_map/ppermute | solution.py:29
  62.2 0.0 collective-permute-start.14
  62.2 2.2 %collective-permute-start.13 = (f32[8,1280]{1,0:T(8,128)S(1)}, f32[8,1280]{1,0:T(8,128)S(1)}, u32[]{:S(2)}, u32[]{:S(2)}) collective-permute-start(f32[8,1280]{1,0:T(8,128)S(1)} %add_add_fusion.1), channel_id=1, source_target_pairs={{0,128},{64,192},{128,0},{192,64},{16,144},{80,208},{144,16},{208,... | collective-permute-start | bytes 122888 | tf_op jit(solution)/shard_map/ppermute | solution.py:29
  64.4 0.0 collective-permute-done.15
  64.4 2.8 %collective-permute-done.14 = f32[8,1280]{1,0:T(8,128)S(1)} collective-permute-done((f32[8,1280]{1,0:T(8,128)S(1)}, f32[8,1280]{1,0:T(8,128)S(1)}, u32[]{:S(2)}, u32[]{:S(2)}) %collective-permute-start.14) | collective-permute-done | bytes 40992 | tf_op jit(solution)/shard_map/ppermute | solution.py:29
  67.2 1.8 %collective-permute-done.13 = f32[8,1280]{1,0:T(8,128)S(1)} collective-permute-done((f32[8,1280]{1,0:T(8,128)S(1)}, f32[8,1280]{1,0:T(8,128)S(1)}, u32[]{:S(2)}, u32[]{:S(2)}) %collective-permute-start.13) | collective-permute-done | bytes 40992 | tf_op jit(solution)/shard_map/ppermute | solution.py:29
  69.0 0.7 broadcast_in_dim.5
  69.8 3.4 %all-to-all-start.1 = ((f32[8,8,1280]{2,1,0:T(8,128)}), f32[8,8,1280]{2,1,0:T(8,128)S(1)}, u32[]{:S(2)}, u32[]{:S(2)}) async-start(f32[8,8,1280]{2,1,0:T(8,128)} %broadcast_in_dim.5), calls=%async_computation.1 | async-start | bytes 655360 | tf_op jit(solution)/shard_map/all_to_all | solution.py:339
  73.2 3.3 %inverse_roots.1 = (f32[8,256]{1,0:T(8,128)S(1)}, f32[64,320]{1,0:T(8,128)S(1)}) custom-call(f32[8,256]{1,0:T(8,128)S(1)} %slice.19.refs_0_, f32[320,128]{1,0:T(8,128)S(1)} %get-tuple-element.26.refs_1_), custom_call_target="tpu_custom_call" | custom-call | flops 20000000 | bytes 32768 | tf_op jit(solution)/shard_map/inverse_roots/pallas_call | solution.py:196
  76.6 2.9 %all-to-all-done.1 = f32[8,8,1280]{2,1,0:T(8,128)S(1)} async-done(((f32[8,8,1280]{2,1,0:T(8,128)}), f32[8,8,1280]{2,1,0:T(8,128)S(1)}, u32[]{:S(2)}, u32[]{:S(2)}) %all-to-all-start.1) | async-done | bytes 327712 | tf_op jit(solution)/shard_map/all_to_all | solution.py:339
  79.5 6.3 %collective-permute-start.16 = (f32[72,1280]{1,0:T(8,128)S(1)}, f32[72,1280]{1,0:T(8,128)S(1)}, u32[]{:S(2)}, u32[]{:S(2)}) collective-permute-start(f32[72,1280]{1,0:T(8,128)S(1)} %select_maximum_fusion), channel_id=1, source_target_pairs={{0,1},{1,0},{2,3},{3,2},{4,5},{5,4},{6,7},{7,6},{8,9},{9,8},{10,11... | collective-permute-start | bytes 1105928 | tf_op jit(solution)/shard_map/ppermute | solution.py:343
  85.8 0.0 copy-done.1
  85.8 0.0 copy-done.2
  85.8 1.4 %shard_map.67 = (f32[4,80,320]{2,1,0:T(8,128)}, f32[4,32,1280]{2,1,0:T(8,128)}, f32[4,80,320]{2,1,0:T(8,128)}) custom-call(f32[64,1280]{1,0:T(8,128)S(1)} %bitcast.10, f32[8,256]{1,0:T(8,128)S(1)} %get-tuple-element.27.root, f32[64,320]{1,0:T(8,128)S(1)} %get-tuple-element.28.factor, f32[4,80,320]{2,1,0:T(8,128)S(1)} %bitcast.11, f32[4,80,320]{2,1,0:T(8,128)S(1)} %bitcast.13), custom_call_target="tpu_custom_call" | custom-call | flops 20000000 | bytes 1000000 | tf_op jit(solution)/shard_map/pallas_call | solution.py:303
  87.2 0.0 collective-permute-done.16.refs_0_
  87.2 1.7 %shard_map.68 = (f32[4,80,320]{2,1,0:T(8,128)}, f32[4,32,1280]{2,1,0:T(8,128)}, f32[4,80,320]{2,1,0:T(8,128)}) custom-call(f32[72,1280]{1,0:T(8,128)S(1)} %collective-permute-done.16.refs_0_, f32[320,128]{1,0:T(8,128)S(1)} %get-tuple-element.26.refs_1_, f32[4,80,320]{2,1,0:T(8,128)S(1)} %bitcast.12, ...), custom_call_target="tpu_custom_call", output_to_operand_aliasing={{0}: (4, {}), {1}: (5, {}), {2}: (6, {})} | custom-call | flops 20000000 | bytes 1000000 | tf_op jit(solution)/shard_map/pallas_call | solution.py:303
  (11 shorter events, 0.1 us)
Async XLA Ops:
  0.6 30.8 %copy-start = (bf16[1,4,320,1280]{3,2,1,0:T(8,128)(2,1)S(1)}, bf16[1,4,320,1280]{3,2,1,0:T(8,128)(2,1)}, u32[]{:S(2)}) copy-start(bf16[1,4,320,1280]{3,2,1,0:T(8,128)(2,1)} %grads.5) | copy-start | bytes 9830404
  3.6 6.3 %collective-permute-start = (f32[80,128]{1,0:T(8,128)S(1)}, f32[80,128]{1,0:T(8,128)S(1)}, u32[]{:S(2)}, u32[]{:S(2)}) collective-permute-start(f32[80,128]{1,0:T(8,128)S(1)} %get-tuple-element.20), channel_id=1, source_target_pairs={{0,32},{16,48},{32,0},{48,16},{64,96},{80,112},{96,64},{112,80},{1... | collective-permute-start | bytes 122888 | tf_op jit(solution)/shard_map/ppermute | solution.py:29
  7.2 4.4 %collective-permute-start.1 = (f32[80,128]{1,0:T(8,128)S(1)}, f32[80,128]{1,0:T(8,128)S(1)}, u32[]{:S(2)}, u32[]{:S(2)}) collective-permute-start(f32[80,128]{1,0:T(8,128)S(1)} %get-tuple-element.21), channel_id=1, source_target_pairs={{0,16},{16,32},{32,48},{48,0},{64,80},{80,96},{96,112},{112,64},{1... | collective-permute-start | bytes 122888 | tf_op jit(solution)/shard_map/ppermute | solution.py:29
  7.5 4.1 %collective-permute-start.2 = (f32[80,128]{1,0:T(8,128)S(1)}, f32[80,128]{1,0:T(8,128)S(1)}, u32[]{:S(2)}, u32[]{:S(2)}) collective-permute-start(f32[80,128]{1,0:T(8,128)S(1)} %get-tuple-element.22), channel_id=1, source_target_pairs={{0,48},{16,0},{32,16},{48,32},{64,112},{80,64},{96,80},{112,96},{1... | collective-permute-start | bytes 122888 | tf_op jit(solution)/shard_map/ppermute | solution.py:29
  11.6 9.1 %collective-permute-start.5 = (f32[80,128]{1,0:T(8,128)S(1)}, f32[80,128]{1,0:T(8,128)S(1)}, u32[]{:S(2)}, u32[]{:S(2)}) collective-permute-start(f32[80,128]{1,0:T(8,128)S(1)} %add_add_fusion.3), channel_id=1, source_target_pairs={{0,192},{64,0},{128,64},{192,128},{16,208},{80,16},{144,80},{208,1... | collective-permute-start | bytes 122888 | tf_op jit(solution)/shard_map/ppermute | solution.py:29
  17.4 5.0 %collective-permute-start.4 = (f32[80,128]{1,0:T(8,128)S(1)}, f32[80,128]{1,0:T(8,128)S(1)}, u32[]{:S(2)}, u32[]{:S(2)}) collective-permute-start(f32[80,128]{1,0:T(8,128)S(1)} %add_add_fusion.3), channel_id=1, source_target_pairs={{0,64},{64,128},{128,192},{192,0},{16,80},{80,144},{144,208},{208,... | collective-permute-start | bytes 122888 | tf_op jit(solution)/shard_map/ppermute | solution.py:29
  17.4 6.8 %collective-permute-start.3 = (f32[80,128]{1,0:T(8,128)S(1)}, f32[80,128]{1,0:T(8,128)S(1)}, u32[]{:S(2)}, u32[]{:S(2)}) collective-permute-start(f32[80,128]{1,0:T(8,128)S(1)} %add_add_fusion.3), channel_id=1, source_target_pairs={{0,128},{64,192},{128,0},{192,64},{16,144},{80,208},{144,16},{208,... | collective-permute-start | bytes 122888 | tf_op jit(solution)/shard_map/ppermute | solution.py:29
  24.2 3.8 %collective-permute-start.8 = (f32[80,128]{1,0:T(8,128)S(1)}, f32[80,128]{1,0:T(8,128)S(1)}, u32[]{:S(2)}, u32[]{:S(2)}) collective-permute-start(f32[80,128]{1,0:T(8,128)S(1)} %add_add_fusion.2.own), channel_id=1, source_target_pairs={{0,48},{16,0},{32,16},{48,32},{64,112},{80,64},{96,80},{112,96},{1... | collective-permute-start | bytes 122888 | tf_op jit(solution)/shard_map/ppermute | solution.py:29
  26.9 4.5 %collective-permute-start.7 = (f32[80,128]{1,0:T(8,128)S(1)}, f32[80,128]{1,0:T(8,128)S(1)}, u32[]{:S(2)}, u32[]{:S(2)}) collective-permute-start(f32[80,128]{1,0:T(8,128)S(1)} %add_add_fusion.2.own), channel_id=1, source_target_pairs={{0,32},{16,48},{32,0},{48,16},{64,96},{80,112},{96,64},{112,80},{1... | collective-permute-start | bytes 122888 | tf_op jit(solution)/shard_map/ppermute | solution.py:29
  26.9 4.5 %collective-permute-start.6 = (f32[80,128]{1,0:T(8,128)S(1)}, f32[80,128]{1,0:T(8,128)S(1)}, u32[]{:S(2)}, u32[]{:S(2)}) collective-permute-start(f32[80,128]{1,0:T(8,128)S(1)} %add_add_fusion.2.own), channel_id=1, source_target_pairs={{0,16},{16,32},{32,48},{48,0},{64,80},{80,96},{96,112},{112,64},{1... | collective-permute-start | bytes 122888 | tf_op jit(solution)/shard_map/ppermute | solution.py:29
  32.2 6.9 %collective-permute-start.9 = (f32[72,1280]{1,0:T(8,128)S(1)}, f32[72,1280]{1,0:T(8,128)S(1)}, u32[]{:S(2)}, u32[]{:S(2)}) collective-permute-start(f32[72,1280]{1,0:T(8,128)S(1)} %get-tuple-element.24), channel_id=1, source_target_pairs={{0,1},{1,0},{2,3},{3,2},{4,5},{5,4},{6,7},{7,6},{8,9},{9,8},{10,11... | collective-permute-start | bytes 1105928 | tf_op jit(solution)/shard_map/ppermute | solution.py:329
  38.1 47.7 %copy-start.1 = (f32[4,320,80]{1,2,0:T(8,128)S(1)}, f32[4,320,80]{1,2,0:T(8,128)}, u32[]{:S(2)}) copy-start(f32[4,320,80]{1,2,0:T(8,128)} %param.6) | copy-start | bytes 1228804
  38.2 47.7 %copy-start.2 = (f32[4,320,80]{1,2,0:T(8,128)S(1)}, f32[4,320,80]{1,2,0:T(8,128)}, u32[]{:S(2)}) copy-start(f32[4,320,80]{1,2,0:T(8,128)} %param.7) | copy-start | bytes 1228804
  51.2 4.1 %collective-permute-start.11 = (f32[8,1280]{1,0:T(8,128)S(1)}, f32[8,1280]{1,0:T(8,128)S(1)}, u32[]{:S(2)}, u32[]{:S(2)}) collective-permute-start(f32[8,1280]{1,0:T(8,128)S(1)} %slice.18), channel_id=1, source_target_pairs={{0,16},{16,32},{32,48},{48,0},{64,80},{80,96},{96,112},{112,64},{1... | collective-permute-start | bytes 122888 | tf_op jit(solution)/shard_map/ppermute | solution.py:29
  51.3 4.1 %collective-permute-start.12 = (f32[8,1280]{1,0:T(8,128)S(1)}, f32[8,1280]{1,0:T(8,128)S(1)}, u32[]{:S(2)}, u32[]{:S(2)}) collective-permute-start(f32[8,1280]{1,0:T(8,128)S(1)} %slice.18), channel_id=1, source_target_pairs={{0,48},{16,0},{32,16},{48,32},{64,112},{80,64},{96,80},{112,96},{1... | collective-permute-start | bytes 122888 | tf_op jit(solution)/shard_map/ppermute | solution.py:29
  53.9 4.4 %collective-permute-start.10 = (f32[8,1280]{1,0:T(8,128)S(1)}, f32[8,1280]{1,0:T(8,128)S(1)}, u32[]{:S(2)}, u32[]{:S(2)}) collective-permute-start(f32[8,1280]{1,0:T(8,128)S(1)} %slice.18), channel_id=1, source_target_pairs={{0,32},{16,48},{32,0},{48,16},{64,96},{80,112},{96,64},{112,80},{1... | collective-permute-start | bytes 122888 | tf_op jit(solution)/shard_map/ppermute | solution.py:29
  58.3 6.1 %collective-permute-start.15 = (f32[8,1280]{1,0:T(8,128)S(1)}, f32[8,1280]{1,0:T(8,128)S(1)}, u32[]{:S(2)}, u32[]{:S(2)}) collective-permute-start(f32[8,1280]{1,0:T(8,128)S(1)} %add_add_fusion.1), channel_id=1, source_target_pairs={{0,192},{64,0},{128,64},{192,128},{16,208},{80,16},{144,80},{208,1... | collective-permute-start | bytes 122888 | tf_op jit(solution)/shard_map/ppermute | solution.py:29
  62.2 5.0 %collective-permute-start.14 = (f32[8,1280]{1,0:T(8,128)S(1)}, f32[8,1280]{1,0:T(8,128)S(1)}, u32[]{:S(2)}, u32[]{:S(2)}) collective-permute-start(f32[8,1280]{1,0:T(8,128)S(1)} %add_add_fusion.1), channel_id=1, source_target_pairs={{0,64},{64,128},{128,192},{192,0},{16,80},{80,144},{144,208},{208,... | collective-permute-start | bytes 122888 | tf_op jit(solution)/shard_map/ppermute | solution.py:29
  62.2 6.8 %collective-permute-start.13 = (f32[8,1280]{1,0:T(8,128)S(1)}, f32[8,1280]{1,0:T(8,128)S(1)}, u32[]{:S(2)}, u32[]{:S(2)}) collective-permute-start(f32[8,1280]{1,0:T(8,128)S(1)} %add_add_fusion.1), channel_id=1, source_target_pairs={{0,128},{64,192},{128,0},{192,64},{16,144},{80,208},{144,16},{208,... | collective-permute-start | bytes 122888 | tf_op jit(solution)/shard_map/ppermute | solution.py:29
  69.8 9.7 %all-to-all-start.1 = ((f32[8,8,1280]{2,1,0:T(8,128)}), f32[8,8,1280]{2,1,0:T(8,128)S(1)}, u32[]{:S(2)}, u32[]{:S(2)}) async-start(f32[8,8,1280]{2,1,0:T(8,128)} %broadcast_in_dim.5), calls=%async_computation.1 | async-start | bytes 655360 | tf_op jit(solution)/shard_map/all_to_all | solution.py:339
  79.5 7.7 %collective-permute-start.16 = (f32[72,1280]{1,0:T(8,128)S(1)}, f32[72,1280]{1,0:T(8,128)S(1)}, u32[]{:S(2)}, u32[]{:S(2)}) collective-permute-start(f32[72,1280]{1,0:T(8,128)S(1)} %select_maximum_fusion), channel_id=1, source_target_pairs={{0,1},{1,0},{2,3},{3,2},{4,5},{5,4},{6,7},{7,6},{8,9},{9,8},{10,11... | collective-permute-start | bytes 1105928 | tf_op jit(solution)/shard_map/ppermute | solution.py:343
